TPU v7x, 32 devices: a whole 2x2x4 slice. The times are simulated.
32 devices in a mesh: dp: 2 (over y), seq: 4 (over z), chan: 4 (over x, core).
Axes of the slice: x: 2, y: 2, z: 4, core: 2. Of those that a mesh axis runs over, the one named last changes fastest.
Arguments:
- layer_input: bfloat16 [2, 512, 2560], P('dp', ('seq', 'chan')), may hold values from -6 to 6
- inner_weight: bfloat16 [2560, 2560], P(None, 'chan'), may hold values from -0.125 to 0.125
- mixer_weight: bfloat16 [2560, 256], replicated, may hold values from -0.01171875 to 0.01171875
- step_weight: bfloat16 [2560, 40], P(None, 'chan'), may hold values from -0.125 to 0.125
- conv_inner: float32 [4, 2560], P(None, 'chan'), may hold values from -3 to 3
- conv_mixer: float32 [4, 256], replicated, may hold values from -3 to 3
- step_bias: float32 [40], P('chan'), may hold values from -2 to 1
- decay_log: float32 [40], P('chan'), as said below
- skip_gain: float32 [40], P('chan'), may hold values from 0.5 to 1.5
- output_grad: bfloat16 [2, 512, 2560], P('dp', 'seq', 'chan'), may hold values from -6 to 6
Outputs:
- input_grad: bfloat16 [2, 512, 2560], P('dp', ('seq', 'chan'))
- inner_weight_grad: float32 [2560, 2560], P(('dp', 'seq'), 'chan')
- mixer_weight_grad: float32 [2560, 256], P(('dp', 'seq', 'chan'))
- step_weight_grad: float32 [2560, 40], P(('dp', 'seq'), 'chan')
Inputs may be any that keep to these rules, and one draw needn't show every extreme that they name: exp(decay_log) is at least 0.2 / 512.
All inputs are finite; a program needn't handle non-finite values.
Results may differ from a plain program's by a relative error of at most 0.014.
Values may be sent and summed in bfloat16 or wider, within the bound.
A program may use at most 128 MiB of HBM per device.

v0:
```python
import functools
import math

import jax
import jax.numpy as jnp
from jax import lax
from jax.experimental import pallas as pl
from jax.experimental.pallas import tpu as pltpu
from jax.sharding import PartitionSpec as P

MESH = pl.DeviceIdType.MESH
HDIM = 64
PAD = 16
LANES = 128
LIMIT = 60 * 2**20
BF = jnp.bfloat16
F32 = jnp.float32
HIGH = lax.Precision.HIGHEST


def size_of(axes, sizes):
    return math.prod(sizes[a] for a in axes)


def index_of(axes, sizes):
    index = 0
    for a in axes:
        index = index * sizes[a] + lax.axis_index(a)
    return index


def coords(axes, sizes, index):
    place = {}
    for a in reversed(axes):
        place[a] = lax.rem(index, sizes[a])
        index = lax.div(index, sizes[a])
    return place


def each(n, step):
    if n <= 12:
        for d in range(1, n):
            step(d)
    else:

        def one(d, carry):
            step(d)
            return carry

        lax.fori_loop(1, n, one, 0)


def exchange_kernel(jobs, tail, plugged, sizes, *refs):
    count = len(jobs)
    extra = 1 if tail else 0
    fed = count + (1 if tail == "up" else 0)
    plug_ins, plug_outs, plug_scratch = plugged.counts if plugged else (0, 0, 0)
    cuts = (fed, plug_ins, count + extra, plug_outs, 2 * (count + extra), plug_scratch)
    groups, at = [], 0
    for cut in cuts:
        groups.append(refs[at : at + cut])
        at += cut
    ins, plug_in, outs, plug_out, sems, scratch = groups
    plug = plugged.bind(sizes, plug_in, plug_out, scratch) if plugged else None
    barrier = pltpu.get_barrier_semaphore()
    chans, seqs = sizes["chan"], sizes["seq"]
    greeted = 0
    for axes in dict.fromkeys(job[0] for job in jobs):
        n, me = size_of(axes, sizes), index_of(axes, sizes)

        def greet(d, axes=axes, n=n, me=me):
            where = coords(axes, sizes, lax.rem(me + d, n))
            pl.semaphore_signal(barrier, inc=1, device_id=where, device_id_type=MESH)

        each(n, greet)
        greeted += n - 1
    if tail:
        spot = lax.axis_index("seq")
        after, before = lax.rem(spot + 1, seqs), lax.rem(spot + seqs - 1, seqs)
        ending = lax.axis_index("chan") == chans - 1
        source = {"seq": before, "chan": jnp.int32(chans - 1)}
        signal_to(barrier, source if tail == "up" else {"seq": before})

        if tail == "up":

            @pl.when(ending)
            def _():
                for c in range(chans):
                    signal_to(barrier, {"seq": after, "chan": jnp.int32(c)})

            greeted += 1 + chans * lax.div(lax.axis_index("chan"), chans - 1)
        else:
            signal_to(barrier, {"seq": after})
            greeted += 2
    if plug:
        greeted += plug.greet(barrier)
    pl.semaphore_wait(barrier, greeted)
    if plug:
        plug.start()

    def describe(k, q, landing, signal):
        axes, mode = jobs[k]
        src = ins[k] if mode == "gather" else ins[k].at[:, q] if mode == "cross" else ins[k].at[q]
        return pltpu.make_async_remote_copy(
            src_ref=src,
            dst_ref=outs[k].at[landing],
            send_sem=sems[2 * k].at[q],
            recv_sem=sems[2 * k + 1].at[signal],
            device_id=coords(axes, sizes, q),
            device_id_type=MESH,
        )

    for k, (axes, mode) in enumerate(jobs):
        n, me = size_of(axes, sizes), index_of(axes, sizes)
        each(n, lambda d, k=k, n=n, me=me: describe(k, lax.rem(me + d, n), me, me).start())
    if tail:
        tail_out = outs[count]
        tail_in = ins[count] if tail == "up" else ins[0].at[pl.ds(ins[0].shape[0] - PAD, PAD)]
        tail_send, tail_recv = sems[2 * count], sems[2 * count + 1]

        def down(c):
            return pltpu.make_async_remote_copy(
                src_ref=tail_in if c == chans - 1 else tail_out,
                dst_ref=tail_out,
                send_sem=tail_send.at[c],
                recv_sem=tail_recv.at[0],
                device_id={"seq": after} if c == chans - 1 else {"chan": jnp.int32(c)},
                device_id_type=MESH,
            )

        def up(slot):
            return pltpu.make_async_remote_copy(
                src_ref=tail_in,
                dst_ref=tail_out.at[slot],
                send_sem=tail_send.at[0],
                recv_sem=tail_recv.at[slot],
                device_id=source,
                device_id_type=MESH,
            )

        if tail == "down":

            @pl.when(ending)
            def _():
                down(chans - 1).start()
        else:
            up(lax.axis_index("chan")).start()
    for k, (axes, mode) in enumerate(jobs):
        me = index_of(axes, sizes)
        kept = ins[k][...] if mode == "gather" else ins[k][:, me] if mode == "cross" else ins[k][me]
        outs[k][me] = kept
    if tail == "down":
        down(chans - 1).wait_recv()

        @pl.when(ending)
        def _():
            for c in range(chans - 1):
                down(c).start()

    if plug:
        plug.run()
    for k, (axes, mode) in enumerate(jobs):
        n, me = size_of(axes, sizes), index_of(axes, sizes)

        def finish(d, k=k, n=n, me=me):
            q = lax.rem(me + d, n)
            describe(k, q, q, q).wait()

        each(n, finish)
    if tail == "down":
        @pl.when(ending)
        def _():
            for c in range(chans):
                down(c).wait_send()
    if tail == "up":
        up(lax.axis_index("chan")).wait_send()

        @pl.when(ending)
        def _():
            for c in range(chans):
                up(c).wait_recv()


def signal_to(barrier, where):
    pl.semaphore_signal(barrier, inc=1, device_id=where, device_id_type=MESH)


def greet_line(barrier, n):
    me = lax.axis_index("seq")
    signal_to(barrier, {"seq": lax.rem(me + 1, n)})
    signal_to(barrier, {"seq": lax.rem(me + n - 1, n)})
    return 2


class Chain:
    counts = (3, 2, 6)
    pieces = 5

    def shapes(self, sizes, arrays):
        shape = jax.ShapeDtypeStruct(arrays[0].shape, BF)
        sems = [pltpu.SemaphoreType.DMA((self.pieces,)) for unused in range(4)]
        return [shape, shape], [pltpu.VMEM(shape.shape, BF)] * 2 + sems

    def bind(self, sizes, ins, outs, scratch):
        bound = Chain()
        bound.n, bound.ins, bound.outs, bound.scratch = sizes["seq"], ins, outs, scratch
        return bound

    def greet(self, barrier):
        return greet_line(barrier, self.n)

    def copy(self, way, piece):
        me = lax.axis_index("seq")
        rows = self.outs[0].shape[0] // self.pieces
        part = pl.ds(pl.multiple_of(piece * rows, rows), rows)
        target = lax.rem(me + 1, self.n) if way == 0 else lax.rem(me + self.n - 1, self.n)
        return pltpu.make_async_remote_copy(
            src_ref=self.scratch[way].at[part],
            dst_ref=self.outs[way].at[part],
            send_sem=self.scratch[2 + way].at[piece],
            recv_sem=self.scratch[4 + way].at[piece],
            device_id={"seq": target},
            device_id_type=MESH,
        )

    def start(self):
        me = lax.axis_index("seq")
        for way, edge in ((0, 0), (1, self.n - 1)):

            @pl.when(me == edge)
            def _(way=way):
                self.outs[way][...] = jnp.zeros(self.outs[way].shape, BF)

    def run(self):
        me = lax.axis_index("seq")
        rows = self.outs[0].shape[0] // self.pieces

        def beat(t):
            for way in (0, 1):
                place = me if way == 0 else self.n - 1 - me
                piece = t - place
                active = (piece >= 0) & (piece < self.pieces)

                @pl.when(active & (place > 0))
                def _(way=way, piece=piece):
                    self.copy(way, piece).wait_recv()

                @pl.when(active & (place < self.n - 1))
                def _(way=way, piece=piece):
                    part = pl.ds(pl.multiple_of(piece * rows, rows), rows)
                    before = self.outs[way][part, :].astype(F32)
                    term = self.ins[way][part, :].astype(F32)
                    self.scratch[way][part, :] = (self.ins[2][part, :] * before + term).astype(BF)
                    self.copy(way, piece).start()

        beat(0)
        each(self.n - 1 + self.pieces, beat)

        for way in (0, 1):

            @pl.when(me != (self.n - 1 if way == 0 else 0))
            def _(way=way):
                for piece in range(self.pieces):
                    self.copy(way, piece).wait_send()


class Grid:
    counts = (1, 1, 10)

    def shapes(self, sizes, arrays):
        d, n = sizes["dp"], sizes["seq"]
        shape = jax.ShapeDtypeStruct((d, n) + arrays[0].shape, BF)
        lengths = (n, d * n, d, d * n, n, n, d * n, d, d * n, d * n)
        return [shape], [pltpu.SemaphoreType.DMA((k,)) for k in lengths]

    def bind(self, sizes, ins, outs, scratch):
        bound = Grid()
        bound.d, bound.n = sizes["dp"], sizes["seq"]
        bound.src, bound.out, bound.sems = ins[0], outs[0], scratch
        return bound

    def greet(self, barrier):
        mine = lax.axis_index("dp")
        for e in range(1, self.d):
            signal_to(barrier, {"dp": lax.rem(mine + e, self.d)})
        return greet_line(barrier, self.n) + self.d - 1

    def copy(self, half, way, e, k, own=False, target=None):
        rows = self.src.shape[0]
        cut = (rows * 5 // 6) // 16 * 16
        part = pl.ds(0, cut) if half == 0 else pl.ds(cut, rows - cut)
        me = lax.axis_index("seq")
        slot = e * self.n + k
        if way == "cross":
            where = {"dp": lax.axis_index("dp") if target is None else target}
            recv = self.sems[1].at[slot] if half == 0 else self.sems[2].at[e]
            to = 0 if target is None else target
            send = self.sems[6].at[to * self.n + k] if half == 0 else self.sems[7].at[to]
        else:
            shift = 1 if way == "up" else self.n - 1
            where = {"seq": lax.rem(me + shift, self.n)}
            recv = self.sems[0].at[k] if half == 0 else self.sems[3].at[slot]
            ups = 4 if way == "up" else 5
            send = self.sems[ups].at[k] if half == 0 else self.sems[ups + 4].at[slot]
        src = self.src.at[part] if own else self.out.at[e, k, part]
        return pltpu.make_async_remote_copy(
            src_ref=src,
            dst_ref=self.out.at[e, k, part],
            send_sem=send,
            recv_sem=recv,
            device_id=where,
            device_id_type=MESH,
        )

    def partners(self):
        mine = lax.axis_index("dp")
        return [lax.rem(mine + e, self.d) for e in range(1, self.d)]

    def both(self, half, e, k, own=False):
        me = lax.axis_index("seq")

        @pl.when(me < self.n - 1)
        def _():
            self.copy(half, "up", e, k, own).start()

        @pl.when(me > 0)
        def _():
            self.copy(half, "down", e, k, own).start()

    def start(self):
        mine, me = lax.axis_index("dp"), lax.axis_index("seq")
        for e in self.partners():
            self.copy(1, "cross", mine, me, True, e).start()
        self.both(1, mine, me, True)
        self.both(0, mine, me, True)
        for e in self.partners():
            self.copy(0, "cross", mine, me, True, e).start()
        self.out[mine, me] = self.src[...]

    def run(self):
        mine, me, n = lax.axis_index("dp"), lax.axis_index("seq"), self.n
        others = self.partners()
        for e in others:
            self.copy(1, "cross", e, me, target=e).wait_recv()
            self.both(1, e, me)

        def hop(d):
            for way, k, there, onward in (
                ("up", me - d, me >= d, me < n - 1),
                ("down", me + d, me + d < n, me > 0),
            ):
                for e in [mine] + others:

                    @pl.when(there)
                    def _(way=way, k=k, e=e):
                        self.copy(1, way, e, k).wait_recv()

                    @pl.when(there & onward)
                    def _(way=way, k=k, e=e):
                        self.copy(1, way, e, k).start()

                @pl.when(there)
                def _(way=way, k=k):
                    self.copy(0, way, mine, k).wait_recv()

                @pl.when(there & onward)
                def _(way=way, k=k):
                    self.copy(0, way, mine, k).start()

                @pl.when(there)
                def _(way=way, k=k):
                    for e in others:
                        self.copy(0, "cross", mine, k, target=e).start()

        each(n, hop)

        def settle(k):
            for e in others:
                self.copy(0, "cross", e, k, target=e).wait_recv()
                self.copy(0, "cross", mine, k, target=e).wait_send()
            for way, sent in (("up", (k <= me) & (me < n - 1)), ("down", (k >= me) & (me > 0))):

                @pl.when(sent)
                def _(way=way, k=k):
                    self.copy(0, way, mine, k).wait_send()
                    for e in [mine] + others:
                        self.copy(1, way, e, k).wait_send()

        settle(0)
        each(n, settle)
        for e in others:
            self.copy(1, "cross", mine, me, target=e).wait_send()


def exchange(sizes, call_id, jobs, arrays, tail=None, tail_array=None, plug=None, plug_arrays=()):
    plan, out_shapes, sems = [], [], []
    for (axes, mode), array in zip(jobs, arrays):
        n = size_of(axes, sizes)
        shape = (n,) + array.shape if mode == "gather" else array.shape
        if mode == "cross":
            shape = (n, array.shape[0]) + array.shape[2:]
        plan.append((axes, mode))
        out_shapes.append(jax.ShapeDtypeStruct(shape, array.dtype))
        sems += [pltpu.SemaphoreType.DMA((n,)), pltpu.SemaphoreType.DMA((n,))]
    arrays = list(arrays)
    if tail:
        if tail == "up":
            arrays.append(tail_array)
            shape = (sizes["chan"],) + tail_array.shape
        else:
            shape = (PAD,) + arrays[0].shape[1:]
        out_shapes.append(jax.ShapeDtypeStruct(shape, arrays[0].dtype))
        sems += [pltpu.SemaphoreType.DMA((sizes["chan"],)), pltpu.SemaphoreType.DMA((sizes["chan"],))]
    if plug:
        arrays += plug_arrays
        plug_shapes, plug_scratch = plug.shapes(sizes, plug_arrays)
        out_shapes += plug_shapes
        sems += plug_scratch
    vmem = pl.BlockSpec(memory_space=pltpu.VMEM)
    return pl.pallas_call(
        functools.partial(exchange_kernel, tuple(plan), tail, plug, sizes),
        out_shape=out_shapes,
        in_specs=[vmem] * len(arrays),
        out_specs=[vmem] * len(out_shapes),
        scratch_shapes=sems,
        compiler_params=pltpu.CompilerParams(
            collective_id=call_id, has_side_effects=True, vmem_limit_bytes=LIMIT
        ),
        name=f"exchange_{call_id}",
    )(*arrays)


def mm(a, b, da, db):
    return lax.dot_general(
        a.astype(BF), b.astype(BF), (((da,), (db,)), ((), ())), preferred_element_type=F32
    )


def exact(a, b, da=1, db=0):
    return lax.dot_general(
        a, b, (((da,), (db,)), ((), ())), precision=HIGH, preferred_element_type=F32
    )


def softplus(v):
    return jnp.maximum(v, 0.0) + jnp.log1p(jnp.exp(-jnp.abs(v)))


def head_mask(width, heads_first):
    shape = (LANES, width) if heads_first else (width, LANES)
    head = lax.broadcasted_iota(jnp.int32, shape, 0 if heads_first else 1)
    column = lax.broadcasted_iota(jnp.int32, shape, 1 if heads_first else 0)
    return (column // HDIM == head).astype(F32)


def decays(raw, bias, decay_log):
    length = raw.shape[0]
    step = softplus(raw + bias)
    rate = jnp.exp(decay_log)
    row = lax.broadcasted_iota(jnp.int32, (length, length), 0)
    col = lax.broadcasted_iota(jnp.int32, (length, length), 1)
    lower = (row >= col).astype(F32)
    cumulative = exact(lower, -step * rate)
    return step, rate, cumulative, row, col, lower


def forward_kernel(
    inner_ref, mixer_ref, raw_ref, conv_inner_ref, conv_mixer_ref, bias_ref, log_ref, grad_ref,
    summed_inner_ref, summed_mixer_ref, state_ref, back_ref, decay_ref, wide_inner, wide_mixer,
):
    length = raw_ref.shape[0]
    width = conv_inner_ref.shape[1]
    taps = conv_inner_ref.shape[0]
    wide_inner[...] = inner_ref[...].astype(F32)
    wide_mixer[...] = mixer_ref[...].astype(F32)
    first = PAD - (taps - 1)

    def convolved(wide, kernel):
        total = kernel[0:1, :] * wide[pl.ds(first, length), :]
        for k in range(1, taps):
            total = total + kernel[k : k + 1, :] * wide[pl.ds(first + k, length), :]
        return total

    inner = convolved(wide_inner, conv_inner_ref)
    mixer = convolved(wide_mixer, conv_mixer_ref)
    summed_inner_ref[...] = inner
    summed_mixer_ref[...] = mixer
    act = inner * jax.nn.sigmoid(inner)
    mix = mixer * jax.nn.sigmoid(mixer)
    half = mix.shape[1] // 2
    step, rate, cumulative, row, col, lower = decays(raw_ref[...], bias_ref[...], log_ref[...])
    last = cumulative[length - 1 : length, :]
    spread = head_mask(width, True)
    tail = exact(jnp.exp(last - cumulative) * step, spread)
    grown = exact(jnp.exp(cumulative), spread)
    upstream = grad_ref[...].astype(F32)
    state_ref[...] = mm(act * tail, mix[:, :half], 0, 0).astype(BF)
    back_ref[...] = mm(grown * upstream, mix[:, half:], 0, 0).astype(BF)
    row_decay = jnp.sum(head_mask(width, False) * jnp.exp(last), axis=1, keepdims=True)
    decay_ref[...] = jnp.broadcast_to(row_decay, decay_ref.shape)


def backward_kernel(
    heads, inner_ref, mixer_ref, raw_ref, conv_inner_ref, conv_mixer_ref, bias_ref, log_ref,
    skip_ref, grad_ref, start_ref, end_ref,
    out_ref, step_ref, z_ref, y_ref, pad_inner, pad_mixer,
):
    length = raw_ref.shape[0]
    width = conv_inner_ref.shape[1]
    taps = conv_inner_ref.shape[0]
    spread = head_mask(width, True)
    spread_down = head_mask(width, False)
    start, end = start_ref[...].astype(F32), end_ref[...].astype(F32)
    inner, mixer = inner_ref[...], mixer_ref[...]
    inner_gate, mixer_gate = jax.nn.sigmoid(inner), jax.nn.sigmoid(mixer)
    act, mix = inner * inner_gate, mixer * mixer_gate
    half = mix.shape[1] // 2
    into, out_of = mix[:, :half], mix[:, half:]
    raw = raw_ref[...]
    step, rate, cumulative, row, col, lower = decays(raw, bias_ref[...], log_ref[...])
    last = cumulative[length - 1 : length, :]
    step_wide = exact(step, spread)
    grown = exact(jnp.exp(cumulative), spread)
    fading = exact(jnp.exp(last - cumulative), spread)
    upstream_low = grad_ref[...]
    upstream = upstream_low.astype(F32)
    stepped_low = (act * step_wide).astype(BF)
    stepped = stepped_low.astype(F32)
    scores = mm(out_of, into, 1, 1)
    causal = row >= col
    across = cumulative.T
    score_grad = jnp.zeros((length, length), F32)
    for h in range(heads):
        cols = slice(h * HDIM, (h + 1) * HDIM)
        gap = cumulative[:, h : h + 1] - across[h : h + 1, :]
        decay = jnp.where(causal, jnp.exp(jnp.where(causal, gap, 0.0)), 0.0)
        weights = (decay * scores).astype(BF)
        grad_h, step_h = upstream_low[:, cols], stepped_low[:, cols]
        score_grad = score_grad + decay * mm(grad_h, step_h, 1, 1)
        z_ref[:, cols] = mm(weights, grad_h, 0, 0)
        y_ref[:, cols] = mm(weights, step_h, 1, 0)
    z = z_ref[...]
    carried = grown * mm(out_of, start, 1, 1)
    ending = fading * mm(into, end, 1, 1)
    act_grad = step_wide * (z + ending) + exact(skip_ref[...], spread)[0:1, :] * upstream
    to_heads = functools.partial(exact, b=spread, da=1, db=1)
    step_grad = to_heads(act * (z + ending))
    tail_term = to_heads(stepped * ending)
    sum_grad = to_heads(upstream * (y_ref[...] + carried) - stepped * z) - tail_term
    held = jnp.sum(start * end, axis=1, keepdims=True)
    overall = jnp.sum(tail_term, axis=0, keepdims=True) + jnp.exp(last) * jnp.sum(
        spread_down * held, axis=0, keepdims=True
    )
    decay_grad = exact(lower, sum_grad, 0, 0) + overall
    step_grad = (step_grad - rate * decay_grad) * jax.nn.sigmoid(raw + bias_ref[...])
    out_grad = mm(score_grad, into, 1, 0) + mm(grown * upstream, start, 1, 0)
    into_grad = mm(score_grad, out_of, 0, 0) + mm(fading * stepped, end, 1, 0)
    inner_slope = inner_gate * (1.0 + inner * (1.0 - inner_gate))
    mixer_slope = mixer_gate * (1.0 + mixer * (1.0 - mixer_gate))
    for pad in (pad_inner, pad_mixer):
        pad[0:PAD, :] = jnp.zeros((PAD, pad.shape[1]), F32)
        pad[PAD + length :, :] = jnp.zeros((PAD, pad.shape[1]), F32)
    pad_inner[PAD : PAD + length, :] = act_grad * inner_slope
    pad_mixer[PAD : PAD + length, :half] = into_grad * mixer_slope[:, :half]
    pad_mixer[PAD : PAD + length, half:] = out_grad * mixer_slope[:, half:]

    def spread_back(pad, kernel):
        total = None
        for k in range(taps):
            term = kernel[k : k + 1, :] * pad[pl.ds(taps - 1 - k, PAD + length), :]
            total = term if total is None else total + term
        return total.astype(BF)

    mixer_end = width + 2 * half
    inner_back = spread_back(pad_inner, conv_inner_ref)
    out_ref[:, 0:width] = inner_back
    out_ref[0:PAD, 0:LANES] = (inner_back[0:PAD, 0:LANES].astype(F32) + step_grad.T[0:PAD, :]).astype(BF)
    out_ref[:, width:mixer_end] = spread_back(pad_mixer, conv_mixer_ref)
    step_ref[...] = step_grad.astype(BF)


def local_call(kernel, out_shapes, scratch, name, *arrays):
    vmem = pl.BlockSpec(memory_space=pltpu.VMEM)
    return pl.pallas_call(
        kernel,
        out_shape=out_shapes,
        in_specs=[vmem] * len(arrays),
        out_specs=jax.tree.map(lambda unused: vmem, out_shapes),
        scratch_shapes=scratch,
        compiler_params=pltpu.CompilerParams(vmem_limit_bytes=LIMIT),
        name=name,
    )(*arrays)


def rows_dot(gradient, weight):
    return lax.dot_general(
        gradient, weight, (((1,), (1,)), ((), ())), preferred_element_type=F32
    )


def body(
    sizes,
    layer_input,
    inner_weight,
    mixer_weight,
    step_weight,
    conv_inner,
    conv_mixer,
    step_bias,
    decay_log,
    skip_gain,
    output_grad,
):
    own = layer_input[0]
    rows, model = own.shape
    chans, seqs, dps = sizes["chan"], sizes["seq"], sizes["dp"]
    groups = dps * seqs
    length = rows * chans
    width = inner_weight.shape[1]
    mixed = mixer_weight.shape[1]
    heads = step_bias.shape[0]
    blocks = own.reshape(rows, dps, seqs, model // groups).transpose(1, 2, 0, 3)
    gathered, own_columns, history = exchange(
        sizes, 0, ((("chan",), "gather"), (("dp",), "swap")), (own, blocks), "down"
    )
    history = jnp.where(lax.axis_index("seq") > 0, history, jnp.zeros_like(history))
    tokens = jnp.concatenate([history, gathered.reshape(length, model)], axis=0)
    lane_pad = ((0, 0), (0, LANES - heads))
    step_wide = jnp.pad(step_weight, lane_pad)
    inner_proj = jnp.dot(tokens, inner_weight, preferred_element_type=F32).astype(BF)
    mixer_proj = jnp.dot(tokens, mixer_weight, preferred_element_type=F32).astype(BF)
    step_raw = jnp.dot(tokens[PAD:], step_wide, preferred_element_type=F32)
    vectors = jnp.pad(jnp.stack((step_bias, decay_log, skip_gain)), ((0, 5), lane_pad[1]))
    bias, rates, skips = vectors[0:1], vectors[1:2], vectors[2:3]
    upstream = output_grad[0]
    inner_sum, mixer_sum, state, back_state, decay = local_call(
        forward_kernel,
        (
            jax.ShapeDtypeStruct((length, width), F32),
            jax.ShapeDtypeStruct((length, mixed), F32),
            jax.ShapeDtypeStruct((width, mixed // 2), BF),
            jax.ShapeDtypeStruct((width, mixed // 2), BF),
            jax.ShapeDtypeStruct((width, mixed // 2), F32),
        ),
        [pltpu.VMEM((PAD + length, width), F32), pltpu.VMEM((PAD + length, mixed), F32)],
        "forward",
        inner_proj, mixer_proj, step_raw, conv_inner, conv_mixer, bias, rates, upstream,
    )
    columns, start, end = exchange(
        sizes,
        1,
        ((("seq",), "cross"),),
        (own_columns,),
        plug=Chain(),
        plug_arrays=(state, back_state, decay),
    )
    assert length == LANES and heads + conv_inner.shape[0] - 1 <= PAD
    grads, step_grads = local_call(
        functools.partial(backward_kernel, heads),
        (
            jax.ShapeDtypeStruct((PAD + length, width + mixed), BF),
            jax.ShapeDtypeStruct((length, LANES), BF),
        ),
        [
            pltpu.VMEM((length, width), F32),
            pltpu.VMEM((length, width), F32),
            pltpu.VMEM((2 * PAD + length, width), F32),
            pltpu.VMEM((2 * PAD + length, mixed), F32),
        ],
        "backward",
        inner_sum, mixer_sum, step_raw, conv_inner, conv_mixer, bias, rates,
        jnp.broadcast_to(skips, (8, LANES)), upstream, start, end,
    )
    partial = rows_dot(grads[:, :width], inner_weight)
    partial = partial + rows_dot(grads[:, width:], mixer_weight)
    main_part = (partial[PAD:] + rows_dot(step_grads, step_wide)).astype(BF)
    tail_part = partial[:PAD].astype(BF)
    parts = main_part.reshape(chans, rows, model)
    parts, columns, tails, all_grads = exchange(
        sizes,
        2,
        ((("chan",), "swap"), (("chan",), "gather")),
        (parts, columns),
        "up",
        tail_part,
        Grid(),
        (grads,),
    )
    total = jnp.sum(parts.astype(F32), axis=0)
    reached = (lax.axis_index("chan") == chans - 1) & (lax.axis_index("seq") < seqs - 1)
    live = lax.broadcasted_iota(jnp.int32, (PAD, 1), 0) > PAD - conv_inner.shape[0]
    tail_sum = jnp.where(reached & live, jnp.sum(tails.astype(F32), axis=0), 0.0)
    total = jnp.concatenate([total[: rows - PAD], total[rows - PAD :] + tail_sum], axis=0)
    input_grad = total.astype(BF)

    split = all_grads
    main, early = split[:, :, PAD:], jnp.where(live, split[:, :, :PAD], 0)
    steps = split[:, :, :heads, :LANES].transpose(0, 1, 3, 2).reshape(groups * length, heads)
    early = jnp.concatenate([early[:, 1:], jnp.zeros_like(early[:, :1])], axis=1)
    final = (main[:, :, length - PAD :].astype(F32) + early.astype(F32)).astype(BF)
    main = jnp.concatenate([main[:, :, : length - PAD], final], axis=2)
    main = main.reshape(groups * length, -1)
    columns = columns.transpose(2, 1, 0, 3, 4).reshape(groups * length, model // groups)
    norm_factor = 1.0 / math.sqrt(groups * length)

    def term(right):
        dims = (((0,), (0,)), ((), ()))
        return norm_factor * lax.dot_general(columns, right, dims, preferred_element_type=F32)

    mixer_terms = term(main[:, width:]).reshape(chans, -1, mixed)
    (mixer_parts,) = exchange(sizes, 3, ((("chan",), "swap"),), (mixer_terms,))
    mixer_weight_grad = jnp.sum(mixer_parts, axis=0)
    return (
        input_grad[None],
        term(main[:, :width]),
        mixer_weight_grad,
        term(steps),
    )


def solution(mesh):
    sizes = dict(mesh.shape)
    in_specs = (
        P("dp", ("seq", "chan"), None),
        P(None, "chan"),
        P(),
        P(None, "chan"),
        P(None, "chan"),
        P(),
        P("chan"),
        P("chan"),
        P("chan"),
        P("dp", "seq", "chan"),
    )
    out_specs = (
        P("dp", ("seq", "chan"), None),
        P(("dp", "seq"), "chan"),
        P(("dp", "seq", "chan"), None),
        P(("dp", "seq"), "chan"),
    )
    return jax.shard_map(
        functools.partial(body, sizes),
        mesh=mesh,
        in_specs=in_specs,
        out_specs=out_specs,
        check_vma=False,
    )
```

profile of v0, /device:TPU:0, one launch (start us, length us, event | category | flops | bytes accessed | tf_op | source)
XLA Modules:
  0.0 124.9 jit_solution(10790694993485800842)
XLA Ops:
  0.7 0.9 select_maximum_fusion
  2.7 1.1 reshape_squeeze.3
  4.6 16.7 %exchange_0.1 = (bf16[4,32,2560]{2,1,0:T(8,128)(2,1)}, bf16[2,4,32,320]{3,2,1,0:T(8,128)(2,1)}, bf16[16,2560]{1,0:T(8,128)(2,1)}) custom-call(bf16[32,2560]{1,0:T(8,128)(2,1)} %bitcast.44, bf16[2,4,32,320]{3,2,1,0:T(8,128)(2,1)} %bitcast.41), custom_call_target="tpu_custom_call" | custom-call | tf_op jit(solution)/shard_map/exchange_0/pallas_call | solution.py:420
  21.4 2.0 %fusion.7.raw_ref = f32[128,128]{1,0:T(8,128)} fusion(bf16[128,2560]{1,0:T(8,128)(2,1)} %bitcast.49, bf16[2560,10]{0,1:T(8,128)(2,1)} %param.13), kind=kOutput, calls=%fused_computation.13 | convolution fusion | flops 83886080 | bytes 772096 | tf_op jit(solution)/shard_map/dot_general | solution.py:632
  23.4 2.6 %convolution_convert_fusion.1.mixer_ref = bf16[144,256]{1,0:T(8,128)(2,1)} fusion(bf16[2560,256]{1,0:T(8,128)(2,1)} %param.12, bf16[128,2560]{1,0:T(8,128)(2,1)} %bitcast.50, bf16[16,2560]{1,0:T(8,128)(2,1)S(1)} %broadcast_select_fusion), kind=kOutput, calls=%fused_computation.10 | convolution fusion | flops 190255104 | bytes 2121728 | tf_op jit(solution)/shard_map/dot_general | solution.py:631
  26.0 1.4 %convolution_convert_fusion.inner_ref = bf16[144,640]{1,0:T(8,128)(2,1)} fusion(bf16[2560,640]{1,0:T(8,128)(2,1)S(1)} %copy-done, bf16[128,2560]{1,0:T(8,128)(2,1)S(1)} %bitcast.51, bf16[16,2560]{1,0:T(8,128)(2,1)S(1)} %broadcast_select_fusion), kind=kOutput, calls=%fused_computation.9 | convolution fusion | flops 473425920 | bytes 4198400 | tf_op jit(solution)/shard_map/dot_general | solution.py:630
  27.4 3.1 %forward.1 = (f32[128,640]{1,0:T(8,128)}, f32[128,256]{1,0:T(8,128)}, bf16[640,128]{1,0:T(8,128)(2,1)}, bf16[640,128]{1,0:T(8,128)(2,1)}, f32[640,128]{1,0:T(8,128)}) custom-call(bf16[144,640]{1,0:T(8,128)(2,1)} %convolution_convert_fusion.inner_ref, bf16[144,256]{1,0:T(8,128)(2,1)} %convolution_convert_fusion.1.mixer_ref, f32[128,128]{1,0:T(8,128)} %fusion.7.raw_ref, ...), custom_call_target="tpu_custom_call" | custom-call | tf_op jit(solution)/shard_map/forward/pallas_call | solution.py:584
  30.5 26.8 %exchange_1.1 = (bf16[4,2,32,320]{3,2,1,0:T(8,128)(2,1)}, bf16[640,128]{1,0:T(8,128)(2,1)}, bf16[640,128]{1,0:T(8,128)(2,1)}) custom-call(bf16[2,4,32,320]{3,2,1,0:T(8,128)(2,1)} %get-tuple-element.25.refs_0_, bf16[640,128]{1,0:T(8,128)(2,1)} %get-tuple-element.26.refs_1_, bf16[640,128]{1,0:T(8,128)(2,1)} %get-tuple-element.27.refs_2_, ...), custom_call_target="tpu_custom_call" | custom-call | tf_op jit(solution)/shard_map/exchange_1/pallas_call | solution.py:420
  57.2 5.5 %backward.1 = (bf16[144,896]{1,0:T(8,128)(2,1)}, bf16[128,128]{1,0:T(8,128)(2,1)}) custom-call(f32[128,640]{1,0:T(8,128)} %get-tuple-element.23.inner_ref, f32[128,256]{1,0:T(8,128)} %get-tuple-element.24.mixer_ref, f32[128,128]{1,0:T(8,128)} %fusion.7.raw_ref, f32[4,640]{1,0:T(4,128)} %conv_inner_ref.3, f32[4,256]{1,0:T(4,128)} %conv_mixer_ref.3, ...), custom_call_target="tpu_custom_call" | custom-call | tf_op jit(solution)/shard_map/backward/pallas_call | solution.py:584
  62.7 2.2 %fusion.10 = f32[144,2560]{1,0:T(8,128)S(1)} fusion(bf16[2560,640]{1,0:T(8,128)(2,1)S(1)} %copy-done, bf16[144,896]{1,0:T(8,128)(2,1)} %get-tuple-element.31.refs_3_), kind=kOutput, calls=%fused_computation.20 | convolution fusion | flops 471859200 | bytes 4935680 | tf_op jit(solution)/shard_map/dot_general | solution.py:596
  65.0 1.5 %convolution_add_fusion = f32[144,2560]{1,0:T(8,128)S(1)} fusion(f32[144,2560]{1,0:T(8,128)S(1)} %fusion.10, bf16[2560,256]{1,0:T(8,128)(2,1)S(1)} %copy-done.2, bf16[144,896]{1,0:T(8,128)(2,1)} %get-tuple-element.31.refs_3_), kind=kOutput, calls=%fused_computation | convolution fusion | flops 189112320 | bytes 4333568 | tf_op jit(solution)/shard_map/dot_general | solution.py:596
  67.2 1.1 fusion
  68.3 34.0 %exchange_2.1 = (bf16[4,32,2560]{2,1,0:T(8,128)(2,1)}, bf16[4,4,2,32,320]{4,3,2,1,0:T(8,128)(2,1)}, bf16[4,16,2560]{2,1,0:T(8,128)(2,1)}, bf16[2,4,144,896]{3,2,1,0:T(8,128)(2,1)}) custom-call(bf16[4,32,2560]{2,1,0:T(8,128)(2,1)} %bitcast.37, bf16[4,2,32,320]{3,2,1,0:T(8,128)(2,1)} %get-tuple-element.33.refs_1_, bf16[16,2560]{1,0:T(8,128)(2,1)} %slice.100.refs_2_, ...), custom_call_target="tpu_custom_call" | custom-call | tf_op jit(solution)/shard_map/exchange_2/pallas_call | solution.py:420
  102.3 1.9 %convert_reduce_fusion = f32[32,2560]{1,0:T(8,128)} fusion(bf16[4,32,2560]{2,1,0:T(8,128)(2,1)} %get-tuple-element.34), kind=kLoop, calls=%fused_computation.6 | loop fusion | flops 573440 | bytes 983040 | tf_op jit(solution)/shard_map/reduce_sum | solution.py:689
  105.0 1.1 fusion.13
  106.1 1.0 convert_reduce_fusion.1
  107.1 1.0 fusion.14
  108.8 1.0 slice.64
  110.4 0.9 copy-done.3
  111.3 0.8 convolution_multiply_fusion.1
  112.2 1.1 convolution_multiply_fusion
  113.3 1.6 %fusion.3 = f32[320,640]{1,0:T(8,128)} fusion(bf16[1024,320]{1,0:T(8,128)(2,1)S(1)} %bitcast.36, bf16[1024,896]{1,0:T(8,128)(2,1)S(1)} %bitcast.39), kind=kOutput, calls=%fused_computation.7 | convolution fusion | flops 419635200 | bytes 2916352 | tf_op jit(solution)/shard_map/dot_general | solution.py:708
  114.9 8.4 %exchange_3.1 = f32[4,80,256]{2,1,0:T(8,128)} custom-call(f32[4,80,256]{2,1,0:T(8,128)} %bitcast.45), custom_call_target="tpu_custom_call" | custom-call | tf_op jit(solution)/shard_map/exchange_3/pallas_call | solution.py:420
  123.3 1.6 %reduce_sum.29 = f32[80,256]{1,0:T(8,128)} reduce(f32[4,80,256]{2,1,0:T(8,128)} %exchange_3.1, f32[]{:T(128)} %constant.6.clone.1), dimensions={0}, to_apply=%region_2.3 | reduce | flops 61440 | bytes 409604 | tf_op jit(solution)/shard_map/reduce_sum | solution.py:712
  (29 shorter events, 4.7 us)
Async XLA Ops:
  0.6 25.3 %copy-start = (bf16[2560,640]{1,0:T(8,128)(2,1)S(1)}, bf16[2560,640]{1,0:T(8,128)(2,1)}, u32[]{:S(2)}) copy-start(bf16[2560,640]{1,0:T(8,128)(2,1)} %param.11) | copy-start | bytes 9830404
  23.4 2.6 %copy-start.6 = (bf16[4,32,2560]{2,1,0:T(8,128)(2,1)S(1)}, bf16[4,32,2560]{2,1,0:T(8,128)(2,1)}, u32[]{:S(2)}) copy-start(bf16[4,32,2560]{2,1,0:T(8,128)(2,1)} %get-tuple-element.22) | copy-start | bytes 1966084
  62.7 2.2 %copy-start.2 = (bf16[2560,256]{1,0:T(8,128)(2,1)S(1)}, bf16[2560,256]{1,0:T(8,128)(2,1)}, u32[]{:S(2)}) copy-start(bf16[2560,256]{1,0:T(8,128)(2,1)} %param.12) | copy-start | bytes 3932164
  65.0 2.2 %copy-start.4 = (bf16[2560,10]{0,1:T(8,128)(2,1)S(1)}, bf16[2560,10]{0,1:T(8,128)(2,1)}, u32[]{:S(2)}) copy-start(bf16[2560,10]{0,1:T(8,128)(2,1)} %param.13) | copy-start | bytes 153604
  65.0 2.2 %copy-start.5 = (bf16[128,128]{1,0:T(8,128)(2,1)S(1)}, bf16[128,128]{1,0:T(8,128)(2,1)}, u32[]{:S(2)}) copy-start(bf16[128,128]{1,0:T(8,128)(2,1)} %get-tuple-element.32) | copy-start | bytes 98308
  105.0 4.9 %copy-start.1 = (bf16[2,4,144,896]{3,2,1,0:T(8,128)(2,1)S(1)}, bf16[2,4,144,896]{3,2,1,0:T(8,128)(2,1)}, u32[]{:S(2)}) copy-start(bf16[2,4,144,896]{3,2,1,0:T(8,128)(2,1)} %get-tuple-element.37) | copy-start | bytes 6193156
  110.1 1.1 copy-start.3
where the time goes:
time: 126 us; the launch traced here: 125 us
  Pallas kernels  94.5 us (75%)
  matrix products  14.4 us (11%)
  local copies, waits for them, and re-layouts  7.62 us (6%)
  other arithmetic  7.56 us (6%)
    pallas_call x4, Pallas kernels, exchange(): pl.pallas_call(functools.partial(exchange_kernel, tuple(plan), tail, plug...  85.9 us
    pallas_call x2, Pallas kernels, local_call(): pl.pallas_call(kernel, out_shape=out_shapes, in_specs=[vmem] * len(arrays...  8.6 us
    dot_general x3, matrix products, rows_dot(): lax.dot_general(gradient, weight, (((1,), (1,)), ((), ())), preferred_ele...  4.85 us
    dot_general x3, matrix products, term(): lax.dot_general(columns, right, dims, preferred_element_type=F32)  3.57 us
    dot_general x1, matrix products, body(): jnp.dot(tokens, mixer_weight, preferred_element_type=F32).astype(BF)  2.58 us

commit v1 on v0

--- a/solution.py
+++ b/solution.py
@@ -231,30 +231,38 @@
             def _(way=way):
                 self.outs[way][...] = jnp.zeros(self.outs[way].shape, BF)
 
-    def run(self):
+    def beat(self, t):
         me = lax.axis_index("seq")
         rows = self.outs[0].shape[0] // self.pieces
-
-        def beat(t):
-            for way in (0, 1):
-                place = me if way == 0 else self.n - 1 - me
-                piece = t - place
-                active = (piece >= 0) & (piece < self.pieces)
-
-                @pl.when(active & (place > 0))
-                def _(way=way, piece=piece):
-                    self.copy(way, piece).wait_recv()
-
-                @pl.when(active & (place < self.n - 1))
-                def _(way=way, piece=piece):
-                    part = pl.ds(pl.multiple_of(piece * rows, rows), rows)
-                    before = self.outs[way][part, :].astype(F32)
-                    term = self.ins[way][part, :].astype(F32)
-                    self.scratch[way][part, :] = (self.ins[2][part, :] * before + term).astype(BF)
-                    self.copy(way, piece).start()
-
-        beat(0)
-        each(self.n - 1 + self.pieces, beat)
+        for way in (0, 1):
+            place = me if way == 0 else self.n - 1 - me
+            piece = t - place
+            active = (piece >= 0) & (piece < self.pieces)
+
+            @pl.when(active & (place > 0))
+            def _(way=way, piece=piece):
+                self.copy(way, piece).wait_recv()
+
+            @pl.when(active & (place < self.n - 1))
+            def _(way=way, piece=piece):
+                part = pl.ds(pl.multiple_of(piece * rows, rows), rows)
+                before = self.outs[way][part, :].astype(F32)
+                term = self.ins[way][part, :].astype(F32)
+                self.scratch[way][part, :] = (self.ins[2][part, :] * before + term).astype(BF)
+                self.copy(way, piece).start()
+
+    def run(self, middle):
+        me = lax.axis_index("seq")
+        half = self.pieces
+        for t in range(1, half):
+            self.beat(t)
+        middle()
+        rest = self.n - 1
+        if rest <= 12:
+            for t in range(half, half + rest):
+                self.beat(t)
+        else:
+            lax.fori_loop(half, half + rest, lambda t, c: (self.beat(t), c)[1], 0)
 
         for way in (0, 1):
 
@@ -262,134 +270,6 @@
             def _(way=way):
                 for piece in range(self.pieces):
                     self.copy(way, piece).wait_send()
-
-
-class Grid:
-    counts = (1, 1, 10)
-
-    def shapes(self, sizes, arrays):
-        d, n = sizes["dp"], sizes["seq"]
-        shape = jax.ShapeDtypeStruct((d, n) + arrays[0].shape, BF)
-        lengths = (n, d * n, d, d * n, n, n, d * n, d, d * n, d * n)
-        return [shape], [pltpu.SemaphoreType.DMA((k,)) for k in lengths]
-
-    def bind(self, sizes, ins, outs, scratch):
-        bound = Grid()
-        bound.d, bound.n = sizes["dp"], sizes["seq"]
-        bound.src, bound.out, bound.sems = ins[0], outs[0], scratch
-        return bound
-
-    def greet(self, barrier):
-        mine = lax.axis_index("dp")
-        for e in range(1, self.d):
-            signal_to(barrier, {"dp": lax.rem(mine + e, self.d)})
-        return greet_line(barrier, self.n) + self.d - 1
-
-    def copy(self, half, way, e, k, own=False, target=None):
-        rows = self.src.shape[0]
-        cut = (rows * 5 // 6) // 16 * 16
-        part = pl.ds(0, cut) if half == 0 else pl.ds(cut, rows - cut)
-        me = lax.axis_index("seq")
-        slot = e * self.n + k
-        if way == "cross":
-            where = {"dp": lax.axis_index("dp") if target is None else target}
-            recv = self.sems[1].at[slot] if half == 0 else self.sems[2].at[e]
-            to = 0 if target is None else target
-            send = self.sems[6].at[to * self.n + k] if half == 0 else self.sems[7].at[to]
-        else:
-            shift = 1 if way == "up" else self.n - 1
-            where = {"seq": lax.rem(me + shift, self.n)}
-            recv = self.sems[0].at[k] if half == 0 else self.sems[3].at[slot]
-            ups = 4 if way == "up" else 5
-            send = self.sems[ups].at[k] if half == 0 else self.sems[ups + 4].at[slot]
-        src = self.src.at[part] if own else self.out.at[e, k, part]
-        return pltpu.make_async_remote_copy(
-            src_ref=src,
-            dst_ref=self.out.at[e, k, part],
-            send_sem=send,
-            recv_sem=recv,
-            device_id=where,
-            device_id_type=MESH,
-        )
-
-    def partners(self):
-        mine = lax.axis_index("dp")
-        return [lax.rem(mine + e, self.d) for e in range(1, self.d)]
-
-    def both(self, half, e, k, own=False):
-        me = lax.axis_index("seq")
-
-        @pl.when(me < self.n - 1)
-        def _():
-            self.copy(half, "up", e, k, own).start()
-
-        @pl.when(me > 0)
-        def _():
-            self.copy(half, "down", e, k, own).start()
-
-    def start(self):
-        mine, me = lax.axis_index("dp"), lax.axis_index("seq")
-        for e in self.partners():
-            self.copy(1, "cross", mine, me, True, e).start()
-        self.both(1, mine, me, True)
-        self.both(0, mine, me, True)
-        for e in self.partners():
-            self.copy(0, "cross", mine, me, True, e).start()
-        self.out[mine, me] = self.src[...]
-
-    def run(self):
-        mine, me, n = lax.axis_index("dp"), lax.axis_index("seq"), self.n
-        others = self.partners()
-        for e in others:
-            self.copy(1, "cross", e, me, target=e).wait_recv()
-            self.both(1, e, me)
-
-        def hop(d):
-            for way, k, there, onward in (
-                ("up", me - d, me >= d, me < n - 1),
-                ("down", me + d, me + d < n, me > 0),
-            ):
-                for e in [mine] + others:
-
-                    @pl.when(there)
-                    def _(way=way, k=k, e=e):
-                        self.copy(1, way, e, k).wait_recv()
-
-                    @pl.when(there & onward)
-                    def _(way=way, k=k, e=e):
-                        self.copy(1, way, e, k).start()
-
-                @pl.when(there)
-                def _(way=way, k=k):
-                    self.copy(0, way, mine, k).wait_recv()
-
-                @pl.when(there & onward)
-                def _(way=way, k=k):
-                    self.copy(0, way, mine, k).start()
-
-                @pl.when(there)
-                def _(way=way, k=k):
-                    for e in others:
-                        self.copy(0, "cross", mine, k, target=e).start()
-
-        each(n, hop)
-
-        def settle(k):
-            for e in others:
-                self.copy(0, "cross", e, k, target=e).wait_recv()
-                self.copy(0, "cross", mine, k, target=e).wait_send()
-            for way, sent in (("up", (k <= me) & (me < n - 1)), ("down", (k >= me) & (me > 0))):
-
-                @pl.when(sent)
-                def _(way=way, k=k):
-                    self.copy(0, way, mine, k).wait_send()
-                    for e in [mine] + others:
-                        self.copy(1, way, e, k).wait_send()
-
-        settle(0)
-        each(n, settle)
-        for e in others:
-            self.copy(1, "cross", mine, me, target=e).wait_send()
 
 
 def exchange(sizes, call_id, jobs, arrays, tail=None, tail_array=None, plug=None, plug_arrays=()):
@@ -501,13 +381,11 @@
 
 
 def backward_kernel(
-    heads, inner_ref, mixer_ref, raw_ref, conv_inner_ref, conv_mixer_ref, bias_ref, log_ref,
-    skip_ref, grad_ref, start_ref, end_ref,
-    out_ref, step_ref, z_ref, y_ref, pad_inner, pad_mixer,
+    heads, inner_ref, mixer_ref, raw_ref, bias_ref, log_ref, skip_ref, grad_ref, start_ref, end_ref,
+    a_in_ref, a_mix_ref, step_ref, z_ref, y_ref,
 ):
     length = raw_ref.shape[0]
-    width = conv_inner_ref.shape[1]
-    taps = conv_inner_ref.shape[0]
+    width = inner_ref.shape[1]
     spread = head_mask(width, True)
     spread_down = head_mask(width, False)
     start, end = start_ref[...].astype(F32), end_ref[...].astype(F32)
@@ -557,26 +435,362 @@
     into_grad = mm(score_grad, out_of, 0, 0) + mm(fading * stepped, end, 1, 0)
     inner_slope = inner_gate * (1.0 + inner * (1.0 - inner_gate))
     mixer_slope = mixer_gate * (1.0 + mixer * (1.0 - mixer_gate))
-    for pad in (pad_inner, pad_mixer):
-        pad[0:PAD, :] = jnp.zeros((PAD, pad.shape[1]), F32)
-        pad[PAD + length :, :] = jnp.zeros((PAD, pad.shape[1]), F32)
-    pad_inner[PAD : PAD + length, :] = act_grad * inner_slope
-    pad_mixer[PAD : PAD + length, :half] = into_grad * mixer_slope[:, :half]
-    pad_mixer[PAD : PAD + length, half:] = out_grad * mixer_slope[:, half:]
-
-    def spread_back(pad, kernel):
+    a_in_ref[...] = act_grad * inner_slope
+    a_mix_ref[:, :half] = into_grad * mixer_slope[:, :half]
+    a_mix_ref[:, half:] = out_grad * mixer_slope[:, half:]
+    step_ref[...] = step_grad
+
+
+def rcopy(src, dst, send, recv, **where):
+    return pltpu.make_async_remote_copy(
+        src_ref=src, dst_ref=dst, send_sem=send, recv_sem=recv, device_id=where, device_id_type=MESH
+    )
+
+
+def greet_all(barrier, axis, n):
+    me = lax.axis_index(axis)
+    each(n, lambda d: signal_to(barrier, {axis: lax.rem(me + d, n)}))
+    return n - 1
+
+
+def mid_kernel(
+    sizes, cols, state, back, decay, xc, start, end, scr0, scr1, xs, cross_s, cross_r, gat_s, gat_r, *chain_sems
+):
+    n, chans = sizes["seq"], sizes["chan"]
+    me, ch = lax.axis_index("seq"), lax.axis_index("chan")
+    barrier = pltpu.get_barrier_semaphore()
+    total = greet_all(barrier, "seq", n) + greet_all(barrier, "chan", chans)
+    chain = Chain()
+    chain.n, chain.ins, chain.outs = n, (state, back, decay), (start, end)
+    chain.scratch = (scr0, scr1) + chain_sems
+    pl.semaphore_wait(barrier, total)
+    chain.start()
+
+    def cross(q, landing, slot):
+        return rcopy(cols.at[:, q], xs.at[landing], cross_s.at[q], cross_r.at[slot], seq=q)
+
+    def gather(q, landing, slot):
+        return rcopy(xs, xc.at[:, :, landing], gat_s.at[q], gat_r.at[slot], chan=q)
+
+    def middle():
+        each(n, lambda d: cross(lax.rem(me + d, n), me, lax.rem(me + d, n)).wait_recv())
+        each(chans, lambda d: gather(lax.rem(ch + d, chans), ch, ch).start())
+        xc[:, :, ch] = xs[...]
+
+    chain.beat(0)
+    each(n, lambda d: cross(lax.rem(me + d, n), me, me).start())
+    xs[me] = cols[:, me]
+    chain.run(middle)
+
+    def settle(d):
+        q = lax.rem(me + d, n)
+        cross(q, me, q).wait_send()
+
+    each(n, settle)
+
+    def settle_gather(d):
+        q = lax.rem(ch + d, chans)
+        gather(q, q, q).wait()
+
+    each(chans, settle_gather)
+
+
+def back_kernel(
+    sizes, heads,
+    a_in, a_mix, st, conv_in, conv_mix, w_in_h, w_mix_h, w_step_h, xc,
+    o_ig, o_dw, o_dwm, o_dws,
+    w_in, w_mix, w_step, pad_in, pad_mix, gin, gsm, hal_o, hal_i, gmp, gm_in, p_o, p_i, m_o, m_i,
+    w_sem, hal_sem, z_r, c_r, u_s, d_s, x_s, c2_r, z2_r, x2_s, u2_s, d2_s,
+    gm_s, gm_r, p_s, p_r, m_s, m_r,
+):
+    D, S, C = sizes["dp"], sizes["seq"], sizes["chan"]
+    mine, me, ch = lax.axis_index("dp"), lax.axis_index("seq"), lax.axis_index("chan")
+    length, width = a_in.shape
+    mixed = a_mix.shape[1]
+    taps = conv_in.shape[0]
+    model = w_in.shape[0]
+    rows = length // C
+    parts = C
+    barrier = pltpu.get_barrier_semaphore()
+    total = greet_all(barrier, "dp", D) + greet_all(barrier, "chan", C) + greet_line(barrier, S)
+    weights = [
+        pltpu.make_async_copy(h, v, w_sem.at[i])
+        for i, (h, v) in enumerate(((w_in_h, w_in), (w_mix_h, w_mix), (w_step_h, w_step)))
+    ]
+    for copy in weights:
+        copy.start()
+    hal_o[:, :width] = a_in[0:8, :]
+    hal_o[:, width:] = a_mix[0:8, :]
+    pad_in[0:length, :] = a_in[...]
+    pad_mix[0:length, :] = a_mix[...]
+    pad_in[length:, :] = jnp.zeros((8, width), F32)
+    pad_mix[length:, :] = jnp.zeros((8, mixed), F32)
+
+    def spread_back(pad, kernel, first, count):
         total = None
         for k in range(taps):
-            term = kernel[k : k + 1, :] * pad[pl.ds(taps - 1 - k, PAD + length), :]
+            term = kernel[k : k + 1, :] * pad[pl.ds(first + taps - 1 - k, count), :]
             total = term if total is None else total + term
         return total.astype(BF)
 
-    mixer_end = width + 2 * half
-    inner_back = spread_back(pad_inner, conv_inner_ref)
-    out_ref[:, 0:width] = inner_back
-    out_ref[0:PAD, 0:LANES] = (inner_back[0:PAD, 0:LANES].astype(F32) + step_grad.T[0:PAD, :]).astype(BF)
-    out_ref[:, width:mixer_end] = spread_back(pad_mixer, conv_mixer_ref)
-    step_ref[...] = step_grad.astype(BF)
+    last = length - rows
+    gin[me, mine, 0:last, :] = spread_back(pad_in, conv_in, 0, last)
+    gmp[0:last, :] = spread_back(pad_mix, conv_mix, 0, last)
+    gsm[me, mine, rows:, 0:LANES] = st[...].T[0:PAD, :].astype(BF)
+    pl.semaphore_wait(barrier, total)
+
+    def others():
+        return [lax.rem(mine + e, D) for e in range(1, D)]
+
+    def halo():
+        return rcopy(hal_o, hal_i, hal_sem.at[0], hal_sem.at[1], seq=lax.rem(me + S - 1, S))
+
+    @pl.when(me > 0)
+    def _():
+        halo().start()
+
+    def part(p, e, k):
+        return gin.at[k, e, pl.ds(p * rows, rows)]
+
+    def zcopy(p, way, k):
+        to = lax.rem(me + (1 if way == "up" else S - 1), S)
+        send = (u_s if way == "up" else d_s).at[p, k]
+        return rcopy(part(p, mine, k), part(p, mine, k), send, z_r.at[p, k], seq=to)
+
+    def ccopy(p, k, e, to):
+        return rcopy(part(p, e, k), part(p, e, k), x_s.at[p, to, k], c_r.at[p, e, k], dp=to)
+
+    def zsmall(way, e, k):
+        to = lax.rem(me + (1 if way == "up" else S - 1), S)
+        send = (u2_s if way == "up" else d2_s).at[e, k]
+        return rcopy(gsm.at[k, e], gsm.at[k, e], send, z2_r.at[e, k], seq=to)
+
+    def csmall(e, to):
+        return rcopy(gsm.at[me, e], gsm.at[me, e], x2_s.at[to], c2_r.at[e], dp=to)
+
+    def onward(make, k):
+        @pl.when(me < S - 1)
+        def _():
+            make("up", k).start()
+
+        @pl.when(me > 0)
+        def _():
+            make("down", k).start()
+
+    def own_part(p):
+        onward(functools.partial(zcopy, p), me)
+        for e in others():
+            ccopy(p, me, mine, e).start()
+
+    def forward(d, p):
+        for way, k, there, more in (
+            ("up", me - d, me >= d, me < S - 1),
+            ("down", me + d, me + d < S, me > 0),
+        ):
+
+            @pl.when(there)
+            def _(way=way, k=k):
+                zcopy(p, way, k).wait_recv()
+
+            @pl.when(there & more)
+            def _(way=way, k=k):
+                zcopy(p, way, k).start()
+
+            @pl.when(there)
+            def _(k=k):
+                for e in others():
+                    ccopy(p, k, mine, e).start()
+
+    def own_small():
+        for e in others():
+            csmall(mine, e).start()
+        onward(lambda way, k: zsmall(way, mine, k), me)
+
+    def cross_small():
+        for e in others():
+            csmall(e, e).wait_recv()
+            onward(lambda way, k, e=e: zsmall(way, e, k), me)
+
+    def forward_small(d):
+        for way, k, there, more in (
+            ("up", me - d, me >= d, me < S - 1),
+            ("down", me + d, me + d < S, me > 0),
+        ):
+            for e in [mine] + others():
+
+                @pl.when(there)
+                def _(way=way, k=k, e=e):
+                    zsmall(way, e, k).wait_recv()
+
+                @pl.when(there & more)
+                def _(way=way, k=k, e=e):
+                    zsmall(way, e, k).start()
+
+    norm = 1.0 / math.sqrt(D * S * length)
+
+    def columns_of(k):
+        block = xc[k]
+        return block.reshape(D * length, block.shape[-1])
+
+    def weight_term(k, first=False):
+        for e in others():
+            for p in range(parts):
+                ccopy(p, k, e, e).wait_recv()
+        x = columns_of(k)
+        term = norm * mm(x, gin[k].reshape(D * length, width), 0, 0)
+        o_dw[...] = term if first else o_dw[...] + term
+
+    def weight_terms(d):
+        for k, there in ((me - d, me >= d), (me + d, me + d < S)):
+
+            @pl.when(there)
+            def _(k=k):
+                weight_term(k)
+
+    for p in range(parts - 1):
+        own_part(p)
+
+    @pl.when(me < S - 1)
+    def _():
+        halo().wait_recv()
+        pad_in[length:, :] = hal_i[:, :width]
+        pad_mix[length:, :] = hal_i[:, width:]
+
+    gin[me, mine, last:, :] = spread_back(pad_in, conv_in, last, rows)
+    gmp[last:, :] = spread_back(pad_mix, conv_mix, last, rows)
+    own_part(parts - 1)
+
+    def share_mix(q, landing, slot):
+        return rcopy(gmp.at[pl.ds(q * rows, rows)], gm_in.at[landing], gm_s.at[q], gm_r.at[slot], chan=q)
+
+    each(C, lambda d: share_mix(lax.rem(ch + d, C), ch, ch).start())
+    for copy in weights:
+        copy.wait()
+    cut = model // parts
+
+    def share_p(j, q, landing, slot):
+        piece = pl.ds(j * cut, cut)
+        return rcopy(
+            p_o.at[q, :, piece], p_i.at[landing, :, piece], p_s.at[j, q], p_r.at[j, slot], chan=q
+        )
+
+    grads = gin[me, mine]
+    mixes = gmp[...]
+    steps = st[...].astype(BF)
+
+    def back_project(j):
+        piece = slice(j * cut, (j + 1) * cut)
+        out = mm(grads, w_in[piece, :], 1, 1) + mm(mixes, w_mix[piece, :], 1, 1)
+        out = out + mm(steps, w_step[piece, :], 1, 1)
+        p_o[:, :, piece] = out.astype(BF).reshape(C, rows, cut)
+        each(C, lambda d: share_p(j, lax.rem(ch + d, C), ch, ch).start())
+
+    def finish_mix():
+        gm_in[ch] = gmp[pl.ds(pl.multiple_of(ch * rows, rows), rows), :]
+        each(C, lambda d: share_mix(lax.rem(ch + d, C), ch, lax.rem(ch + d, C)).wait_recv())
+        mix = gm_in[0].astype(F32)
+        for q in range(1, C):
+            mix = mix + gm_in[q].astype(F32)
+        gsm[me, mine, 0:rows, :] = mix.astype(BF)
+        own_small()
+
+    for j in range(parts):
+        back_project(j)
+        forward(1, j)
+        if j == 0:
+            finish_mix()
+    weight_term(me, True)
+
+    def hop(d):
+        for p in range(parts):
+            forward(d, p)
+        if isinstance(d, int) and d == 2:
+            cross_small()
+        forward_small(d - 1)
+        weight_terms(d - 1)
+
+    hop(2)
+    if S > 3:
+        if S <= 12:
+            for d in range(3, S):
+                hop(d)
+        else:
+            lax.fori_loop(3, S, lambda d, c: (hop(d), c)[1], 0)
+    forward_small(S - 1)
+
+    mixer_columns = xc[:, :, ch].reshape(S * D * rows, xc.shape[-1])
+    mixer_grads = gsm[:, :, 0:rows, :].reshape(S * D * rows, mixed)
+    mixer_term = norm * mm(mixer_columns, mixer_grads, 0, 0)
+    band = mixer_term.shape[0] // C
+    for q in range(C):
+        m_o[q] = mixer_term[q * band : (q + 1) * band, :].astype(BF)
+
+    def share_m(q, landing, slot):
+        return rcopy(m_o.at[q], m_i.at[landing], m_s.at[q], m_r.at[slot], chan=q)
+
+    each(C, lambda d: share_m(lax.rem(ch + d, C), ch, ch).start())
+    step_total = None
+    for k in range(S) if S <= 12 else ():
+        for e in range(D):
+            x = xc[k, e].reshape(length, xc.shape[-1])
+            term = mm(x, gsm[k, e, rows:, 0:LANES], 0, 1)
+            step_total = term if step_total is None else step_total + term
+    if step_total is None:
+
+        def one(k, carry):
+            for e in range(D):
+                x = xc[k, e].reshape(length, xc.shape[-1])
+                carry = carry + mm(x, gsm[k, e, rows:, 0:LANES], 0, 1)
+            return carry
+
+        step_total = lax.fori_loop(0, S, one, jnp.zeros((xc.shape[-1], PAD), F32))
+    o_dws[...] = (norm * step_total)[:, :heads]
+
+    p_i[ch] = p_o[ch]
+    for j in range(parts):
+        each(C, lambda d, j=j: share_p(j, lax.rem(ch + d, C), ch, lax.rem(ch + d, C)).wait_recv())
+    total_ig = p_i[0].astype(F32)
+    for q in range(1, C):
+        total_ig = total_ig + p_i[q].astype(F32)
+    o_ig[...] = total_ig.astype(BF)
+    weight_terms(S - 1)
+    m_i[ch] = m_o[ch]
+    each(C, lambda d: share_m(lax.rem(ch + d, C), ch, lax.rem(ch + d, C)).wait_recv())
+    total_m = m_i[0].astype(F32)
+    for q in range(1, C):
+        total_m = total_m + m_i[q].astype(F32)
+    o_dwm[...] = total_m
+
+    @pl.when(me > 0)
+    def _():
+        halo().wait_send()
+
+    def settle_chan(d):
+        q = lax.rem(ch + d, C)
+        share_mix(q, ch, ch).wait_send()
+        share_m(q, ch, ch).wait_send()
+        for j in range(parts):
+            share_p(j, q, ch, ch).wait_send()
+
+    each(C, settle_chan)
+
+    def settle_line(k):
+        for e in others():
+            for p in range(parts):
+                ccopy(p, k, mine, e).wait_send()
+        for way, sent in (("up", (k <= me) & (me < S - 1)), ("down", (k >= me) & (me > 0))):
+
+            @pl.when(sent)
+            def _(way=way):
+                for p in range(parts):
+                    zcopy(p, way, k).wait_send()
+                for e in [mine] + others():
+                    zsmall(way, e, k).wait_send()
+
+    settle_line(0)
+    each(S, settle_line)
+    for e in others():
+        csmall(mine, e).wait_send()
 
 
 def local_call(kernel, out_shapes, scratch, name, *arrays):
@@ -590,12 +804,6 @@
         compiler_params=pltpu.CompilerParams(vmem_limit_bytes=LIMIT),
         name=name,
     )(*arrays)
-
-
-def rows_dot(gradient, weight):
-    return lax.dot_general(
-        gradient, weight, (((1,), (1,)), ((), ())), preferred_element_type=F32
-    )
 
 
 def body(
@@ -646,76 +854,86 @@
         "forward",
         inner_proj, mixer_proj, step_raw, conv_inner, conv_mixer, bias, rates, upstream,
     )
-    columns, start, end = exchange(
-        sizes,
-        1,
-        ((("seq",), "cross"),),
-        (own_columns,),
-        plug=Chain(),
-        plug_arrays=(state, back_state, decay),
-    )
     assert length == LANES and heads + conv_inner.shape[0] - 1 <= PAD
-    grads, step_grads = local_call(
+    cols = model // groups
+    dma = pltpu.SemaphoreType.DMA
+    vmem = pl.BlockSpec(memory_space=pltpu.VMEM)
+    hbm = pl.BlockSpec(memory_space=pl.ANY)
+    xc, start, end = pl.pallas_call(
+        functools.partial(mid_kernel, sizes),
+        out_shape=(
+            jax.ShapeDtypeStruct((seqs, dps, chans, rows, cols), BF),
+            jax.ShapeDtypeStruct(state.shape, BF),
+            jax.ShapeDtypeStruct(state.shape, BF),
+        ),
+        in_specs=[vmem] * 4,
+        out_specs=(vmem,) * 3,
+        scratch_shapes=[
+            pltpu.VMEM(state.shape, BF),
+            pltpu.VMEM(state.shape, BF),
+            pltpu.VMEM((seqs, dps, rows, cols), BF),
+            dma((seqs,)), dma((seqs,)), dma((chans,)), dma((chans,)),
+        ]
+        + [dma((Chain.pieces,)) for unused in range(4)],
+        compiler_params=pltpu.CompilerParams(
+            collective_id=1, has_side_effects=True, vmem_limit_bytes=LIMIT
+        ),
+        name="middle",
+    )(own_columns, state, back_state, decay)
+    a_in, a_mix, steps = local_call(
         functools.partial(backward_kernel, heads),
         (
-            jax.ShapeDtypeStruct((PAD + length, width + mixed), BF),
-            jax.ShapeDtypeStruct((length, LANES), BF),
+            jax.ShapeDtypeStruct((length, width), F32),
+            jax.ShapeDtypeStruct((length, mixed), F32),
+            jax.ShapeDtypeStruct((length, LANES), F32),
         ),
-        [
-            pltpu.VMEM((length, width), F32),
-            pltpu.VMEM((length, width), F32),
-            pltpu.VMEM((2 * PAD + length, width), F32),
-            pltpu.VMEM((2 * PAD + length, mixed), F32),
-        ],
+        [pltpu.VMEM((length, width), F32), pltpu.VMEM((length, width), F32)],
         "backward",
-        inner_sum, mixer_sum, step_raw, conv_inner, conv_mixer, bias, rates,
+        inner_sum, mixer_sum, step_raw, bias, rates,
         jnp.broadcast_to(skips, (8, LANES)), upstream, start, end,
     )
-    partial = rows_dot(grads[:, :width], inner_weight)
-    partial = partial + rows_dot(grads[:, width:], mixer_weight)
-    main_part = (partial[PAD:] + rows_dot(step_grads, step_wide)).astype(BF)
-    tail_part = partial[:PAD].astype(BF)
-    parts = main_part.reshape(chans, rows, model)
-    parts, columns, tails, all_grads = exchange(
-        sizes,
-        2,
-        ((("chan",), "swap"), (("chan",), "gather")),
-        (parts, columns),
-        "up",
-        tail_part,
-        Grid(),
-        (grads,),
-    )
-    total = jnp.sum(parts.astype(F32), axis=0)
-    reached = (lax.axis_index("chan") == chans - 1) & (lax.axis_index("seq") < seqs - 1)
-    live = lax.broadcasted_iota(jnp.int32, (PAD, 1), 0) > PAD - conv_inner.shape[0]
-    tail_sum = jnp.where(reached & live, jnp.sum(tails.astype(F32), axis=0), 0.0)
-    total = jnp.concatenate([total[: rows - PAD], total[rows - PAD :] + tail_sum], axis=0)
-    input_grad = total.astype(BF)
-
-    split = all_grads
-    main, early = split[:, :, PAD:], jnp.where(live, split[:, :, :PAD], 0)
-    steps = split[:, :, :heads, :LANES].transpose(0, 1, 3, 2).reshape(groups * length, heads)
-    early = jnp.concatenate([early[:, 1:], jnp.zeros_like(early[:, :1])], axis=1)
-    final = (main[:, :, length - PAD :].astype(F32) + early.astype(F32)).astype(BF)
-    main = jnp.concatenate([main[:, :, : length - PAD], final], axis=2)
-    main = main.reshape(groups * length, -1)
-    columns = columns.transpose(2, 1, 0, 3, 4).reshape(groups * length, model // groups)
-    norm_factor = 1.0 / math.sqrt(groups * length)
-
-    def term(right):
-        dims = (((0,), (0,)), ((), ()))
-        return norm_factor * lax.dot_general(columns, right, dims, preferred_element_type=F32)
-
-    mixer_terms = term(main[:, width:]).reshape(chans, -1, mixed)
-    (mixer_parts,) = exchange(sizes, 3, ((("chan",), "swap"),), (mixer_terms,))
-    mixer_weight_grad = jnp.sum(mixer_parts, axis=0)
-    return (
-        input_grad[None],
-        term(main[:, :width]),
-        mixer_weight_grad,
-        term(steps),
-    )
+    small = rows + PAD
+    band = cols // chans
+    input_grad, inner_grad, mixer_grad, step_grad = pl.pallas_call(
+        functools.partial(back_kernel, sizes, heads),
+        out_shape=(
+            jax.ShapeDtypeStruct((rows, model), BF),
+            jax.ShapeDtypeStruct((cols, width), F32),
+            jax.ShapeDtypeStruct((band, mixed), F32),
+            jax.ShapeDtypeStruct((cols, heads), F32),
+        ),
+        in_specs=[vmem] * 5 + [hbm] * 3 + [vmem],
+        out_specs=(vmem,) * 4,
+        scratch_shapes=[
+            pltpu.VMEM((model, width), BF),
+            pltpu.VMEM((model, mixed), BF),
+            pltpu.VMEM((model, LANES), BF),
+            pltpu.VMEM((length + 8, width), F32),
+            pltpu.VMEM((length + 8, mixed), F32),
+            pltpu.VMEM((seqs, dps, length, width), BF),
+            pltpu.VMEM((seqs, dps, small, mixed), BF),
+            pltpu.VMEM((8, width + mixed), F32),
+            pltpu.VMEM((8, width + mixed), F32),
+            pltpu.VMEM((length, mixed), BF),
+            pltpu.VMEM((chans, rows, mixed), BF),
+            pltpu.VMEM((chans, rows, model), BF),
+            pltpu.VMEM((chans, rows, model), BF),
+            pltpu.VMEM((chans, band, mixed), BF),
+            pltpu.VMEM((chans, band, mixed), BF),
+            dma((3,)), dma((2,)),
+            dma((chans, seqs)), dma((chans, dps, seqs)),
+            dma((chans, seqs)), dma((chans, seqs)), dma((chans, dps, seqs)),
+            dma((dps,)), dma((dps, seqs)), dma((dps,)), dma((dps, seqs)), dma((dps, seqs)),
+            dma((chans,)), dma((chans,)),
+            dma((chans, chans)), dma((chans, chans)),
+            dma((chans,)), dma((chans,)),
+        ],
+        compiler_params=pltpu.CompilerParams(
+            collective_id=2, has_side_effects=True, vmem_limit_bytes=LIMIT
+        ),
+        name="back",
+    )(a_in, a_mix, steps, conv_inner, conv_mixer, inner_weight, mixer_weight, step_wide, xc)
+    return input_grad[None], inner_grad, mixer_grad, step_grad
 
 
 def solution(mesh):

time: 126 us -> 99.1 us (0.79)
  Pallas kernels: 94.5 us -> 81.4 us
  matrix products: 14.4 us -> 4.59 us
  other arithmetic: 7.56 us -> 0.72 us
  local copies, waits for them, and re-layouts: 7.62 us -> 11.2 us
    pallas_call x4 -> x1, Pallas kernels: 85.9 us -> 16.8 us  [exchange(): pl.pallas_call(functools.partial(exchange_kernel, tuple(plan), tail, plug...]
    pallas_call x0 -> x2, Pallas kernels: none -> 56.4 us  [the longest x1 29.3 us: body(): pl.pallas_call(functools.partial(back_kernel, sizes, heads), out_shape=(j...]
    dot_general x6 -> x0, matrix products: 8.42 us -> none  [the longest x3 4.85 us: rows_dot(): lax.dot_general(gradient, weight, (((1,), (1,)), ((), ())), preferred_ele...]
    unnamed x14 -> x13, local copies, waits for them, and re-layouts: 0.91 us -> 7.25 us
    reduce_sum x3 -> x0, other arithmetic: 4.6 us -> none  [the longest x1 1.93 us: body(): total = jnp.sum(parts.astype(F32), axis=0)]
    concatenate x3 -> x0, other arithmetic: 1.94 us -> none  [the longest x2 1.69 us: body(): jnp.concatenate([total[:rows - PAD], total[rows - PAD:] + tail_sum], axis=0)]
    slice x3 -> x0, local copies, waits for them, and re-layouts: 1.74 us -> none  [the longest x1 0.96 us: body(): main, early = (split[:, :, PAD:], jnp.where(live, split[:, :, :PAD], 0))]
    dot_general x1, matrix products: 2.58 us -> 1 us  [body(): jnp.dot(tokens, mixer_weight, preferred_element_type=F32).astype(BF)]
where the time goes in v1:
time: 99.1 us; the launch traced here: 98.7 us
  Pallas kernels  81.4 us (82%)
  local copies, waits for them, and re-layouts  11.2 us (11%)
  matrix products  4.59 us (5%)
    pallas_call x1, Pallas kernels, body(): pl.pallas_call(functools.partial(back_kernel, sizes, heads), out_shape=(j...  29.3 us
    pallas_call x1, Pallas kernels, body(): pl.pallas_call(functools.partial(mid_kernel, sizes), out_shape=(jax.Shape...  27 us
    pallas_call x1, Pallas kernels, exchange(): pl.pallas_call(functools.partial(exchange_kernel, tuple(plan), tail, plug...  16.8 us
    pallas_call x2, Pallas kernels, local_call(): pl.pallas_call(kernel, out_shape=out_shapes, in_specs=[vmem] * len(arrays...  8.31 us
    unnamed x13, local copies, waits for them, and re-layouts  7.25 us
    dot_general x1, matrix products, body(): step_raw = jnp.dot(tokens[PAD:], step_wide, preferred_element_type=F32)  2.18 us

profile of v1, /device:TPU:0, one launch (start us, length us, event | category | flops | bytes accessed | tf_op | source)
XLA Modules:
  0.0 98.7 jit_solution(17007909304436289178)
XLA Ops:
  0.6 0.7 select_maximum_fusion
  1.3 0.6 slice_bitcast_fusion
  1.9 0.6 broadcast_in_dim.15.skip_ref
  2.5 1.1 %reshape_squeeze.3 = bf16[32,2,4,320]{3,2,1,0:T(4,128)(2,1)S(1)} reshape(bf16[1,32,2560]{2,1,0:T(8,128)(2,1)} %param.10) | data formatting | bytes 327680 | tf_op jit(solution)/shard_map/reshape;squeeze | solution.py:830
  3.6 0.7 copy.20
  4.4 1.2 %copy.17 = bf16[2560,10]{1,0:T(8,128)(2,1)S(1)} copy(bf16[2560,10]{0,1:T(8,128)(2,1)} %param.13) | data formatting | bytes 102400 | tf_op args[3]
  5.6 1.0 pad.8.w_step_h
  6.6 16.8 %exchange_0.1 = (bf16[4,32,2560]{2,1,0:T(8,128)(2,1)}, bf16[2,4,32,320]{3,2,1,0:T(8,128)(2,1)}, bf16[16,2560]{1,0:T(8,128)(2,1)}) custom-call(bf16[32,2560]{1,0:T(8,128)(2,1)} %bitcast.21, bf16[2,4,32,320]{3,2,1,0:T(8,128)(2,1)} %bitcast.15), custom_call_target="tpu_custom_call" | custom-call | tf_op jit(solution)/shard_map/exchange_0/pallas_call | solution.py:300
  23.3 0.0 copy-start.2
  23.4 0.0 copy-start
  23.4 2.2 %fusion.2.raw_ref = f32[128,128]{1,0:T(8,128)} fusion(bf16[128,2560]{1,0:T(8,128)(2,1)} %bitcast.18, bf16[2560,10]{1,0:T(8,128)(2,1)S(1)} %copy.17), kind=kOutput, calls=%fused_computation.12 | convolution fusion | flops 83886080 | bytes 772096 | tf_op jit(solution)/shard_map/dot_general | solution.py:840
  25.6 0.0 copy-done.1
  25.6 0.0 copy-done.2
  25.6 1.0 %convolution_convert_fusion.1.mixer_ref = bf16[144,256]{1,0:T(8,128)(2,1)} fusion(bf16[2560,256]{1,0:T(8,128)(2,1)S(1)} %copy-done.1, bf16[128,2560]{1,0:T(8,128)(2,1)S(1)} %bitcast.19, bf16[16,2560]{1,0:T(8,128)(2,1)S(1)} %broadcast_select_fusion), kind=kOutput, calls=%fused_computation.1 | convolution fusion | flops 190255104 | bytes 2121728 | tf_op jit(solution)/shard_map/dot_general | solution.py:839
  26.6 0.0 copy-done
  26.6 1.4 %convolution_convert_fusion.inner_ref = bf16[144,640]{1,0:T(8,128)(2,1)} fusion(bf16[2560,640]{1,0:T(8,128)(2,1)S(1)} %copy-done, bf16[128,2560]{1,0:T(8,128)(2,1)S(1)} %bitcast.20, bf16[16,2560]{1,0:T(8,128)(2,1)S(1)} %broadcast_select_fusion), kind=kOutput, calls=%fused_computation | convolution fusion | flops 473425920 | bytes 4198400 | tf_op jit(solution)/shard_map/dot_general | solution.py:838
  28.0 3.1 %forward.1 = (f32[128,640]{1,0:T(8,128)}, f32[128,256]{1,0:T(8,128)}, bf16[640,128]{1,0:T(8,128)(2,1)}, bf16[640,128]{1,0:T(8,128)(2,1)}, f32[640,128]{1,0:T(8,128)}) custom-call(bf16[144,640]{1,0:T(8,128)(2,1)} %convolution_convert_fusion.inner_ref, bf16[144,256]{1,0:T(8,128)(2,1)} %convolution_convert_fusion.1.mixer_ref, f32[128,128]{1,0:T(8,128)} %fusion.2.raw_ref, ...), custom_call_target="tpu_custom_call" | custom-call | tf_op jit(solution)/shard_map/forward/pallas_call | solution.py:798
  31.1 27.0 %middle.1 = (bf16[4,2,4,32,320]{4,3,2,1,0:T(8,128)(2,1)}, bf16[640,128]{1,0:T(8,128)(2,1)}, bf16[640,128]{1,0:T(8,128)(2,1)}) custom-call(bf16[2,4,32,320]{3,2,1,0:T(8,128)(2,1)} %get-tuple-element.26.cols, bf16[640,128]{1,0:T(8,128)(2,1)} %get-tuple-element.27.state, bf16[640,128]{1,0:T(8,128)(2,1)} %get-tuple-element.28.back, ...), custom_call_target="tpu_custom_call" | custom-call | tf_op jit(solution)/shard_map/middle/pallas_call | solution.py:862
  58.1 5.2 %backward.1 = (f32[128,640]{1,0:T(8,128)}, f32[128,256]{1,0:T(8,128)}, f32[128,128]{1,0:T(8,128)}) custom-call(f32[128,640]{1,0:T(8,128)} %get-tuple-element.24.inner_ref, f32[128,256]{1,0:T(8,128)} %get-tuple-element.25.mixer_ref, f32[128,128]{1,0:T(8,128)} %fusion.2.raw_ref, f32[1,128]{1,0:T(1,128)} %get-tuple-element.50.bias_ref, ...), custom_call_target="tpu_custom_call" | custom-call | tf_op jit(solution)/shard_map/backward/pallas_call | solution.py:798
  63.3 29.3 %back.1 = (bf16[32,2560]{1,0:T(8,128)(2,1)}, f32[320,640]{1,0:T(8,128)}, f32[80,256]{1,0:T(8,128)}, f32[320,10]{1,0:T(8,128)}) custom-call(f32[128,640]{1,0:T(8,128)} %get-tuple-element.32.a_in, f32[128,256]{1,0:T(8,128)} %get-tuple-element.33.a_mix, f32[128,128]{1,0:T(8,128)} %get-tuple-element.34.st, f32[4,640]{1,0:T(4,128)} %conv_in.1, ...), custom_call_target="tpu_custom_call" | custom-call | tf_op jit(solution)/shard_map/back/pallas_call | solution.py:897
  92.7 1.7 %copy.18 = f32[320,10]{0,1:T(8,128)} copy(f32[320,10]{1,0:T(8,128)} %get-tuple-element.47) | data formatting | bytes 25600
  94.4 1.6 %copy.24 = bf16[1,32,2560]{2,1,0:T(8,128)(2,1)} copy(bf16[1,32,2560]{2,1,0:T(8,128)(2,1)} %bitcast.22) | data formatting | bytes 327680
  95.9 2.1 %copy.25 = f32[320,640]{1,0:T(8,128)} copy(f32[320,640]{1,0:T(8,128)} %get-tuple-element.56) | data formatting | bytes 1638400
  98.0 0.6 copy.26
  (4 shorter events, 0.0 us)
Async XLA Ops:
  5.6 20.0 %copy-start.1 = (bf16[2560,256]{1,0:T(8,128)(2,1)S(1)}, bf16[2560,256]{1,0:T(8,128)(2,1)}, u32[]{:S(2)}) copy-start(bf16[2560,256]{1,0:T(8,128)(2,1)} %w_mix_h.1) | copy-start | bytes 3932164
  23.3 2.2 %copy-start.2 = (bf16[4,32,2560]{2,1,0:T(8,128)(2,1)S(1)}, bf16[4,32,2560]{2,1,0:T(8,128)(2,1)}, u32[]{:S(2)}) copy-start(bf16[4,32,2560]{2,1,0:T(8,128)(2,1)} %get-tuple-element.23) | copy-start | bytes 1966084
  23.4 3.2 %copy-start = (bf16[2560,640]{1,0:T(8,128)(2,1)S(1)}, bf16[2560,640]{1,0:T(8,128)(2,1)}, u32[]{:S(2)}) copy-start(bf16[2560,640]{1,0:T(8,128)(2,1)} %w_in_h.1) | copy-start | bytes 9830404
  92.7 5.4 %copy-start.3 = (f32[80,256]{1,0:T(8,128)S(1)}, f32[80,256]{1,0:T(8,128)}, u32[]{:S(2)}) copy-start(f32[80,256]{1,0:T(8,128)} %get-tuple-element.57) | copy-start | bytes 245764

commit v2 on v1

v2 whole, which is shorter than its diff:
```python
import functools
import math

import jax
import jax.numpy as jnp
from jax import lax
from jax.experimental import pallas as pl
from jax.experimental.pallas import tpu as pltpu
from jax.sharding import PartitionSpec as P

MESH = pl.DeviceIdType.MESH
HDIM = 64
PAD = 16
LANES = 128
LIMIT = 40 * 2**20
BF = jnp.bfloat16
F32 = jnp.float32
HIGH = lax.Precision.HIGHEST


def each(n, step):
    if n <= 12:
        for d in range(1, n):
            step(d)
    else:

        def one(d, carry):
            step(d)
            return carry

        lax.fori_loop(1, n, one, 0)


def signal_to(barrier, where):
    pl.semaphore_signal(barrier, inc=1, device_id=where, device_id_type=MESH)


def greet_line(barrier, n):
    me = lax.axis_index("seq")
    signal_to(barrier, {"seq": lax.rem(me + 1, n)})
    signal_to(barrier, {"seq": lax.rem(me + n - 1, n)})
    return 2


class Chain:
    pieces = 5

    def copy(self, way, piece):
        me = lax.axis_index("seq")
        rows = self.outs[0].shape[0] // self.pieces
        part = pl.ds(pl.multiple_of(piece * rows, rows), rows)
        target = lax.rem(me + 1, self.n) if way == 0 else lax.rem(me + self.n - 1, self.n)
        return pltpu.make_async_remote_copy(
            src_ref=self.scratch[way].at[part],
            dst_ref=self.outs[way].at[part],
            send_sem=self.scratch[2 + way].at[piece],
            recv_sem=self.scratch[4 + way].at[piece],
            device_id={"seq": target},
            device_id_type=MESH,
        )

    def start(self):
        me = lax.axis_index("seq")
        for way, edge in ((0, 0), (1, self.n - 1)):

            @pl.when(me == edge)
            def _(way=way):
                self.outs[way][...] = jnp.zeros(self.outs[way].shape, BF)

    def beat(self, t):
        me = lax.axis_index("seq")
        rows = self.outs[0].shape[0] // self.pieces
        for way in (0, 1):
            place = me if way == 0 else self.n - 1 - me
            piece = t - place
            active = (piece >= 0) & (piece < self.pieces)

            @pl.when(active & (place > 0))
            def _(way=way, piece=piece):
                self.copy(way, piece).wait_recv()

            @pl.when(active & (place < self.n - 1))
            def _(way=way, piece=piece):
                part = pl.ds(pl.multiple_of(piece * rows, rows), rows)
                before = self.outs[way][part, :].astype(F32)
                term = self.ins[way][part, :].astype(F32)
                self.scratch[way][part, :] = (self.ins[2][part, :] * before + term).astype(BF)
                self.copy(way, piece).start()

    def run(self):
        me = lax.axis_index("seq")
        half = self.pieces
        for t in range(1, half):
            self.beat(t)
        rest = self.n - 1
        if rest <= 12:
            for t in range(half, half + rest):
                self.beat(t)
        else:
            lax.fori_loop(half, half + rest, lambda t, c: (self.beat(t), c)[1], 0)

        for way in (0, 1):

            @pl.when(me != (self.n - 1 if way == 0 else 0))
            def _(way=way):
                for piece in range(self.pieces):
                    self.copy(way, piece).wait_send()


def mm(a, b, da, db):
    return lax.dot_general(
        a.astype(BF), b.astype(BF), (((da,), (db,)), ((), ())), preferred_element_type=F32
    )


def exact(a, b, da=1, db=0):
    return lax.dot_general(
        a, b, (((da,), (db,)), ((), ())), precision=HIGH, preferred_element_type=F32
    )


def softplus(v):
    return jnp.maximum(v, 0.0) + jnp.log1p(jnp.exp(-jnp.abs(v)))


def head_mask(width, heads_first):
    shape = (LANES, width) if heads_first else (width, LANES)
    head = lax.broadcasted_iota(jnp.int32, shape, 0 if heads_first else 1)
    column = lax.broadcasted_iota(jnp.int32, shape, 1 if heads_first else 0)
    return (column // HDIM == head).astype(F32)


def decays(raw, bias, decay_log):
    length = raw.shape[0]
    step = softplus(raw + bias)
    rate = jnp.exp(decay_log)
    row = lax.broadcasted_iota(jnp.int32, (length, length), 0)
    col = lax.broadcasted_iota(jnp.int32, (length, length), 1)
    lower = (row >= col).astype(F32)
    cumulative = exact(lower, -step * rate)
    return step, rate, cumulative, row, col, lower


def front_kernel(
    sizes, heads,
    own, w_in_h, w_mix_h, w_step, conv_in, conv_mix, bias, log, grad,
    sum_in, sum_mix, raw_ref, state_ref, back_ref, decay_ref, xs,
    w_in, w_mix, wst, xg, blocks, mid, wide_in, wide_mix, hal_o, hal_i, vec,
    w_sem, near_s, near_r, far_s, far_r, relay_s, relay_r, swap_s, swap_r, cross_s, cross_r, hal_sem,
):
    D, S, C = sizes["dp"], sizes["seq"], sizes["chan"]
    mine, me, ch = lax.axis_index("dp"), lax.axis_index("seq"), lax.axis_index("chan")
    rows, model = own.shape
    length, width = sum_in.shape
    mixed = sum_mix.shape[1]
    taps = conv_in.shape[0]
    cols = model // (D * S)
    half = mixed // 2
    barrier = pltpu.get_barrier_semaphore()
    total = greet_all(barrier, "dp", D) + greet_all(barrier, "seq", S) + greet_all(barrier, "chan", C)
    weights = [
        pltpu.make_async_copy(h, v, w_sem.at[i])
        for i, (h, v) in enumerate(((w_in_h, w_in), (w_mix_h, w_mix)))
    ]
    for copy in weights:
        copy.start()
    for d in range(D):
        for k in range(S):
            at = (d * S + k) * cols
            blocks[d, k] = own[:, at : at + cols]
    pieces = C
    cut = model // pieces
    sides = C // 2
    side, low = lax.div(ch, 2), lax.rem(ch, 2)
    partner = ch + 1 - 2 * low

    def block(c, p):
        return xg.at[pl.ds(pl.multiple_of(c * rows, rows), rows), pl.ds(p * cut, cut)]

    def mine_at(p):
        return own.at[:, pl.ds(p * cut, cut)]

    def near(c, p):
        return rcopy(mine_at(p), block(c, p), near_s.at[p], near_r.at[p], chan=partner)

    def far(to, c, slot, p):
        return rcopy(
            mine_at(p), block(c, p), far_s.at[to, p], far_r.at[slot, p], chan=2 * to + low
        )

    def relay(source, lane, p):
        c = 2 * source + lane
        return rcopy(block(c, p), block(c, p), relay_s.at[source, p], relay_r.at[source, p], chan=partner)

    def swap(q, landing, slot):
        return rcopy(blocks.at[q], mid.at[landing], swap_s.at[q], swap_r.at[slot], dp=q)

    def cross(q, landing, slot):
        return rcopy(mid.at[:, q], xs.at[landing], cross_s.at[q], cross_r.at[slot], seq=q)

    pl.semaphore_wait(barrier, total)
    for p in range(pieces):
        for d in range(1, sides):
            far(lax.rem(side + d, sides), ch, side, p).start()
        near(ch, p).start()
    each(D, lambda d: swap(lax.rem(mine + d, D), mine, mine).start())
    mid[mine] = blocks[mine]
    xg[pl.ds(pl.multiple_of(ch * rows, rows), rows), :] = own[...]
    wst[...] = jnp.zeros(wst.shape, BF)
    wst[0:heads, :] = w_step[...]
    vec[...] = jnp.zeros(vec.shape, F32)
    vec[0:1, 0:heads] = bias[...]
    vec[1:2, 0:heads] = log[...]

    def pass_on(p):
        for d in range(1, sides):
            source = lax.rem(side + d, sides)
            far(source, ch, source, p).wait_recv()
            relay(source, low, p).start()

    def project(p):
        near(partner, p).wait_recv()
        for d in range(1, sides):
            source = lax.rem(side + d, sides)
            relay(source, 1 - low, p).wait_recv()
        piece = slice(p * cut, (p + 1) * cut)
        x = xg[:, piece]
        inner = mm(x, w_in[piece, :], 1, 0)
        mixer = mm(x, w_mix[piece, :], 1, 0)
        raw = mm(x, wst[:, piece], 1, 1)
        if p == 0:
            wide_in[PAD:, :], wide_mix[PAD:, :], raw_ref[...] = inner, mixer, raw
        else:
            wide_in[PAD:, :] = wide_in[PAD:, :] + inner
            wide_mix[PAD:, :] = wide_mix[PAD:, :] + mixer
            raw_ref[...] = raw_ref[...] + raw

    pass_on(0)
    for copy in weights:
        copy.wait()
    for p in range(pieces):
        if p + 1 < pieces:
            pass_on(p + 1)
        project(p)
        if p == pieces // 2:
            each(D, lambda d: swap(lax.rem(mine + d, D), mine, lax.rem(mine + d, D)).wait_recv())
            each(S, lambda d: cross(lax.rem(me + d, S), me, me).start())
            xs[me] = mid[:, me]
    inner_low = wide_in[PAD:, :].astype(BF)
    mixer_low = wide_mix[PAD:, :].astype(BF)
    hal_o[:, :width] = inner_low[length - PAD :, :]
    hal_o[:, width:] = mixer_low[length - PAD :, :]

    def halo():
        return rcopy(hal_o, hal_i, hal_sem.at[0], hal_sem.at[1], seq=lax.rem(me + 1, S))

    @pl.when(me < S - 1)
    def _():
        halo().start()

    wide_in[PAD:, :] = inner_low.astype(F32)
    wide_mix[PAD:, :] = mixer_low.astype(F32)
    wide_in[0:PAD, :] = jnp.zeros((PAD, width), F32)
    wide_mix[0:PAD, :] = jnp.zeros((PAD, mixed), F32)

    def convolved(wide, kernel, first, count):
        first = first + PAD - (taps - 1)
        total = kernel[0:1, :] * wide[pl.ds(first, count), :]
        for k in range(1, taps):
            total = total + kernel[k : k + 1, :] * wide[pl.ds(first + k, count), :]
        return total

    sum_in[PAD:, :] = convolved(wide_in, conv_in, PAD, length - PAD)
    sum_mix[PAD:, :] = convolved(wide_mix, conv_mix, PAD, length - PAD)
    step, rate, cumulative, row, col, lower = decays(raw_ref[...], vec[0:1, :], vec[1:2, :])
    last = cumulative[length - 1 : length, :]
    spread = head_mask(width, True)
    tail = exact(jnp.exp(last - cumulative) * step, spread)
    grown = exact(jnp.exp(cumulative), spread)
    pulled = grown * grad[...].astype(F32)
    row_decay = jnp.sum(head_mask(width, False) * jnp.exp(last), axis=1, keepdims=True)
    decay_ref[...] = jnp.broadcast_to(row_decay, decay_ref.shape)

    @pl.when(me > 0)
    def _():
        halo().wait_recv()
        wide_in[0:PAD, :] = hal_i[:, :width].astype(F32)
        wide_mix[0:PAD, :] = hal_i[:, width:].astype(F32)

    sum_in[0:PAD, :] = convolved(wide_in, conv_in, 0, PAD)
    sum_mix[0:PAD, :] = convolved(wide_mix, conv_mix, 0, PAD)
    mixer = sum_mix[...]
    mix = mixer * jax.nn.sigmoid(mixer)
    back_ref[...] = mm(pulled, mix[:, half:], 0, 0).astype(BF)
    inner = sum_in[...]
    act = inner * jax.nn.sigmoid(inner)
    state_ref[...] = mm(act * tail, mix[:, :half], 0, 0).astype(BF)

    @pl.when(me < S - 1)
    def _():
        halo().wait_send()

    for p in range(pieces):
        near(ch, p).wait_send()
        for d in range(1, sides):
            source = lax.rem(side + d, sides)
            far(source, ch, source, p).wait_send()
            relay(source, low, p).wait_send()
    each(D, lambda d: swap(lax.rem(mine + d, D), mine, mine).wait_send())

    def settle(d):
        q = lax.rem(me + d, S)
        cross(q, me, q).wait()

    each(S, settle)


def backward_kernel(
    heads, inner_ref, mixer_ref, raw_ref, bias_ref, log_ref, skip_ref, grad_ref, start_ref, end_ref,
    a_in_ref, a_mix_ref, step_ref, z_ref, y_ref, vec,
):
    length = raw_ref.shape[0]
    width = inner_ref.shape[1]
    spread = head_mask(width, True)
    spread_down = head_mask(width, False)
    vec[...] = jnp.zeros(vec.shape, F32)
    for i, ref in enumerate((bias_ref, log_ref, skip_ref)):
        vec[i : i + 1, 0:heads] = ref[...]
    bias, skips = vec[0:1, :], vec[2:3, :]
    start, end = start_ref[...].astype(F32), end_ref[...].astype(F32)
    inner, mixer = inner_ref[...], mixer_ref[...]
    inner_gate, mixer_gate = jax.nn.sigmoid(inner), jax.nn.sigmoid(mixer)
    act, mix = inner * inner_gate, mixer * mixer_gate
    half = mix.shape[1] // 2
    into, out_of = mix[:, :half], mix[:, half:]
    raw = raw_ref[...]
    step, rate, cumulative, row, col, lower = decays(raw, bias, vec[1:2, :])
    last = cumulative[length - 1 : length, :]
    step_wide = exact(step, spread)
    grown = exact(jnp.exp(cumulative), spread)
    fading = exact(jnp.exp(last - cumulative), spread)
    upstream_low = grad_ref[...]
    upstream = upstream_low.astype(F32)
    stepped_low = (act * step_wide).astype(BF)
    stepped = stepped_low.astype(F32)
    scores = mm(out_of, into, 1, 1)
    causal = row >= col
    across = cumulative.T
    score_grad = jnp.zeros((length, length), F32)
    for h in range(heads):
        cols = slice(h * HDIM, (h + 1) * HDIM)
        gap = cumulative[:, h : h + 1] - across[h : h + 1, :]
        decay = jnp.where(causal, jnp.exp(jnp.where(causal, gap, 0.0)), 0.0)
        weights = (decay * scores).astype(BF)
        grad_h, step_h = upstream_low[:, cols], stepped_low[:, cols]
        score_grad = score_grad + decay * mm(grad_h, step_h, 1, 1)
        z_ref[:, cols] = mm(weights, grad_h, 0, 0)
        y_ref[:, cols] = mm(weights, step_h, 1, 0)
    z = z_ref[...]
    carried = grown * mm(out_of, start, 1, 1)
    ending = fading * mm(into, end, 1, 1)
    act_grad = step_wide * (z + ending) + exact(jnp.broadcast_to(skips, (8, LANES)), spread)[0:1, :] * upstream
    to_heads = functools.partial(exact, b=spread, da=1, db=1)
    step_grad = to_heads(act * (z + ending))
    tail_term = to_heads(stepped * ending)
    sum_grad = to_heads(upstream * (y_ref[...] + carried) - stepped * z) - tail_term
    held = jnp.sum(start * end, axis=1, keepdims=True)
    overall = jnp.sum(tail_term, axis=0, keepdims=True) + jnp.exp(last) * jnp.sum(
        spread_down * held, axis=0, keepdims=True
    )
    decay_grad = exact(lower, sum_grad, 0, 0) + overall
    step_grad = (step_grad - rate * decay_grad) * jax.nn.sigmoid(raw + bias)
    out_grad = mm(score_grad, into, 1, 0) + mm(grown * upstream, start, 1, 0)
    into_grad = mm(score_grad, out_of, 0, 0) + mm(fading * stepped, end, 1, 0)
    inner_slope = inner_gate * (1.0 + inner * (1.0 - inner_gate))
    mixer_slope = mixer_gate * (1.0 + mixer * (1.0 - mixer_gate))
    a_in_ref[...] = act_grad * inner_slope
    a_mix_ref[:, :half] = into_grad * mixer_slope[:, :half]
    a_mix_ref[:, half:] = out_grad * mixer_slope[:, half:]
    step_ref[...] = step_grad


def rcopy(src, dst, send, recv, **where):
    return pltpu.make_async_remote_copy(
        src_ref=src, dst_ref=dst, send_sem=send, recv_sem=recv, device_id=where, device_id_type=MESH
    )


def greet_all(barrier, axis, n):
    me = lax.axis_index(axis)
    each(n, lambda d: signal_to(barrier, {axis: lax.rem(me + d, n)}))
    return n - 1


def mid_kernel(
    sizes, xs, state, back, decay, xc, start, end, scr0, scr1, gat_s, gat_r, *chain_sems
):
    n, chans = sizes["seq"], sizes["chan"]
    ch = lax.axis_index("chan")
    barrier = pltpu.get_barrier_semaphore()
    total = greet_line(barrier, n) + greet_all(barrier, "chan", chans)
    chain = Chain()
    chain.n, chain.ins, chain.outs = n, (state, back, decay), (start, end)
    chain.scratch = (scr0, scr1) + chain_sems
    pl.semaphore_wait(barrier, total)
    chain.start()

    def gather(q, landing, slot):
        return rcopy(xs, xc.at[:, :, landing], gat_s.at[q], gat_r.at[slot], chan=q)

    chain.beat(0)
    each(chans, lambda d: gather(lax.rem(ch + d, chans), ch, ch).start())
    xc[:, :, ch] = xs[...]
    chain.run()

    def settle_gather(d):
        q = lax.rem(ch + d, chans)
        gather(q, q, q).wait()

    each(chans, settle_gather)


def back_kernel(
    sizes, heads,
    a_in, a_mix, st, conv_in, conv_mix, w_in_h, w_mix_h, w_step, xc,
    p_i, o_dw, m_i, o_dws,
    w_in, w_mix, wst, pad_in, pad_mix, gin, gsm, hal_o, hal_i, gmp, gm_in, p_o, m_o,
    w_sem, hal_sem, z_r, c_r, u_s, d_s, x_s, c2_r, z2_r, x2_s, u2_s, d2_s,
    gm_s, gm_r, p_s, p_r, m_s, m_r,
):
    D, S, C = sizes["dp"], sizes["seq"], sizes["chan"]
    mine, me, ch = lax.axis_index("dp"), lax.axis_index("seq"), lax.axis_index("chan")
    length, width = a_in.shape
    mixed = a_mix.shape[1]
    taps = conv_in.shape[0]
    model = w_in.shape[0]
    rows = length // C
    parts = C
    barrier = pltpu.get_barrier_semaphore()
    total = greet_all(barrier, "dp", D) + greet_all(barrier, "chan", C) + greet_line(barrier, S)
    weights = [
        pltpu.make_async_copy(h, v, w_sem.at[i])
        for i, (h, v) in enumerate(((w_in_h, w_in), (w_mix_h, w_mix)))
    ]
    for copy in weights:
        copy.start()
    wst[...] = jnp.zeros(wst.shape, BF)
    wst[0:heads, :] = w_step[...]
    hal_o[:, :width] = a_in[0:8, :]
    hal_o[:, width:] = a_mix[0:8, :]
    pad_in[0:length, :] = a_in[...]
    pad_mix[0:length, :] = a_mix[...]
    pad_in[length:, :] = jnp.zeros((8, width), F32)
    pad_mix[length:, :] = jnp.zeros((8, mixed), F32)

    def spread_back(pad, kernel, first, count):
        total = None
        for k in range(taps):
            term = kernel[k : k + 1, :] * pad[pl.ds(first + taps - 1 - k, count), :]
            total = term if total is None else total + term
        return total.astype(BF)

    last = length - rows
    gin[me, mine, 0:last, :] = spread_back(pad_in, conv_in, 0, last)
    gmp[0:last, :] = spread_back(pad_mix, conv_mix, 0, last)
    gsm[me, mine, rows:, 0:LANES] = st[...].T[0:PAD, :].astype(BF)
    pl.semaphore_wait(barrier, total)

    def others():
        return [lax.rem(mine + e, D) for e in range(1, D)]

    def halo():
        return rcopy(hal_o, hal_i, hal_sem.at[0], hal_sem.at[1], seq=lax.rem(me + S - 1, S))

    @pl.when(me > 0)
    def _():
        halo().start()

    def part(p, e, k):
        return gin.at[k, e, pl.ds(p * rows, rows)]

    def zcopy(p, way, k):
        to = lax.rem(me + (1 if way == "up" else S - 1), S)
        send = (u_s if way == "up" else d_s).at[p, k]
        return rcopy(part(p, mine, k), part(p, mine, k), send, z_r.at[p, k], seq=to)

    def ccopy(p, k, e, to):
        return rcopy(part(p, e, k), part(p, e, k), x_s.at[p, to, k], c_r.at[p, e, k], dp=to)

    def zsmall(way, e, k):
        to = lax.rem(me + (1 if way == "up" else S - 1), S)
        send = (u2_s if way == "up" else d2_s).at[e, k]
        return rcopy(gsm.at[k, e], gsm.at[k, e], send, z2_r.at[e, k], seq=to)

    def csmall(e, to):
        return rcopy(gsm.at[me, e], gsm.at[me, e], x2_s.at[to], c2_r.at[e], dp=to)

    def onward(make, k):
        @pl.when(me < S - 1)
        def _():
            make("up", k).start()

        @pl.when(me > 0)
        def _():
            make("down", k).start()

    def own_part(p):
        onward(functools.partial(zcopy, p), me)
        for e in others():
            ccopy(p, me, mine, e).start()

    def forward(d, p):
        for way, k, there, more in (
            ("up", me - d, me >= d, me < S - 1),
            ("down", me + d, me + d < S, me > 0),
        ):

            @pl.when(there)
            def _(way=way, k=k):
                zcopy(p, way, k).wait_recv()

            @pl.when(there & more)
            def _(way=way, k=k):
                zcopy(p, way, k).start()

            @pl.when(there)
            def _(k=k):
                for e in others():
                    ccopy(p, k, mine, e).start()

    def own_small():
        for e in others():
            csmall(mine, e).start()
        onward(lambda way, k: zsmall(way, mine, k), me)

    def cross_small():
        for e in others():
            csmall(e, e).wait_recv()
            onward(lambda way, k, e=e: zsmall(way, e, k), me)

    def forward_small(d):
        for way, k, there, more in (
            ("up", me - d, me >= d, me < S - 1),
            ("down", me + d, me + d < S, me > 0),
        ):
            for e in [mine] + others():

                @pl.when(there)
                def _(way=way, k=k, e=e):
                    zsmall(way, e, k).wait_recv()

                @pl.when(there & more)
                def _(way=way, k=k, e=e):
                    zsmall(way, e, k).start()

    norm = 1.0 / math.sqrt(D * S * length)

    def columns_of(k):
        block = xc[k]
        return block.reshape(D * length, block.shape[-1])

    def weight_term(k, first=False):
        for e in others():
            for p in range(parts):
                ccopy(p, k, e, e).wait_recv()
        x = columns_of(k)
        term = norm * mm(x, gin[k].reshape(D * length, width), 0, 0)
        o_dw[...] = term if first else o_dw[...] + term

    def weight_terms(d):
        for k, there in ((me - d, me >= d), (me + d, me + d < S)):

            @pl.when(there)
            def _(k=k):
                weight_term(k)

    for p in range(parts - 1):
        own_part(p)

    @pl.when(me < S - 1)
    def _():
        halo().wait_recv()
        pad_in[length:, :] = hal_i[:, :width]
        pad_mix[length:, :] = hal_i[:, width:]

    gin[me, mine, last:, :] = spread_back(pad_in, conv_in, last, rows)
    gmp[last:, :] = spread_back(pad_mix, conv_mix, last, rows)
    own_part(parts - 1)

    def share_mix(q, landing, slot):
        return rcopy(gmp.at[pl.ds(q * rows, rows)], gm_in.at[landing], gm_s.at[q], gm_r.at[slot], chan=q)

    each(C, lambda d: share_mix(lax.rem(ch + d, C), ch, ch).start())
    for copy in weights:
        copy.wait()
    cut = model // parts

    def share_p(j, q, landing, slot):
        piece = pl.ds(j * cut, cut)
        return rcopy(
            p_o.at[q, :, piece], p_i.at[landing, :, piece], p_s.at[j, q], p_r.at[j, slot], chan=q
        )

    grads = gin[me, mine]
    mixes = gmp[...]
    steps = st[:, 0:PAD].astype(BF)

    def back_project(j):
        piece = slice(j * cut, (j + 1) * cut)
        out = mm(grads, w_in[piece, :], 1, 1) + mm(mixes, w_mix[piece, :], 1, 1)
        out = out + mm(steps, wst[:, piece], 1, 0)
        p_o[:, :, piece] = out.astype(BF).reshape(C, rows, cut)
        each(C, lambda d: share_p(j, lax.rem(ch + d, C), ch, ch).start())

    def finish_mix():
        gm_in[ch] = gmp[pl.ds(pl.multiple_of(ch * rows, rows), rows), :]
        each(C, lambda d: share_mix(lax.rem(ch + d, C), ch, lax.rem(ch + d, C)).wait_recv())
        mix = gm_in[0].astype(F32)
        for q in range(1, C):
            mix = mix + gm_in[q].astype(F32)
        gsm[me, mine, 0:rows, :] = mix.astype(BF)
        own_small()

    for j in range(parts):
        back_project(j)
        forward(1, j)
        if j == 0:
            finish_mix()
    weight_term(me, True)

    def hop(d):
        for p in range(parts):
            forward(d, p)
        if isinstance(d, int) and d == 2:
            cross_small()
        forward_small(d - 1)
        weight_terms(d - 1)

    hop(2)
    if S > 3:
        if S <= 12:
            for d in range(3, S):
                hop(d)
        else:
            lax.fori_loop(3, S, lambda d, c: (hop(d), c)[1], 0)
    forward_small(S - 1)

    mixer_columns = xc[:, :, ch].reshape(S * D * rows, xc.shape[-1])
    mixer_grads = gsm[:, :, 0:rows, :].reshape(S * D * rows, mixed)
    mixer_term = norm * mm(mixer_columns, mixer_grads, 0, 0)
    band = mixer_term.shape[0] // C
    for q in range(C):
        m_o[q] = mixer_term[q * band : (q + 1) * band, :].astype(BF)

    def share_m(q, landing, slot):
        return rcopy(m_o.at[q], m_i.at[landing], m_s.at[q], m_r.at[slot], chan=q)

    each(C, lambda d: share_m(lax.rem(ch + d, C), ch, ch).start())
    step_total = None
    for k in range(S) if S <= 12 else ():
        for e in range(D):
            x = xc[k, e].reshape(length, xc.shape[-1])
            term = mm(gsm[k, e, rows:, 0:LANES], x, 1, 0)
            step_total = term if step_total is None else step_total + term
    if step_total is None:

        def one(k, carry):
            for e in range(D):
                x = xc[k, e].reshape(length, xc.shape[-1])
                carry = carry + mm(gsm[k, e, rows:, 0:LANES], x, 1, 0)
            return carry

        step_total = lax.fori_loop(0, S, one, jnp.zeros((PAD, xc.shape[-1]), F32))
    o_dws[...] = (norm * step_total)[:heads, :]

    p_i[ch] = p_o[ch]
    for j in range(parts):
        each(C, lambda d, j=j: share_p(j, lax.rem(ch + d, C), ch, lax.rem(ch + d, C)).wait_recv())
    weight_terms(S - 1)
    m_i[ch] = m_o[ch]
    each(C, lambda d: share_m(lax.rem(ch + d, C), ch, lax.rem(ch + d, C)).wait_recv())

    @pl.when(me > 0)
    def _():
        halo().wait_send()

    def settle_chan(d):
        q = lax.rem(ch + d, C)
        share_mix(q, ch, ch).wait_send()
        share_m(q, ch, ch).wait_send()
        for j in range(parts):
            share_p(j, q, ch, ch).wait_send()

    each(C, settle_chan)

    def settle_line(k):
        for e in others():
            for p in range(parts):
                ccopy(p, k, mine, e).wait_send()
        for way, sent in (("up", (k <= me) & (me < S - 1)), ("down", (k >= me) & (me > 0))):

            @pl.when(sent)
            def _(way=way):
                for p in range(parts):
                    zcopy(p, way, k).wait_send()
                for e in [mine] + others():
                    zsmall(way, e, k).wait_send()

    settle_line(0)
    each(S, settle_line)
    for e in others():
        csmall(mine, e).wait_send()


def finish_kernel(parts, dw, mixes, dws, o_ig, o_dw, o_dwm, o_dws, ig, dwm, sems):
    copies = [
        pltpu.make_async_copy(a, b, sems.at[i])
        for i, (a, b) in enumerate(((dw, o_dw), (dws, o_dws), (ig, o_ig), (dwm, o_dwm)))
    ]
    copies[0].start()
    copies[1].start()
    total = parts[0].astype(F32)
    for q in range(1, parts.shape[0]):
        total = total + parts[q].astype(F32)
    ig[...] = total.astype(BF)
    copies[2].start()
    total = mixes[0].astype(F32)
    for q in range(1, mixes.shape[0]):
        total = total + mixes[q].astype(F32)
    dwm[...] = total
    copies[3].start()
    for copy in copies:
        copy.wait()


def local_call(kernel, out_shapes, scratch, name, *arrays):
    vmem = pl.BlockSpec(memory_space=pltpu.VMEM)
    return pl.pallas_call(
        kernel,
        out_shape=out_shapes,
        in_specs=[vmem] * len(arrays),
        out_specs=jax.tree.map(lambda unused: vmem, out_shapes),
        scratch_shapes=scratch,
        compiler_params=pltpu.CompilerParams(vmem_limit_bytes=LIMIT),
        name=name,
    )(*arrays)


def body(
    sizes,
    layer_input,
    inner_weight,
    mixer_weight,
    step_weight,
    conv_inner,
    conv_mixer,
    step_bias,
    decay_log,
    skip_gain,
    output_grad,
):
    own = layer_input[0]
    rows, model = own.shape
    chans, seqs, dps = sizes["chan"], sizes["seq"], sizes["dp"]
    groups = dps * seqs
    length = rows * chans
    width = inner_weight.shape[1]
    mixed = mixer_weight.shape[1]
    heads = step_bias.shape[0]
    cols = model // groups
    state_size = mixed // 2
    assert length == LANES and heads + conv_inner.shape[0] - 1 <= PAD
    upstream = output_grad[0]
    step_rows = step_weight.T
    bias, rates, skips = (v.reshape(1, heads) for v in (step_bias, decay_log, skip_gain))
    dma = pltpu.SemaphoreType.DMA
    vmem = pl.BlockSpec(memory_space=pltpu.VMEM)
    hbm = pl.BlockSpec(memory_space=pl.ANY)
    state_shape = jax.ShapeDtypeStruct((width, state_size), BF)
    inner_sum, mixer_sum, step_raw, state, back_state, decay, xs = pl.pallas_call(
        functools.partial(front_kernel, sizes, heads),
        out_shape=(
            jax.ShapeDtypeStruct((length, width), F32),
            jax.ShapeDtypeStruct((length, mixed), F32),
            jax.ShapeDtypeStruct((length, LANES), F32),
            state_shape,
            state_shape,
            jax.ShapeDtypeStruct((width, state_size), F32),
            jax.ShapeDtypeStruct((seqs, dps, rows, cols), BF),
        ),
        in_specs=[vmem] + [hbm] * 2 + [vmem] * 6,
        out_specs=(vmem,) * 7,
        scratch_shapes=[
            pltpu.VMEM((model, width), BF),
            pltpu.VMEM((model, mixed), BF),
            pltpu.VMEM((LANES, model), BF),
            pltpu.VMEM((length, model), BF),
            pltpu.VMEM((dps, seqs, rows, cols), BF),
            pltpu.VMEM((dps, seqs, rows, cols), BF),
            pltpu.VMEM((PAD + length, width), F32),
            pltpu.VMEM((PAD + length, mixed), F32),
            pltpu.VMEM((PAD, width + mixed), BF),
            pltpu.VMEM((PAD, width + mixed), BF),
            pltpu.VMEM((8, LANES), F32),
            dma((2,)),
            dma((chans,)), dma((chans,)),
            dma((chans // 2, chans)), dma((chans // 2, chans)),
            dma((chans // 2, chans)), dma((chans // 2, chans)),
            dma((dps,)), dma((dps,)), dma((seqs,)), dma((seqs,)), dma((2,)),
        ],
        compiler_params=pltpu.CompilerParams(
            collective_id=0, has_side_effects=True, vmem_limit_bytes=LIMIT
        ),
        name="front",
    )(own, inner_weight, mixer_weight, step_rows, conv_inner, conv_mixer, bias, rates, upstream)
    xc, start, end = pl.pallas_call(
        functools.partial(mid_kernel, sizes),
        out_shape=(
            jax.ShapeDtypeStruct((seqs, dps, chans, rows, cols), BF),
            state_shape,
            state_shape,
        ),
        in_specs=[vmem] * 4,
        out_specs=(vmem,) * 3,
        scratch_shapes=[
            pltpu.VMEM(state.shape, BF),
            pltpu.VMEM(state.shape, BF),
            dma((chans,)), dma((chans,)),
        ]
        + [dma((Chain.pieces,)) for unused in range(4)],
        compiler_params=pltpu.CompilerParams(
            collective_id=1, has_side_effects=True, vmem_limit_bytes=LIMIT
        ),
        name="middle",
    )(xs, state, back_state, decay)
    a_in, a_mix, steps = local_call(
        functools.partial(backward_kernel, heads),
        (
            jax.ShapeDtypeStruct((length, width), F32),
            jax.ShapeDtypeStruct((length, mixed), F32),
            jax.ShapeDtypeStruct((length, LANES), F32),
        ),
        [pltpu.VMEM((length, width), F32), pltpu.VMEM((length, width), F32), pltpu.VMEM((8, LANES), F32)],
        "backward",
        inner_sum, mixer_sum, step_raw, bias, rates, skips, upstream, start, end,
    )
    small = rows + PAD
    band = cols // chans
    parts, inner_grad, mix_parts, step_grad = pl.pallas_call(
        functools.partial(back_kernel, sizes, heads),
        out_shape=(
            jax.ShapeDtypeStruct((chans, rows, model), BF),
            jax.ShapeDtypeStruct((cols, width), F32),
            jax.ShapeDtypeStruct((chans, band, mixed), BF),
            jax.ShapeDtypeStruct((heads, cols), F32),
        ),
        in_specs=[vmem] * 5 + [hbm] * 2 + [vmem] * 2,
        out_specs=(vmem,) * 4,
        scratch_shapes=[
            pltpu.VMEM((model, width), BF),
            pltpu.VMEM((model, mixed), BF),
            pltpu.VMEM((PAD, model), BF),
            pltpu.VMEM((length + 8, width), F32),
            pltpu.VMEM((length + 8, mixed), F32),
            pltpu.VMEM((seqs, dps, length, width), BF),
            pltpu.VMEM((seqs, dps, small, mixed), BF),
            pltpu.VMEM((8, width + mixed), F32),
            pltpu.VMEM((8, width + mixed), F32),
            pltpu.VMEM((length, mixed), BF),
            pltpu.VMEM((chans, rows, mixed), BF),
            pltpu.VMEM((chans, rows, model), BF),
            pltpu.VMEM((chans, band, mixed), BF),
            dma((2,)), dma((2,)),
            dma((chans, seqs)), dma((chans, dps, seqs)),
            dma((chans, seqs)), dma((chans, seqs)), dma((chans, dps, seqs)),
            dma((dps,)), dma((dps, seqs)), dma((dps,)), dma((dps, seqs)), dma((dps, seqs)),
            dma((chans,)), dma((chans,)),
            dma((chans, chans)), dma((chans, chans)),
            dma((chans,)), dma((chans,)),
        ],
        compiler_params=pltpu.CompilerParams(
            collective_id=2, has_side_effects=True, vmem_limit_bytes=LIMIT
        ),
        name="back",
    )(a_in, a_mix, steps, conv_inner, conv_mixer, inner_weight, mixer_weight, step_rows, xc)
    input_grad, inner_grad, mixer_grad, step_grad = pl.pallas_call(
        finish_kernel,
        out_shape=(
            jax.ShapeDtypeStruct((rows, model), BF),
            jax.ShapeDtypeStruct((cols, width), F32),
            jax.ShapeDtypeStruct((band, mixed), F32),
            jax.ShapeDtypeStruct((heads, cols), F32),
        ),
        in_specs=[vmem] * 4,
        out_specs=(hbm,) * 4,
        scratch_shapes=[
            pltpu.VMEM((rows, model), BF),
            pltpu.VMEM((band, mixed), F32),
            dma((4,)),
        ],
        compiler_params=pltpu.CompilerParams(vmem_limit_bytes=LIMIT),
        name="finish",
    )(parts, inner_grad, mix_parts, step_grad)
    return input_grad[None], inner_grad, mixer_grad, step_grad.T


def solution(mesh):
    sizes = dict(mesh.shape)
    in_specs = (
        P("dp", ("seq", "chan"), None),
        P(None, "chan"),
        P(),
        P(None, "chan"),
        P(None, "chan"),
        P(),
        P("chan"),
        P("chan"),
        P("chan"),
        P("dp", "seq", "chan"),
    )
    out_specs = (
        P("dp", ("seq", "chan"), None),
        P(("dp", "seq"), "chan"),
        P(("dp", "seq", "chan"), None),
        P(("dp", "seq"), "chan"),
    )
    return jax.shard_map(
        functools.partial(body, sizes),
        mesh=mesh,
        in_specs=in_specs,
        out_specs=out_specs,
        check_vma=False,
    )
```

time: 99.1 us -> 80 us (0.81)
  Pallas kernels: 81.4 us -> 70.1 us
  matrix products: 4.59 us -> 0 us
  local copies, waits for them, and re-layouts: 11.2 us -> 8.7 us
    pallas_call x1, Pallas kernels: 27 us -> 21.4 us  [body(): pl.pallas_call(functools.partial(mid_kernel, sizes), out_shape=(jax.Shape...]
    pallas_call x2 -> x1, Pallas kernels: 8.31 us -> 3.32 us  [local_call(): pl.pallas_call(kernel, out_shape=out_shapes, in_specs=[vmem] * len(arrays...]
    dot_general x3 -> x0, matrix products: 4.59 us -> none  [the longest x1 2.18 us: body(): step_raw = jnp.dot(tokens[PAD:], step_wide, preferred_element_type=F32)]
    pallas_call x1, Pallas kernels: 29.3 us -> 27 us  [body(): pl.pallas_call(functools.partial(back_kernel, sizes, heads), out_shape=(j...]
    another operation x2 -> x0, local copies, waits for them, and re-layouts: 1.84 us -> none  [body(): blocks = own.reshape(rows, dps, seqs, model // groups).transpose(1, 2, 0, 3)]
    pallas_call x1 -> x2, Pallas kernels: 16.8 us -> 18.4 us  [the longest x1 17.4 us: body(): pl.pallas_call(functools.partial(front_kernel, sizes, heads), out_shape=(...]
    unnamed x13 -> x36, local copies, waits for them, and re-layouts: 7.25 us -> 8.7 us
    broadcast_in_dim x2 -> x0, local copies, waits for them, and re-layouts: 1.17 us -> none  [body(): jnp.broadcast_to(skips, (8, LANES))]
where the time goes in v2:
time: 80 us; the launch traced here: 79.6 us
  Pallas kernels  70.1 us (88%)
  local copies, waits for them, and re-layouts  8.7 us (11%)
  between operations  0.8 us (1%)
    pallas_call x1, Pallas kernels, body(): pl.pallas_call(functools.partial(back_kernel, sizes, heads), out_shape=(j...  27 us
    pallas_call x1, Pallas kernels, body(): pl.pallas_call(functools.partial(mid_kernel, sizes), out_shape=(jax.Shape...  21.4 us
    pallas_call x1, Pallas kernels, body(): pl.pallas_call(functools.partial(front_kernel, sizes, heads), out_shape=(...  17.4 us
    unnamed x36, local copies, waits for them, and re-layouts  8.7 us
    pallas_call x1, Pallas kernels, local_call(): pl.pallas_call(kernel, out_shape=out_shapes, in_specs=[vmem] * len(arrays...  3.32 us

profile of v2, /device:TPU:0, one launch (start us, length us, event | category | flops | bytes accessed | tf_op | source)
XLA Modules:
  0.0 79.6 jit_solution(11234035392767314208)
XLA Ops:
  0.6 0.0 copy-start.17
  0.6 0.0 copy-start.16
  0.7 0.0 copy-start.14
  0.7 0.0 copy-start
  0.7 1.9 %copy-done = bf16[2560,640]{1,0:T(8,128)(2,1)S(1)} copy-done((bf16[2560,640]{1,0:T(8,128)(2,1)S(1)}, bf16[2560,640]{1,0:T(8,128)(2,1)}, u32[]{:S(2)}) %copy-start) | copy-done | bytes 3276824
  2.6 1.3 %copy-done.2 = bf16[2560,256]{1,0:T(8,128)(2,1)S(1)} copy-done((bf16[2560,256]{1,0:T(8,128)(2,1)S(1)}, bf16[2560,256]{1,0:T(8,128)(2,1)}, u32[]{:S(2)}) %copy-start.2) | copy-done | bytes 1310744
  3.9 0.9 %copy-done.4 = bf16[1,128,640]{2,1,0:T(8,128)(2,1)S(1)} copy-done((bf16[1,128,640]{2,1,0:T(8,128)(2,1)S(1)}, bf16[1,128,640]{2,1,0:T(8,128)(2,1)}, u32[]{:S(2)}) %copy-start.4) | copy-done | bytes 163864
  4.8 0.9 %copy-done.6 = bf16[2560,10]{0,1:T(8,128)(2,1)S(1)} copy-done((bf16[2560,10]{0,1:T(8,128)(2,1)S(1)}, bf16[2560,10]{0,1:T(8,128)(2,1)}, u32[]{:S(2)}) %copy-start.6) | copy-done | bytes 51224
  5.7 0.9 %copy-done.8 = bf16[1,32,2560]{2,1,0:T(8,128)(2,1)S(1)} copy-done((bf16[1,32,2560]{2,1,0:T(8,128)(2,1)S(1)}, bf16[1,32,2560]{2,1,0:T(8,128)(2,1)}, u32[]{:S(2)}) %copy-start.8) | copy-done | bytes 163864
  6.6 0.7 copy-done.9
  7.4 0.7 copy-done.11
  8.0 0.7 copy-done.13
  8.7 0.7 copy-done.15
  9.4 0.0 copy-start.10
  9.4 0.0 copy-start.12
  9.4 17.4 %front.1 = (f32[128,640]{1,0:T(8,128)S(1)}, f32[128,256]{1,0:T(8,128)S(1)}, f32[128,128]{1,0:T(8,128)S(1)}, bf16[640,128]{1,0:T(8,128)(2,1)S(1)}, bf16[640,128]{...) custom-call(bf16[32,2560]{1,0:T(8,128)(2,1)S(1)} %bitcast.12, ...), custom_call_target="tpu_custom_call" | custom-call | tf_op jit(solution)/shard_map/front/pallas_call | solution.py:780
  26.8 21.4 %middle.1 = (bf16[4,2,4,32,320]{4,3,2,1,0:T(8,128)(2,1)S(1)}, bf16[640,128]{1,0:T(8,128)(2,1)S(1)}, bf16[640,128]{1,0:T(8,128)(2,1)S(1)}) custom-call(bf16[4,2,32,320]{3,2,1,0:T(8,128)(2,1)S(1)} %get-tuple-element.28.xs, bf16[640,128]{1,0:T(8,128)(2,1)S(1)} %get-tuple-element.29.state, bf16[640,128]{1,0:T(8,128)(2,1)S(1)} %get-tuple-element.30.back, ...), custom_call_target="tpu_custom_call" | custom-call | tf_op jit(solution)/shard_map/middle/pallas_call | solution.py:816
  48.2 0.0 copy-done.17
  48.2 0.0 copy-done.16
  48.2 0.0 copy-done.14
  48.2 0.0 copy-done.5
  48.2 3.3 %backward.1 = (f32[128,640]{1,0:T(8,128)S(1)}, f32[128,256]{1,0:T(8,128)S(1)}, f32[128,128]{1,0:T(8,128)S(1)}) custom-call(f32[128,640]{1,0:T(8,128)S(1)} %get-tuple-element.25.inner_ref, f32[128,256]{1,0:T(8,128)S(1)} %get-tuple-element.26.mixer_ref, f32[128,128]{1,0:T(8,128)S(1)} %get-tuple-element.27.raw_ref, f32[1,10]{1,0:T(1,128)S(1)} %bitcast.14, ...), custom_call_target="tpu_custom_call" | custom-call | tf_op jit(solution)/shard_map/backward/pallas_call | solution.py:738
  51.6 27.0 %back.1 = (bf16[4,32,2560]{2,1,0:T(8,128)(2,1)S(1)}, f32[320,640]{1,0:T(8,128)S(1)}, bf16[4,80,256]{2,1,0:T(8,128)(2,1)S(1)}, f32[10,320]{1,0:T(8,128)S(1)}) custom-call(f32[128,640]{1,0:T(8,128)S(1)} %get-tuple-element.34.a_in, f32[128,256]{1,0:T(8,128)S(1)} %get-tuple-element.35.a_mix, f32[128,128]{1,0:T(8,128)S(1)} %get-tuple-element.36.st, ...), custom_call_target="tpu_custom_call" | custom-call | tf_op jit(solution)/shard_map/back/pallas_call | solution.py:849
  78.6 1.0 %finish.1 = (bf16[32,2560]{1,0:T(8,128)(2,1)}, f32[320,640]{1,0:T(8,128)}, f32[80,256]{1,0:T(8,128)}, f32[10,320]{1,0:T(8,128)}) custom-call(bf16[4,32,2560]{2,1,0:T(8,128)(2,1)S(1)} %get-tuple-element.38.parts, f32[320,640]{1,0:T(8,128)S(1)} %get-tuple-element.39.dw, bf16[4,80,256]{2,1,0:T(8,128)(2,1)S(1)} %get-tuple-element.40.mixes, ...), custom_call_target="tpu_custom_call" | custom-call | tf_op jit(solution)/shard_map/finish/pallas_call | solution.py:886
  (17 shorter events, 0.0 us)
Async XLA Ops:
  0.6 47.5 %copy-start.17 = (f32[10]{0:T(128)S(1)}, f32[10]{0:T(128)}, u32[]{:S(2)}) copy-start(f32[10]{0:T(128)} %param.18) | copy-start | bytes 124
  0.6 47.5 %copy-start.16 = (f32[10]{0:T(128)S(1)}, f32[10]{0:T(128)}, u32[]{:S(2)}) copy-start(f32[10]{0:T(128)} %param.17) | copy-start | bytes 124
  0.7 47.5 %copy-start.14 = (f32[10]{0:T(128)S(1)}, f32[10]{0:T(128)}, u32[]{:S(2)}) copy-start(f32[10]{0:T(128)} %param.16) | copy-start | bytes 124
  0.7 1.9 %copy-start = (bf16[2560,640]{1,0:T(8,128)(2,1)S(1)}, bf16[2560,640]{1,0:T(8,128)(2,1)}, u32[]{:S(2)}) copy-start(bf16[2560,640]{1,0:T(8,128)(2,1)} %w_in_h.3) | copy-start | bytes 9830404
  2.6 1.3 %copy-start.2 = (bf16[2560,256]{1,0:T(8,128)(2,1)S(1)}, bf16[2560,256]{1,0:T(8,128)(2,1)}, u32[]{:S(2)}) copy-start(bf16[2560,256]{1,0:T(8,128)(2,1)} %w_mix_h.3) | copy-start | bytes 3932164
  3.9 0.9 %copy-start.4 = (bf16[1,128,640]{2,1,0:T(8,128)(2,1)S(1)}, bf16[1,128,640]{2,1,0:T(8,128)(2,1)}, u32[]{:S(2)}) copy-start(bf16[1,128,640]{2,1,0:T(8,128)(2,1)} %param.19) | copy-start | bytes 491524
  4.8 0.9 %copy-start.6 = (bf16[2560,10]{0,1:T(8,128)(2,1)S(1)}, bf16[2560,10]{0,1:T(8,128)(2,1)}, u32[]{:S(2)}) copy-start(bf16[2560,10]{0,1:T(8,128)(2,1)} %param.13) | copy-start | bytes 153604
  5.7 0.9 %copy-start.8 = (bf16[1,32,2560]{2,1,0:T(8,128)(2,1)S(1)}, bf16[1,32,2560]{2,1,0:T(8,128)(2,1)}, u32[]{:S(2)}) copy-start(bf16[1,32,2560]{2,1,0:T(8,128)(2,1)} %param.10) | copy-start | bytes 491524
  6.6 0.7 copy-start.9
  7.3 0.7 copy-start.11
  8.0 0.7 copy-start.13
  8.7 0.7 copy-start.15
  9.3 38.9 %copy-start.5 = (bf16[1,128,640]{2,1,0:T(8,128)(2,1)S(1)}, bf16[1,128,640]{2,1,0:T(8,128)(2,1)}, u32[]{:S(2)}) copy-start(bf16[1,128,640]{2,1,0:T(8,128)(2,1)} %param.19) | copy-start | bytes 491524
  9.3 42.2 %copy-start.1 = (bf16[2560,640]{1,0:T(8,128)(2,1)S(1)}, bf16[2560,640]{1,0:T(8,128)(2,1)}, u32[]{:S(2)}) copy-start(bf16[2560,640]{1,0:T(8,128)(2,1)} %w_in_h.3) | copy-start | bytes 9830404
  9.4 42.2 %copy-start.3 = (bf16[2560,256]{1,0:T(8,128)(2,1)S(1)}, bf16[2560,256]{1,0:T(8,128)(2,1)}, u32[]{:S(2)}) copy-start(bf16[2560,256]{1,0:T(8,128)(2,1)} %w_mix_h.3) | copy-start | bytes 3932164
  9.4 42.2 %copy-start.7 = (bf16[2560,10]{0,1:T(8,128)(2,1)S(1)}, bf16[2560,10]{0,1:T(8,128)(2,1)}, u32[]{:S(2)}) copy-start(bf16[2560,10]{0,1:T(8,128)(2,1)} %param.13) | copy-start | bytes 153604
  9.4 42.2 %copy-start.10 = (f32[4,640]{1,0:T(4,128)S(1)}, f32[4,640]{1,0:T(4,128)}, u32[]{:S(2)}) copy-start(f32[4,640]{1,0:T(4,128)} %conv_in.3) | copy-start | bytes 30724
  9.4 42.2 %copy-start.12 = (f32[4,256]{1,0:T(4,128)S(1)}, f32[4,256]{1,0:T(4,128)}, u32[]{:S(2)}) copy-start(f32[4,256]{1,0:T(4,128)} %conv_mix.3) | copy-start | bytes 12292

commit v3 on v2

v3 whole, which is shorter than its diff:
```python
import functools
import math
import types

import jax
import jax.numpy as jnp
from jax import lax
from jax.experimental import pallas as pl
from jax.experimental.pallas import tpu as pltpu
from jax.sharding import PartitionSpec as P

MESH = pl.DeviceIdType.MESH
HDIM = 64
PAD = 16
LANES = 128
LIMIT = 48 * 2**20
BF = jnp.bfloat16
F32 = jnp.float32
HIGH = lax.Precision.HIGHEST
PIECES = 10
LOADED = (
    "own", "w_in", "w_mix", "w_step", "conv_in", "conv_mix", "bias", "log", "skip", "grad",
)


def each(n, step):
    if n <= 12:
        for d in range(1, n):
            step(d)
    else:

        def one(d, carry):
            step(d)
            return carry

        lax.fori_loop(1, n, one, 0)


def signal_to(barrier, where):
    pl.semaphore_signal(barrier, inc=1, device_id=where, device_id_type=MESH)


def mm(a, b, da, db):
    return lax.dot_general(
        a.astype(BF), b.astype(BF), (((da,), (db,)), ((), ())), preferred_element_type=F32
    )


def exact(a, b, da=1, db=0):
    return lax.dot_general(
        a, b, (((da,), (db,)), ((), ())), precision=HIGH, preferred_element_type=F32
    )


def softplus(v):
    return jnp.maximum(v, 0.0) + jnp.log1p(jnp.exp(-jnp.abs(v)))


def head_mask(width, heads_first):
    shape = (LANES, width) if heads_first else (width, LANES)
    head = lax.broadcasted_iota(jnp.int32, shape, 0 if heads_first else 1)
    column = lax.broadcasted_iota(jnp.int32, shape, 1 if heads_first else 0)
    return (column // HDIM == head).astype(F32)


def decays(raw, bias, decay_log):
    length = raw.shape[0]
    step = softplus(raw + bias)
    rate = jnp.exp(decay_log)
    row = lax.broadcasted_iota(jnp.int32, (length, length), 0)
    col = lax.broadcasted_iota(jnp.int32, (length, length), 1)
    lower = (row >= col).astype(F32)
    cumulative = exact(lower, -step * rate)
    return step, rate, cumulative, row, col, lower


def rcopy(src, dst, send, recv, **where):
    return pltpu.make_async_remote_copy(
        src_ref=src, dst_ref=dst, send_sem=send, recv_sem=recv, device_id=where, device_id_type=MESH
    )


def greet_all(barrier, axis, n):
    me = lax.axis_index(axis)
    each(n, lambda d: signal_to(barrier, {axis: lax.rem(me + d, n)}))
    return n - 1


def convolved(wide, kernel, first, count):
    taps = kernel.shape[0]
    first = first + PAD - (taps - 1)
    total = kernel[0:1, :] * wide[pl.ds(first, count), :]
    for k in range(1, taps):
        total = total + kernel[k : k + 1, :] * wide[pl.ds(first + k, count), :]
    return total


def spread_back(pad, kernel, first, count):
    taps = kernel.shape[0]
    total = None
    for k in range(taps):
        term = kernel[k : k + 1, :] * pad[pl.ds(first + taps - 1 - k, count), :]
        total = term if total is None else total + term
    return total.astype(BF)


def layer_kernel(names, sizes, heads, *refs):
    r = types.SimpleNamespace(**dict(zip(names, refs, strict=True)))
    place = (lax.axis_index("dp"), lax.axis_index("seq"), lax.axis_index("chan"))
    D, S, C = sizes["dp"], sizes["seq"], sizes["chan"]
    barrier = pltpu.get_barrier_semaphore()
    total = greet_all(barrier, "dp", D) + greet_all(barrier, "seq", S) + greet_all(barrier, "chan", C)
    loads = {
        key: pltpu.make_async_copy(getattr(r, key + "_h"), getattr(r, key), r.load_sem.at[i])
        for i, key in enumerate(LOADED)
    }
    for copy in loads.values():
        copy.start()
    front(r, sizes, place, heads, loads, barrier, total)
    scan_back(r, sizes, place, heads)
    back(r, sizes, place, heads)


def front(r, sizes, place, heads, loads, barrier, total):
    D, S, C = sizes["dp"], sizes["seq"], sizes["chan"]
    mine, me, ch = place
    rows, model = r.own.shape
    length, width = r.sum_in.shape
    mixed = r.sum_mix.shape[1]
    cols = model // (D * S)
    half = mixed // 2
    pieces = C
    cut = model // pieces
    sides = C // 2
    side, low = lax.div(ch, 2), lax.rem(ch, 2)
    partner = ch + 1 - 2 * low

    def block(c, p):
        return r.xg.at[pl.ds(pl.multiple_of(c * rows, rows), rows), pl.ds(p * cut, cut)]

    def mine_at(p):
        return r.own.at[:, pl.ds(p * cut, cut)]

    def near(c, p):
        return rcopy(mine_at(p), block(c, p), r.near_s.at[p], r.near_r.at[p], chan=partner)

    def far(to, c, slot, p):
        return rcopy(
            mine_at(p), block(c, p), r.far_s.at[to, p], r.far_r.at[slot, p], chan=2 * to + low
        )

    def relay(source, lane, p):
        c = 2 * source + lane
        here = block(c, p)
        return rcopy(here, here, r.relay_s.at[source, p], r.relay_r.at[source, p], chan=partner)

    def swap(q, landing, slot):
        return rcopy(r.blocks.at[q], r.mid.at[landing], r.swap_s.at[q], r.swap_r.at[slot], dp=q)

    def cross(q, landing, slot):
        return rcopy(r.mid.at[:, q], r.xs.at[landing], r.cross_s.at[q], r.cross_r.at[slot], seq=q)

    loads["own"].wait()
    pl.semaphore_wait(barrier, total)
    for p in range(pieces):
        for d in range(1, sides):
            far(lax.rem(side + d, sides), ch, side, p).start()
        near(ch, p).start()
    for d in range(D):
        for k in range(S):
            at = (d * S + k) * cols
            r.blocks[d, k] = r.own[:, at : at + cols]
    each(D, lambda d: swap(lax.rem(mine + d, D), mine, mine).start())
    r.mid[mine] = r.blocks[mine]
    r.xg[pl.ds(pl.multiple_of(ch * rows, rows), rows), :] = r.own[...]
    r.wst[...] = jnp.zeros(r.wst.shape, BF)
    r.vec[...] = jnp.zeros(r.vec.shape, F32)
    for key in LOADED[1:]:
        loads[key].wait()
    r.wst[0:heads, :] = r.w_step[...]
    for i, ref in enumerate((r.bias, r.log, r.skip)):
        r.vec[i : i + 1, 0:heads] = ref[...]

    def pass_on(p):
        for d in range(1, sides):
            source = lax.rem(side + d, sides)
            far(source, ch, source, p).wait_recv()
            relay(source, low, p).start()

    def project(p):
        near(partner, p).wait_recv()
        for d in range(1, sides):
            source = lax.rem(side + d, sides)
            relay(source, 1 - low, p).wait_recv()
        piece = slice(p * cut, (p + 1) * cut)
        x = r.xg[:, piece]
        inner = mm(x, r.w_in[piece, :], 1, 0)
        mixer = mm(x, r.w_mix[piece, :], 1, 0)
        raw = mm(x, r.wst[:, piece], 1, 1)
        if p == 0:
            r.wide_in[PAD:, :], r.wide_mix[PAD:, :], r.raw[...] = inner, mixer, raw
        else:
            r.wide_in[PAD:, :] = r.wide_in[PAD:, :] + inner
            r.wide_mix[PAD:, :] = r.wide_mix[PAD:, :] + mixer
            r.raw[...] = r.raw[...] + raw

    pass_on(0)
    for p in range(pieces):
        if p + 1 < pieces:
            pass_on(p + 1)
        project(p)
        if p == pieces // 2:
            each(D, lambda d: swap(lax.rem(mine + d, D), mine, lax.rem(mine + d, D)).wait_recv())
            each(S, lambda d: cross(lax.rem(me + d, S), me, me).start())
            r.xs[me] = r.mid[:, me]
    inner_low = r.wide_in[PAD:, :].astype(BF)
    mixer_low = r.wide_mix[PAD:, :].astype(BF)
    r.fh_o[:, :width] = inner_low[length - PAD :, :]
    r.fh_o[:, width:] = mixer_low[length - PAD :, :]

    def halo():
        return rcopy(r.fh_o, r.fh_i, r.fh_sem.at[0], r.fh_sem.at[1], seq=lax.rem(me + 1, S))

    @pl.when(me < S - 1)
    def _():
        halo().start()

    r.wide_in[PAD:, :] = inner_low.astype(F32)
    r.wide_mix[PAD:, :] = mixer_low.astype(F32)
    r.wide_in[0:PAD, :] = jnp.zeros((PAD, width), F32)
    r.wide_mix[0:PAD, :] = jnp.zeros((PAD, mixed), F32)
    r.sum_in[PAD:, :] = convolved(r.wide_in, r.conv_in, PAD, length - PAD)
    r.sum_mix[PAD:, :] = convolved(r.wide_mix, r.conv_mix, PAD, length - PAD)
    step, rate, cumulative, row, col, lower = decays(r.raw[...], r.vec[0:1, :], r.vec[1:2, :])
    last = cumulative[length - 1 : length, :]
    spread = head_mask(width, True)
    r.cum[...] = cumulative
    step_wide = exact(step, spread)
    fading = exact(jnp.exp(last - cumulative), spread)
    grown = exact(jnp.exp(cumulative), spread)
    r.step_wide[...] = step_wide
    r.fading[...] = fading
    r.grown[...] = grown
    pulled = (grown * r.grad[...].astype(F32)).astype(BF)
    r.pulled[...] = pulled
    row_decay = jnp.sum(head_mask(width, False) * jnp.exp(last), axis=1, keepdims=True)
    r.decay[...] = jnp.broadcast_to(row_decay, r.decay.shape)

    @pl.when(me > 0)
    def _():
        halo().wait_recv()
        r.wide_in[0:PAD, :] = r.fh_i[:, :width].astype(F32)
        r.wide_mix[0:PAD, :] = r.fh_i[:, width:].astype(F32)

    r.sum_in[0:PAD, :] = convolved(r.wide_in, r.conv_in, 0, PAD)
    r.sum_mix[0:PAD, :] = convolved(r.wide_mix, r.conv_mix, 0, PAD)
    mixer = r.sum_mix[...]
    mix = mixer * jax.nn.sigmoid(mixer)
    r.mix[...] = mix.astype(BF)
    r.back_term[...] = mm(pulled, mix[:, half:], 0, 0).astype(BF)
    inner = r.sum_in[...]
    act = inner * jax.nn.sigmoid(inner)
    r.act[...] = act
    r.state_term[...] = mm(act * (fading * step_wide), mix[:, :half], 0, 0).astype(BF)

    @pl.when(me < S - 1)
    def _():
        halo().wait_send()

    for p in range(pieces):
        near(ch, p).wait_send()
        for d in range(1, sides):
            source = lax.rem(side + d, sides)
            far(source, ch, source, p).wait_send()
            relay(source, low, p).wait_send()
    each(D, lambda d: swap(lax.rem(mine + d, D), mine, mine).wait_send())

    def settle(d):
        q = lax.rem(me + d, S)
        cross(q, me, q).wait()

    each(S, settle)


def scan_back(r, sizes, place, heads):
    S, C = sizes["seq"], sizes["chan"]
    mine, me, ch = place
    length, width = r.sum_in.shape
    half = r.sum_mix.shape[1] // 2
    pieces, lag = PIECES, PIECES // 2
    size = width // pieces
    terms, outs, scratch = (r.state_term, r.back_term), (r.start, r.end), (r.scr0, r.scr1)
    spots = (me, S - 1 - me)

    def carry(way, piece, first=False):
        part = pl.ds(pl.multiple_of(piece * size, size), size)
        to = lax.rem(me + 1, S) if way == 0 else lax.rem(me + S - 1, S)
        source = terms[way] if first else scratch[way]
        sems = r.chain_s.at[way, piece], r.chain_r.at[way, piece]
        return rcopy(source.at[part], outs[way].at[part], *sems, seq=to)

    for way in (0, 1):

        @pl.when(spots[way] == 0)
        def _(way=way):
            for piece in range(pieces):
                carry(way, piece, True).start()
            outs[way][...] = jnp.zeros(outs[way].shape, BF)

    def beat(t):
        for way in (0, 1):
            spot = spots[way]
            piece = t - lag * (spot - 1)

            @pl.when((piece >= 0) & (piece < pieces) & (spot > 0) & (spot < S - 1))
            def _(way=way, piece=piece):
                carry(way, piece).wait_recv()
                part = pl.ds(pl.multiple_of(piece * size, size), size)
                before = outs[way][part, :].astype(F32)
                term = terms[way][part, :].astype(F32)
                scratch[way][part, :] = (r.decay[part, :] * before + term).astype(BF)
                carry(way, piece).start()

    def gather(q, landing, slot):
        return rcopy(r.xs, r.xc.at[:, :, landing], r.gat_s.at[q], r.gat_r.at[slot], chan=q)

    each(C, lambda d: gather(lax.rem(ch + d, C), ch, ch).start())
    r.xc[:, :, ch] = r.xs[...]

    spread = head_mask(width, True)
    cumulative = r.cum[...]
    across = cumulative.T
    row = lax.broadcasted_iota(jnp.int32, (length, length), 0)
    col = lax.broadcasted_iota(jnp.int32, (length, length), 1)
    causal = row >= col
    lower = causal.astype(F32)
    into, out_of = r.mix[:, :half], r.mix[:, half:]
    scores = mm(out_of, into, 1, 1)
    act = r.act[...]
    stepped_low = (act * r.step_wide[...]).astype(BF)
    r.stepped[...] = stepped_low

    def head(h):
        cols = slice(h * HDIM, (h + 1) * HDIM)
        gap = cumulative[:, h : h + 1] - across[h : h + 1, :]
        decay = jnp.where(causal, jnp.exp(jnp.where(causal, gap, 0.0)), 0.0)
        weights = (decay * scores).astype(BF)
        grad_h, step_h = r.grad[:, cols], r.stepped[:, cols]
        term = decay * mm(grad_h, step_h, 1, 1)
        r.score_grad[...] = term if h == 0 else r.score_grad[...] + term
        r.z[:, cols] = mm(weights, grad_h, 0, 0)
        r.y[:, cols] = mm(weights, step_h, 1, 0)

    beats = pieces + lag * max(S - 3, 0)
    early = heads // 2
    for h in range(early):
        head(h)
    if beats <= 24:
        for t in range(beats):
            beat(t)
            if early + t < heads:
                head(early + t)
    else:
        for h in range(early, heads):
            head(h)
        lax.fori_loop(0, beats, lambda t, c: (beat(t), c)[1], 0)

    upstream = r.grad[...].astype(F32)
    stepped = r.stepped[...].astype(F32)
    step_wide = r.step_wide[...]
    skip_wide = exact(jnp.broadcast_to(r.vec[2:3, :], (8, LANES)), spread)[0:1, :]
    inner, mixer = r.sum_in[...], r.sum_mix[...]
    inner_gate, mixer_gate = jax.nn.sigmoid(inner), jax.nn.sigmoid(mixer)
    inner_slope = inner_gate * (1.0 + inner * (1.0 - inner_gate))
    mixer_slope = mixer_gate * (1.0 + mixer * (1.0 - mixer_gate))
    to_heads = functools.partial(exact, b=spread, da=1, db=1)
    z = r.z[...]
    r.slope_in[...] = inner_slope
    r.slope_mix[...] = mixer_slope
    r.local[...] = (step_wide * z + skip_wide * upstream) * inner_slope
    local_step = to_heads(r.act[...] * z)
    local_sum = to_heads(upstream * r.y[...] - stepped * z)
    score_grad = r.score_grad[...]
    out_local = mm(score_grad, into, 1, 0)
    into_local = mm(score_grad, out_of, 0, 0)
    faded = (r.fading[...] * stepped).astype(BF)

    for way in (0, 1):

        @pl.when(spots[way] == S - 1)
        def _(way=way):
            for piece in range(pieces):
                carry(way, piece).wait_recv()

    start, end = r.start[...], r.end[...]
    carried = r.grown[...] * mm(out_of, start, 1, 1)
    ending = r.fading[...] * mm(into, end, 1, 1)
    r.pad_in[0:length, :] = r.local[...] + (r.step_wide[...] * ending) * r.slope_in[...]
    r.pad_mix[0:length, :half] = (into_local + mm(faded, end, 1, 0)) * r.slope_mix[:, :half]
    r.pad_mix[0:length, half:] = (out_local + mm(r.pulled[...], start, 1, 0)) * r.slope_mix[:, half:]
    step_grad = local_step + to_heads(r.act[...] * ending)
    tail_term = to_heads(stepped * ending)
    sum_grad = local_sum + to_heads(upstream * carried) - tail_term
    held = jnp.sum(start.astype(F32) * end.astype(F32), axis=1, keepdims=True)
    last = cumulative[length - 1 : length, :]
    overall = jnp.sum(tail_term, axis=0, keepdims=True) + jnp.exp(last) * jnp.sum(
        head_mask(width, False) * held, axis=0, keepdims=True
    )
    decay_grad = exact(lower, sum_grad, 0, 0) + overall
    rate = jnp.exp(r.vec[1:2, :])
    step_grad = (step_grad - rate * decay_grad) * jax.nn.sigmoid(r.raw[...] + r.vec[0:1, :])
    r.steps[...] = step_grad.astype(BF)

    for way in (0, 1):

        @pl.when(spots[way] < S - 1)
        def _(way=way):
            for piece in range(pieces):
                carry(way, piece).wait_send()

    def settle_gather(d):
        q = lax.rem(ch + d, C)
        gather(q, q, q).wait()

    each(C, settle_gather)


def back(r, sizes, place, heads):
    D, S, C = sizes["dp"], sizes["seq"], sizes["chan"]
    mine, me, ch = place
    length, width = r.sum_in.shape
    mixed = r.sum_mix.shape[1]
    model = r.w_in.shape[0]
    rows = length // C
    parts = C
    r.hal_o[:, :width] = r.pad_in[0:8, :]
    r.hal_o[:, width:] = r.pad_mix[0:8, :]
    r.pad_in[length:, :] = jnp.zeros((8, width), F32)
    r.pad_mix[length:, :] = jnp.zeros((8, mixed), F32)
    last = length - rows
    r.gin[me, mine, 0:last, :] = spread_back(r.pad_in, r.conv_in, 0, last)
    r.gmp[0:last, :] = spread_back(r.pad_mix, r.conv_mix, 0, last)
    r.gsm[me, mine, rows:, 0:LANES] = r.steps[...].astype(F32).T[0:PAD, :].astype(BF)

    def others():
        return [lax.rem(mine + e, D) for e in range(1, D)]

    def halo():
        return rcopy(r.hal_o, r.hal_i, r.hal_sem.at[0], r.hal_sem.at[1], seq=lax.rem(me + S - 1, S))

    @pl.when(me > 0)
    def _():
        halo().start()

    def part(p, e, k):
        return r.gin.at[k, e, pl.ds(p * rows, rows)]

    def zcopy(p, way, k):
        to = lax.rem(me + (1 if way == "up" else S - 1), S)
        send = (r.u_s if way == "up" else r.d_s).at[p, k]
        return rcopy(part(p, mine, k), part(p, mine, k), send, r.z_r.at[p, k], seq=to)

    def ccopy(p, k, e, to):
        return rcopy(part(p, e, k), part(p, e, k), r.x_s.at[p, to, k], r.c_r.at[p, e, k], dp=to)

    def zsmall(way, e, k):
        to = lax.rem(me + (1 if way == "up" else S - 1), S)
        send = (r.u2_s if way == "up" else r.d2_s).at[e, k]
        return rcopy(r.gsm.at[k, e], r.gsm.at[k, e], send, r.z2_r.at[e, k], seq=to)

    def csmall(e, to):
        return rcopy(r.gsm.at[me, e], r.gsm.at[me, e], r.x2_s.at[to], r.c2_r.at[e], dp=to)

    def onward(make, k):
        @pl.when(me < S - 1)
        def _():
            make("up", k).start()

        @pl.when(me > 0)
        def _():
            make("down", k).start()

    def own_part(p):
        onward(functools.partial(zcopy, p), me)
        for e in others():
            ccopy(p, me, mine, e).start()

    def forward(d, p):
        for way, k, there, more in (
            ("up", me - d, me >= d, me < S - 1),
            ("down", me + d, me + d < S, me > 0),
        ):

            @pl.when(there)
            def _(way=way, k=k):
                zcopy(p, way, k).wait_recv()

            @pl.when(there & more)
            def _(way=way, k=k):
                zcopy(p, way, k).start()

            @pl.when(there)
            def _(k=k):
                for e in others():
                    ccopy(p, k, mine, e).start()

    def own_small():
        for e in others():
            csmall(mine, e).start()
        onward(lambda way, k: zsmall(way, mine, k), me)

    def cross_small():
        for e in others():
            csmall(e, e).wait_recv()
            onward(lambda way, k, e=e: zsmall(way, e, k), me)

    def forward_small(d):
        for way, k, there, more in (
            ("up", me - d, me >= d, me < S - 1),
            ("down", me + d, me + d < S, me > 0),
        ):
            for e in [mine] + others():

                @pl.when(there)
                def _(way=way, k=k, e=e):
                    zsmall(way, e, k).wait_recv()

                @pl.when(there & more)
                def _(way=way, k=k, e=e):
                    zsmall(way, e, k).start()

    norm = 1.0 / math.sqrt(D * S * length)

    def columns_of(k):
        block = r.xc[k]
        return block.reshape(D * length, block.shape[-1])

    def weight_term(k, first=False):
        for e in others():
            for p in range(parts):
                ccopy(p, k, e, e).wait_recv()
        x = columns_of(k)
        term = norm * mm(x, r.gin[k].reshape(D * length, width), 0, 0)
        r.o_dw[...] = term if first else r.o_dw[...] + term

    def weight_terms(d):
        for k, there in ((me - d, me >= d), (me + d, me + d < S)):

            @pl.when(there)
            def _(k=k):
                weight_term(k)

    for p in range(parts - 1):
        own_part(p)

    @pl.when(me < S - 1)
    def _():
        halo().wait_recv()
        r.pad_in[length:, :] = r.hal_i[:, :width]
        r.pad_mix[length:, :] = r.hal_i[:, width:]

    r.gin[me, mine, last:, :] = spread_back(r.pad_in, r.conv_in, last, rows)
    r.gmp[last:, :] = spread_back(r.pad_mix, r.conv_mix, last, rows)
    own_part(parts - 1)

    def share_mix(q, landing, slot):
        return rcopy(r.gmp.at[pl.ds(q * rows, rows)], r.gm_in.at[landing], r.gm_s.at[q], r.gm_r.at[slot], chan=q)

    each(C, lambda d: share_mix(lax.rem(ch + d, C), ch, ch).start())
    cut = model // parts

    def share_p(j, q, landing, slot):
        piece = pl.ds(j * cut, cut)
        return rcopy(
            r.p_o.at[q, :, piece], r.p_i.at[landing, :, piece], r.p_s.at[j, q], r.p_r.at[j, slot], chan=q
        )

    grads = r.gin[me, mine]
    mixes = r.gmp[...]
    steps = r.steps[:, 0:PAD]

    def back_project(j):
        piece = slice(j * cut, (j + 1) * cut)
        out = mm(grads, r.w_in[piece, :], 1, 1) + mm(mixes, r.w_mix[piece, :], 1, 1)
        out = out + mm(steps, r.wst[0:PAD, piece], 1, 0)
        r.p_o[:, :, piece] = out.astype(BF).reshape(C, rows, cut)
        each(C, lambda d: share_p(j, lax.rem(ch + d, C), ch, ch).start())

    def finish_mix():
        r.gm_in[ch] = r.gmp[pl.ds(pl.multiple_of(ch * rows, rows), rows), :]
        each(C, lambda d: share_mix(lax.rem(ch + d, C), ch, lax.rem(ch + d, C)).wait_recv())
        mix = r.gm_in[0].astype(F32)
        for q in range(1, C):
            mix = mix + r.gm_in[q].astype(F32)
        r.gsm[me, mine, 0:rows, :] = mix.astype(BF)
        own_small()

    for j in range(parts):
        back_project(j)
        forward(1, j)
        if j == 0:
            finish_mix()
    weight_term(me, True)

    def hop(d):
        for p in range(parts):
            forward(d, p)
        if isinstance(d, int) and d == 2:
            cross_small()
        forward_small(d - 1)
        weight_terms(d - 1)

    hop(2)
    if S > 3:
        if S <= 12:
            for d in range(3, S):
                hop(d)
        else:
            lax.fori_loop(3, S, lambda d, c: (hop(d), c)[1], 0)
    forward_small(S - 1)

    mixer_columns = r.xc[:, :, ch].reshape(S * D * rows, r.xc.shape[-1])
    mixer_grads = r.gsm[:, :, 0:rows, :].reshape(S * D * rows, mixed)
    mixer_term = norm * mm(mixer_columns, mixer_grads, 0, 0)
    band = mixer_term.shape[0] // C
    for q in range(C):
        r.m_o[q] = mixer_term[q * band : (q + 1) * band, :].astype(BF)

    def share_m(q, landing, slot):
        return rcopy(r.m_o.at[q], r.m_i.at[landing], r.m_s.at[q], r.m_r.at[slot], chan=q)

    each(C, lambda d: share_m(lax.rem(ch + d, C), ch, ch).start())
    step_total = None
    for k in range(S) if S <= 12 else ():
        for e in range(D):
            x = r.xc[k, e].reshape(length, r.xc.shape[-1])
            term = mm(r.gsm[k, e, rows:, 0:LANES], x, 1, 0)
            step_total = term if step_total is None else step_total + term
    if step_total is None:

        def one(k, carry):
            for e in range(D):
                x = r.xc[k, e].reshape(length, r.xc.shape[-1])
                carry = carry + mm(r.gsm[k, e, rows:, 0:LANES], x, 1, 0)
            return carry

        step_total = lax.fori_loop(0, S, one, jnp.zeros((PAD, r.xc.shape[-1]), F32))
    r.o_dws[...] = (norm * step_total)[:heads, :]

    r.p_i[ch] = r.p_o[ch]
    for j in range(parts):
        each(C, lambda d, j=j: share_p(j, lax.rem(ch + d, C), ch, lax.rem(ch + d, C)).wait_recv())
    weight_terms(S - 1)
    r.m_i[ch] = r.m_o[ch]
    each(C, lambda d: share_m(lax.rem(ch + d, C), ch, lax.rem(ch + d, C)).wait_recv())

    @pl.when(me > 0)
    def _():
        halo().wait_send()

    def settle_chan(d):
        q = lax.rem(ch + d, C)
        share_mix(q, ch, ch).wait_send()
        share_m(q, ch, ch).wait_send()
        for j in range(parts):
            share_p(j, q, ch, ch).wait_send()

    each(C, settle_chan)

    def settle_line(k):
        for e in others():
            for p in range(parts):
                ccopy(p, k, mine, e).wait_send()
        for way, sent in (("up", (k <= me) & (me < S - 1)), ("down", (k >= me) & (me > 0))):

            @pl.when(sent)
            def _(way=way):
                for p in range(parts):
                    zcopy(p, way, k).wait_send()
                for e in [mine] + others():
                    zsmall(way, e, k).wait_send()

    settle_line(0)
    each(S, settle_line)
    for e in others():
        csmall(mine, e).wait_send()


def finish_kernel(parts, dw, mixes, dws, o_ig, o_dw, o_dwm, o_dws, ig, dwm, sems):
    copies = [
        pltpu.make_async_copy(a, b, sems.at[i])
        for i, (a, b) in enumerate(((dw, o_dw), (dws, o_dws), (ig, o_ig), (dwm, o_dwm)))
    ]
    copies[0].start()
    copies[1].start()
    total = parts[0].astype(F32)
    for q in range(1, parts.shape[0]):
        total = total + parts[q].astype(F32)
    ig[...] = total.astype(BF)
    copies[2].start()
    total = mixes[0].astype(F32)
    for q in range(1, mixes.shape[0]):
        total = total + mixes[q].astype(F32)
    dwm[...] = total
    copies[3].start()
    for copy in copies:
        copy.wait()


def body(
    sizes,
    layer_input,
    inner_weight,
    mixer_weight,
    step_weight,
    conv_inner,
    conv_mixer,
    step_bias,
    decay_log,
    skip_gain,
    output_grad,
):
    own = layer_input[0]
    rows, model = own.shape
    chans, seqs, dps = sizes["chan"], sizes["seq"], sizes["dp"]
    groups = dps * seqs
    length = rows * chans
    width = inner_weight.shape[1]
    mixed = mixer_weight.shape[1]
    heads = step_bias.shape[0]
    cols = model // groups
    state_size = mixed // 2
    assert width % PIECES == 0 and chans % 2 == 0 and seqs > 2
    assert length == LANES and heads + conv_inner.shape[0] - 1 <= PAD
    upstream = output_grad[0]
    step_rows = step_weight.T
    bias, rates, skips = (v.reshape(1, heads) for v in (step_bias, decay_log, skip_gain))
    dma = pltpu.SemaphoreType.DMA
    vmem = pl.BlockSpec(memory_space=pltpu.VMEM)
    hbm = pl.BlockSpec(memory_space=pltpu.HBM)
    small = rows + PAD
    band = cols // chans

    def low(*shape):
        return pltpu.VMEM(shape, BF)

    def full(*shape):
        return pltpu.VMEM(shape, F32)

    inputs = dict(
        own=own, w_in=inner_weight, w_mix=mixer_weight, w_step=step_rows, conv_in=conv_inner,
        conv_mix=conv_mixer, bias=bias, log=rates, skip=skips, grad=upstream,
    )
    outputs = dict(
        p_i=jax.ShapeDtypeStruct((chans, rows, model), BF),
        o_dw=jax.ShapeDtypeStruct((cols, width), F32),
        m_i=jax.ShapeDtypeStruct((chans, band, mixed), BF),
        o_dws=jax.ShapeDtypeStruct((heads, cols), F32),
    )
    scratch = {key: pltpu.VMEM(v.shape, v.dtype) for key, v in inputs.items()}
    scratch |= dict(
        wst=low(LANES, model), xg=low(length, model),
        blocks=low(dps, seqs, rows, cols), mid=low(dps, seqs, rows, cols),
        xs=low(seqs, dps, rows, cols), xc=low(seqs, dps, chans, rows, cols),
        wide_in=full(PAD + length, width), wide_mix=full(PAD + length, mixed),
        fh_o=low(PAD, width + mixed), fh_i=low(PAD, width + mixed), vec=full(8, LANES),
        sum_in=full(length, width), sum_mix=full(length, mixed), raw=full(length, LANES),
        cum=full(length, LANES), step_wide=full(length, width), fading=full(length, width),
        grown=full(length, width), pulled=low(length, width), decay=full(width, state_size),
        mix=low(length, mixed), act=full(length, width), stepped=low(length, width),
        state_term=low(width, state_size), back_term=low(width, state_size),
        start=low(width, state_size), end=low(width, state_size),
        scr0=low(width, state_size), scr1=low(width, state_size),
        z=full(length, width), y=full(length, width), score_grad=full(length, length),
        local=full(length, width), slope_in=full(length, width), slope_mix=full(length, mixed),
        steps=low(length, LANES),
        pad_in=full(length + 8, width), pad_mix=full(length + 8, mixed),
        gin=low(seqs, dps, length, width), gsm=low(seqs, dps, small, mixed),
        hal_o=full(8, width + mixed), hal_i=full(8, width + mixed),
        gmp=low(length, mixed), gm_in=low(chans, rows, mixed),
        p_o=low(chans, rows, model), m_o=low(chans, band, mixed),
        load_sem=dma((len(LOADED),)), fh_sem=dma((2,)), hal_sem=dma((2,)),
        near_s=dma((chans,)), near_r=dma((chans,)),
        far_s=dma((chans // 2, chans)), far_r=dma((chans // 2, chans)),
        relay_s=dma((chans // 2, chans)), relay_r=dma((chans // 2, chans)),
        swap_s=dma((dps,)), swap_r=dma((dps,)), cross_s=dma((seqs,)), cross_r=dma((seqs,)),
        gat_s=dma((chans,)), gat_r=dma((chans,)),
        chain_s=dma((2, PIECES)), chain_r=dma((2, PIECES)),
        z_r=dma((chans, seqs)), c_r=dma((chans, dps, seqs)),
        u_s=dma((chans, seqs)), d_s=dma((chans, seqs)), x_s=dma((chans, dps, seqs)),
        c2_r=dma((dps,)), z2_r=dma((dps, seqs)), x2_s=dma((dps,)),
        u2_s=dma((dps, seqs)), d2_s=dma((dps, seqs)),
        gm_s=dma((chans,)), gm_r=dma((chans,)),
        p_s=dma((chans, chans)), p_r=dma((chans, chans)), m_s=dma((chans,)), m_r=dma((chans,)),
    )
    names = [key + "_h" for key in inputs] + list(outputs) + list(scratch)
    parts, inner_grad, mix_parts, step_grad = pl.pallas_call(
        functools.partial(layer_kernel, names, sizes, heads),
        out_shape=tuple(outputs.values()),
        in_specs=[hbm] * len(inputs),
        out_specs=(vmem,) * len(outputs),
        scratch_shapes=list(scratch.values()),
        compiler_params=pltpu.CompilerParams(
            collective_id=0, has_side_effects=True, vmem_limit_bytes=LIMIT
        ),
        name="layer",
    )(*inputs.values())
    input_grad, inner_grad, mixer_grad, step_grad = pl.pallas_call(
        finish_kernel,
        out_shape=(
            jax.ShapeDtypeStruct((rows, model), BF),
            jax.ShapeDtypeStruct((cols, width), F32),
            jax.ShapeDtypeStruct((band, mixed), F32),
            jax.ShapeDtypeStruct((heads, cols), F32),
        ),
        in_specs=[vmem] * 4,
        out_specs=(pl.BlockSpec(memory_space=pl.ANY),) * 4,
        scratch_shapes=[
            pltpu.VMEM((rows, model), BF),
            pltpu.VMEM((band, mixed), F32),
            dma((4,)),
        ],
        compiler_params=pltpu.CompilerParams(vmem_limit_bytes=LIMIT),
        name="finish",
    )(parts, inner_grad, mix_parts, step_grad)
    return input_grad[None], inner_grad, mixer_grad, step_grad.T


def solution(mesh):
    sizes = dict(mesh.shape)
    in_specs = (
        P("dp", ("seq", "chan"), None),
        P(None, "chan"),
        P(),
        P(None, "chan"),
        P(None, "chan"),
        P(),
        P("chan"),
        P("chan"),
        P("chan"),
        P("dp", "seq", "chan"),
    )
    out_specs = (
        P("dp", ("seq", "chan"), None),
        P(("dp", "seq"), "chan"),
        P(("dp", "seq", "chan"), None),
        P(("dp", "seq"), "chan"),
    )
    return jax.shard_map(
        functools.partial(body, sizes),
        mesh=mesh,
        in_specs=in_specs,
        out_specs=out_specs,
        check_vma=False,
    )
```

time: 80 us -> 68.5 us (0.86)
  Pallas kernels: 70.1 us -> 60.1 us
  local copies, waits for them, and re-layouts: 8.7 us -> 7.38 us
    pallas_call x4 -> x1, Pallas kernels: 69.1 us -> 59.1 us  [body(): pl.pallas_call(functools.partial(layer_kernel, names, sizes, heads), out_...]
    unnamed x36 -> x18, local copies, waits for them, and re-layouts: 8.7 us -> 7.38 us
where the time goes in v3:
time: 68.5 us; the launch traced here: 68.2 us
  Pallas kernels  60.1 us (88%)
  local copies, waits for them, and re-layouts  7.38 us (11%)
    pallas_call x1, Pallas kernels, body(): pl.pallas_call(functools.partial(layer_kernel, names, sizes, heads), out_...  59.1 us
    unnamed x18, local copies, waits for them, and re-layouts  7.38 us

profile of v3, /device:TPU:0, one launch (start us, length us, event | category | flops | bytes accessed | tf_op | source)
XLA Modules:
  0.0 68.2 jit_solution(13312025963280801599)
XLA Ops:
  0.6 0.0 copy-start
  0.6 1.3 %copy-done = bf16[2560,256]{1,0:T(8,128)(2,1)S(1)} copy-done((bf16[2560,256]{1,0:T(8,128)(2,1)S(1)}, bf16[2560,256]{1,0:T(8,128)(2,1)}, u32[]{:S(2)}) %copy-start) | copy-done | bytes 1310744
  2.0 0.0 copy-start.1
  2.0 0.9 %copy-done.1 = bf16[1,32,2560]{2,1,0:T(8,128)(2,1)S(1)} copy-done((bf16[1,32,2560]{2,1,0:T(8,128)(2,1)S(1)}, bf16[1,32,2560]{2,1,0:T(8,128)(2,1)}, u32[]{:S(2)}) %copy-start.1) | copy-done | bytes 163864
  2.9 0.0 copy-start.2
  2.9 0.9 %copy-done.2 = bf16[1,128,640]{2,1,0:T(8,128)(2,1)S(1)} copy-done((bf16[1,128,640]{2,1,0:T(8,128)(2,1)S(1)}, bf16[1,128,640]{2,1,0:T(8,128)(2,1)}, u32[]{:S(2)}) %copy-start.2) | copy-done | bytes 163864
  3.8 0.0 copy-start.3
  3.8 0.9 %copy-done.3 = bf16[2560,10]{0,1:T(8,128)(2,1)S(1)} copy-done((bf16[2560,10]{0,1:T(8,128)(2,1)S(1)}, bf16[2560,10]{0,1:T(8,128)(2,1)}, u32[]{:S(2)}) %copy-start.3) | copy-done | bytes 51224
  4.7 0.0 copy-start.4
  4.7 0.7 %copy-done.4 = f32[4,640]{1,0:T(4,128)S(1)} copy-done((f32[4,640]{1,0:T(4,128)S(1)}, f32[4,640]{1,0:T(4,128)}, u32[]{:S(2)}) %copy-start.4) | copy-done | bytes 10264
  5.4 0.0 copy-start.5
  5.4 0.7 %copy-done.5 = f32[4,256]{1,0:T(4,128)S(1)} copy-done((f32[4,256]{1,0:T(4,128)S(1)}, f32[4,256]{1,0:T(4,128)}, u32[]{:S(2)}) %copy-start.5) | copy-done | bytes 4120
  6.1 0.0 copy-start.6
  6.1 0.7 copy-done.6
  6.7 0.0 copy-start.7
  6.7 0.7 copy-done.7
  7.4 0.0 copy-start.8
  7.4 0.7 copy-done.8
  8.0 59.1 %layer.1 = (bf16[4,32,2560]{2,1,0:T(8,128)(2,1)S(1)}, f32[320,640]{1,0:T(8,128)S(1)}, bf16[4,80,256]{2,1,0:T(8,128)(2,1)S(1)}, f32[10,320]{1,0:T(8,128)S(1)}) custom-call(bf16[32,2560]{1,0:T(8,128)(2,1)S(1)} %bitcast.8, bf16[2560,640]{1,0:T(8,128)(2,1)} %refs_1_.1, bf16[2560,256]{1,0:T(8,128)(2,1)S(1)} %copy-done, bf16[10,2560]{1,0:T(8,128)(2,1)S(1)} %bitcast.10, ...), custom_call_target="tpu_custom_call" | custom-call | tf_op jit(solution)/shard_map/layer/pallas_call | solution.py:797
  67.2 1.0 %finish.1 = (bf16[32,2560]{1,0:T(8,128)(2,1)}, f32[320,640]{1,0:T(8,128)}, f32[80,256]{1,0:T(8,128)}, f32[10,320]{1,0:T(8,128)}) custom-call(bf16[4,32,2560]{2,1,0:T(8,128)(2,1)S(1)} %get-tuple-element.12.parts, f32[320,640]{1,0:T(8,128)S(1)} %get-tuple-element.13.dw, bf16[4,80,256]{2,1,0:T(8,128)(2,1)S(1)} %get-tuple-element.14.mixes, ...), custom_call_target="tpu_custom_call" | custom-call | tf_op jit(solution)/shard_map/finish/pallas_call | solution.py:808
Async XLA Ops:
  0.6 1.3 %copy-start = (bf16[2560,256]{1,0:T(8,128)(2,1)S(1)}, bf16[2560,256]{1,0:T(8,128)(2,1)}, u32[]{:S(2)}) copy-start(bf16[2560,256]{1,0:T(8,128)(2,1)} %refs_2_.1) | copy-start | bytes 3932164
  2.0 0.9 %copy-start.1 = (bf16[1,32,2560]{2,1,0:T(8,128)(2,1)S(1)}, bf16[1,32,2560]{2,1,0:T(8,128)(2,1)}, u32[]{:S(2)}) copy-start(bf16[1,32,2560]{2,1,0:T(8,128)(2,1)} %param.10) | copy-start | bytes 491524
  2.9 0.9 %copy-start.2 = (bf16[1,128,640]{2,1,0:T(8,128)(2,1)S(1)}, bf16[1,128,640]{2,1,0:T(8,128)(2,1)}, u32[]{:S(2)}) copy-start(bf16[1,128,640]{2,1,0:T(8,128)(2,1)} %param.19) | copy-start | bytes 491524
  3.8 0.9 %copy-start.3 = (bf16[2560,10]{0,1:T(8,128)(2,1)S(1)}, bf16[2560,10]{0,1:T(8,128)(2,1)}, u32[]{:S(2)}) copy-start(bf16[2560,10]{0,1:T(8,128)(2,1)} %param.13) | copy-start | bytes 153604
  4.7 0.7 %copy-start.4 = (f32[4,640]{1,0:T(4,128)S(1)}, f32[4,640]{1,0:T(4,128)}, u32[]{:S(2)}) copy-start(f32[4,640]{1,0:T(4,128)} %refs_4_.1) | copy-start | bytes 30724
  5.4 0.7 %copy-start.5 = (f32[4,256]{1,0:T(4,128)S(1)}, f32[4,256]{1,0:T(4,128)}, u32[]{:S(2)}) copy-start(f32[4,256]{1,0:T(4,128)} %refs_5_.1) | copy-start | bytes 12292
  6.1 0.7 copy-start.6
  6.7 0.7 copy-start.7
  7.4 0.7 copy-start.8

commit v4 on v3

--- a/solution.py
+++ b/solution.py
@@ -804,7 +804,7 @@
             collective_id=0, has_side_effects=True, vmem_limit_bytes=LIMIT
         ),
         name="layer",
-    )(*inputs.values())
+    )(*(pltpu.with_memory_space_constraint(v, pltpu.HBM) for v in inputs.values()))
     input_grad, inner_grad, mixer_grad, step_grad = pl.pallas_call(
         finish_kernel,
         out_shape=(

time: 68.5 us -> 61 us (0.89)
  local copies, waits for them, and re-layouts: 7.38 us -> 0 us
    unnamed x18 -> x0, local copies, waits for them, and re-layouts: 7.38 us -> none
where the time goes in v4:
time: 61 us; the launch traced here: 60.9 us
  Pallas kernels  60.2 us (99%)
  between operations  0.64 us (1%)
    pallas_call x1, Pallas kernels, body(): pl.pallas_call(functools.partial(layer_kernel, names, sizes, heads), out_...  59.2 us

profile of v4, /device:TPU:0, one launch (start us, length us, event | category | flops | bytes accessed | tf_op | source)
XLA Modules:
  0.0 60.9 jit_solution(16726551926078456162)
XLA Ops:
  0.6 59.2 %layer.1 = (bf16[4,32,2560]{2,1,0:T(8,128)(2,1)S(1)}, f32[320,640]{1,0:T(8,128)S(1)}, bf16[4,80,256]{2,1,0:T(8,128)(2,1)S(1)}, f32[10,320]{1,0:T(8,128)S(1)}) custom-call(bf16[32,2560]{1,0:T(8,128)(2,1)} %bitcast.8, bf16[2560,640]{1,0:T(8,128)(2,1)} %refs_1_.1, bf16[2560,256]{1,0:T(8,128)(2,1)} %refs_2_.1, bf16[10,2560]{1,0:T(8,128)(2,1)} %bitcast.10, ...), custom_call_target="tpu_custom_call" | custom-call | tf_op jit(solution)/shard_map/layer/pallas_call | solution.py:797
  59.8 1.0 %finish.1 = (bf16[32,2560]{1,0:T(8,128)(2,1)}, f32[320,640]{1,0:T(8,128)}, f32[80,256]{1,0:T(8,128)}, f32[10,320]{1,0:T(8,128)}) custom-call(bf16[4,32,2560]{2,1,0:T(8,128)(2,1)S(1)} %get-tuple-element.12.parts, f32[320,640]{1,0:T(8,128)S(1)} %get-tuple-element.13.dw, bf16[4,80,256]{2,1,0:T(8,128)(2,1)S(1)} %get-tuple-element.14.mixes, ...), custom_call_target="tpu_custom_call" | custom-call | tf_op jit(solution)/shard_map/finish/pallas_call | solution.py:808

commit v5 on v4

--- a/solution.py
+++ b/solution.py
@@ -110,6 +110,14 @@
     D, S, C = sizes["dp"], sizes["seq"], sizes["chan"]
     barrier = pltpu.get_barrier_semaphore()
     total = greet_all(barrier, "dp", D) + greet_all(barrier, "seq", S) + greet_all(barrier, "chan", C)
+    after = lax.rem(place[1] + 1, S)
+
+    @pl.when(place[2] == C - 1)
+    def _():
+        for c in range(C):
+            signal_to(barrier, {"seq": after, "chan": jnp.int32(c)})
+
+    total += 1
     loads = {
         key: pltpu.make_async_copy(getattr(r, key + "_h"), getattr(r, key), r.load_sem.at[i])
         for i, key in enumerate(LOADED)
@@ -433,24 +441,42 @@
     model = r.w_in.shape[0]
     rows = length // C
     parts = C
+    mixes_low = r.pad_mix[0:length, :].astype(BF)
+    r.am[0:length, :] = mixes_low
+    r.am[length:, :] = jnp.zeros((PAD, mixed), BF)
+
+    def share_mix(q, landing, slot):
+        some = r.am.at[pl.ds(pl.multiple_of(q * rows, rows), rows + PAD)]
+        return rcopy(some, r.gm_in.at[landing], r.gm_s.at[q], r.gm_r.at[slot], chan=q)
+
+    def mix_tail(slot):
+        return rcopy(
+            r.am.at[pl.ds(0, PAD)], r.mt_in.at[slot], r.mt_s.at[0], r.mt_r.at[slot],
+            seq=lax.rem(me + S - 1, S), chan=jnp.int32(C - 1),
+        )
+
+    each(C, lambda d: share_mix(lax.rem(ch + d, C), ch, ch).start())
+
+    @pl.when(me > 0)
+    def _():
+        mix_tail(ch).start()
+
     r.hal_o[:, :width] = r.pad_in[0:8, :]
     r.hal_o[:, width:] = r.pad_mix[0:8, :]
+
+    def halo():
+        return rcopy(r.hal_o, r.hal_i, r.hal_sem.at[0], r.hal_sem.at[1], seq=lax.rem(me + S - 1, S))
+
+    @pl.when(me > 0)
+    def _():
+        halo().start()
+
     r.pad_in[length:, :] = jnp.zeros((8, width), F32)
     r.pad_mix[length:, :] = jnp.zeros((8, mixed), F32)
     last = length - rows
-    r.gin[me, mine, 0:last, :] = spread_back(r.pad_in, r.conv_in, 0, last)
-    r.gmp[0:last, :] = spread_back(r.pad_mix, r.conv_mix, 0, last)
-    r.gsm[me, mine, rows:, 0:LANES] = r.steps[...].astype(F32).T[0:PAD, :].astype(BF)
 
     def others():
         return [lax.rem(mine + e, D) for e in range(1, D)]
-
-    def halo():
-        return rcopy(r.hal_o, r.hal_i, r.hal_sem.at[0], r.hal_sem.at[1], seq=lax.rem(me + S - 1, S))
-
-    @pl.when(me > 0)
-    def _():
-        halo().start()
 
     def part(p, e, k):
         return r.gin.at[k, e, pl.ds(p * rows, rows)]
@@ -463,10 +489,8 @@
     def ccopy(p, k, e, to):
         return rcopy(part(p, e, k), part(p, e, k), r.x_s.at[p, to, k], r.c_r.at[p, e, k], dp=to)
 
-    def zsmall(way, e, k):
-        to = lax.rem(me + (1 if way == "up" else S - 1), S)
-        send = (r.u2_s if way == "up" else r.d2_s).at[e, k]
-        return rcopy(r.gsm.at[k, e], r.gsm.at[k, e], send, r.z2_r.at[e, k], seq=to)
+    def small_to(e, k, q):
+        return rcopy(r.gsm.at[k, e], r.gsm.at[k, e], r.z2_s.at[e, q], r.z2_r.at[e, k], seq=q)
 
     def csmall(e, to):
         return rcopy(r.gsm.at[me, e], r.gsm.at[me, e], r.x2_s.at[to], r.c2_r.at[e], dp=to)
@@ -504,30 +528,13 @@
                 for e in others():
                     ccopy(p, k, mine, e).start()
 
-    def own_small():
-        for e in others():
-            csmall(mine, e).start()
-        onward(lambda way, k: zsmall(way, mine, k), me)
+    def send_small(e):
+        each(S, lambda d: small_to(e, me, lax.rem(me + d, S)).start())
 
     def cross_small():
         for e in others():
             csmall(e, e).wait_recv()
-            onward(lambda way, k, e=e: zsmall(way, e, k), me)
-
-    def forward_small(d):
-        for way, k, there, more in (
-            ("up", me - d, me >= d, me < S - 1),
-            ("down", me + d, me + d < S, me > 0),
-        ):
-            for e in [mine] + others():
-
-                @pl.when(there)
-                def _(way=way, k=k, e=e):
-                    zsmall(way, e, k).wait_recv()
-
-                @pl.when(there & more)
-                def _(way=way, k=k, e=e):
-                    zsmall(way, e, k).start()
+            send_small(e)
 
     norm = 1.0 / math.sqrt(D * S * length)
 
@@ -551,7 +558,13 @@
                 weight_term(k)
 
     for p in range(parts - 1):
+        piece = slice(p * rows, (p + 1) * rows)
+        r.gin[me, mine, piece, :] = spread_back(r.pad_in, r.conv_in, p * rows, rows)
         own_part(p)
+    r.gmp[0:last, :] = spread_back(r.pad_mix, r.conv_mix, 0, last)
+    r.gsm[me, mine, rows:, 0:LANES] = r.steps[...].astype(F32).T[0:PAD, :].astype(BF)
+    own_rows = pl.ds(pl.multiple_of(ch * rows, rows), rows + PAD)
+    r.gm_in[ch] = r.am[own_rows, :]
 
     @pl.when(me < S - 1)
     def _():
@@ -560,13 +573,27 @@
         r.pad_mix[length:, :] = r.hal_i[:, width:]
 
     r.gin[me, mine, last:, :] = spread_back(r.pad_in, r.conv_in, last, rows)
+    own_part(parts - 1)
     r.gmp[last:, :] = spread_back(r.pad_mix, r.conv_mix, last, rows)
-    own_part(parts - 1)
-
-    def share_mix(q, landing, slot):
-        return rcopy(r.gmp.at[pl.ds(q * rows, rows)], r.gm_in.at[landing], r.gm_s.at[q], r.gm_r.at[slot], chan=q)
-
-    each(C, lambda d: share_mix(lax.rem(ch + d, C), ch, ch).start())
+    each(C, lambda d: share_mix(lax.rem(ch + d, C), ch, lax.rem(ch + d, C)).wait_recv())
+    mix = r.gm_in[0].astype(F32)
+    for q in range(1, C):
+        mix = mix + r.gm_in[q].astype(F32)
+    r.gmt[...] = mix
+
+    @pl.when((me < S - 1) & (ch == C - 1))
+    def _():
+        for q in range(C):
+            mix_tail(q).wait_recv()
+        tail = r.mt_in[0].astype(F32)
+        for q in range(1, C):
+            tail = tail + r.mt_in[q].astype(F32)
+        r.gmt[rows:, :] = tail
+
+    r.gsm[me, mine, 0:rows, :] = spread_back(r.gmt, r.conv_mix, 0, rows)
+    for e in others():
+        csmall(mine, e).start()
+    send_small(mine)
     cut = model // parts
 
     def share_p(j, q, landing, slot):
@@ -586,38 +613,20 @@
         r.p_o[:, :, piece] = out.astype(BF).reshape(C, rows, cut)
         each(C, lambda d: share_p(j, lax.rem(ch + d, C), ch, ch).start())
 
-    def finish_mix():
-        r.gm_in[ch] = r.gmp[pl.ds(pl.multiple_of(ch * rows, rows), rows), :]
-        each(C, lambda d: share_mix(lax.rem(ch + d, C), ch, lax.rem(ch + d, C)).wait_recv())
-        mix = r.gm_in[0].astype(F32)
-        for q in range(1, C):
-            mix = mix + r.gm_in[q].astype(F32)
-        r.gsm[me, mine, 0:rows, :] = mix.astype(BF)
-        own_small()
-
     for j in range(parts):
+        if j == parts - 1:
+            cross_small()
         back_project(j)
         forward(1, j)
-        if j == 0:
-            finish_mix()
     weight_term(me, True)
 
     def hop(d):
         for p in range(parts):
             forward(d, p)
-        if isinstance(d, int) and d == 2:
-            cross_small()
-        forward_small(d - 1)
-        weight_terms(d - 1)
 
     hop(2)
-    if S > 3:
-        if S <= 12:
-            for d in range(3, S):
-                hop(d)
-        else:
-            lax.fori_loop(3, S, lambda d, c: (hop(d), c)[1], 0)
-    forward_small(S - 1)
+    for e in [mine] + others():
+        each(S, lambda d, e=e: small_to(e, lax.rem(me + d, S), lax.rem(me + d, S)).wait_recv())
 
     mixer_columns = r.xc[:, :, ch].reshape(S * D * rows, r.xc.shape[-1])
     mixer_grads = r.gsm[:, :, 0:rows, :].reshape(S * D * rows, mixed)
@@ -647,16 +656,22 @@
         step_total = lax.fori_loop(0, S, one, jnp.zeros((PAD, r.xc.shape[-1]), F32))
     r.o_dws[...] = (norm * step_total)[:heads, :]
 
+    if S <= 12:
+        for d in range(3, S):
+            hop(d)
+    else:
+        lax.fori_loop(3, S, lambda d, c: (hop(d), c)[1], 0)
     r.p_i[ch] = r.p_o[ch]
+    r.m_i[ch] = r.m_o[ch]
     for j in range(parts):
         each(C, lambda d, j=j: share_p(j, lax.rem(ch + d, C), ch, lax.rem(ch + d, C)).wait_recv())
-    weight_terms(S - 1)
-    r.m_i[ch] = r.m_o[ch]
+    each(S, weight_terms)
     each(C, lambda d: share_m(lax.rem(ch + d, C), ch, lax.rem(ch + d, C)).wait_recv())
 
     @pl.when(me > 0)
     def _():
         halo().wait_send()
+        mix_tail(ch).wait_send()
 
     def settle_chan(d):
         q = lax.rem(ch + d, C)
@@ -677,13 +692,13 @@
             def _(way=way):
                 for p in range(parts):
                     zcopy(p, way, k).wait_send()
-                for e in [mine] + others():
-                    zsmall(way, e, k).wait_send()
 
     settle_line(0)
     each(S, settle_line)
     for e in others():
         csmall(mine, e).wait_send()
+    for e in [mine] + others():
+        each(S, lambda d, e=e: small_to(e, me, lax.rem(me + d, S)).wait_send())
 
 
 def finish_kernel(parts, dw, mixes, dws, o_ig, o_dw, o_dwm, o_dws, ig, dwm, sems):
@@ -777,7 +792,8 @@
         pad_in=full(length + 8, width), pad_mix=full(length + 8, mixed),
         gin=low(seqs, dps, length, width), gsm=low(seqs, dps, small, mixed),
         hal_o=full(8, width + mixed), hal_i=full(8, width + mixed),
-        gmp=low(length, mixed), gm_in=low(chans, rows, mixed),
+        gmp=low(length, mixed), gm_in=low(chans, small, mixed), gmt=full(small, mixed),
+        am=low(length + PAD, mixed), mt_in=low(chans, PAD, mixed),
         p_o=low(chans, rows, model), m_o=low(chans, band, mixed),
         load_sem=dma((len(LOADED),)), fh_sem=dma((2,)), hal_sem=dma((2,)),
         near_s=dma((chans,)), near_r=dma((chans,)),
@@ -789,7 +805,7 @@
         z_r=dma((chans, seqs)), c_r=dma((chans, dps, seqs)),
         u_s=dma((chans, seqs)), d_s=dma((chans, seqs)), x_s=dma((chans, dps, seqs)),
         c2_r=dma((dps,)), z2_r=dma((dps, seqs)), x2_s=dma((dps,)),
-        u2_s=dma((dps, seqs)), d2_s=dma((dps, seqs)),
+        z2_s=dma((dps, seqs)), mt_s=dma((1,)), mt_r=dma((chans,)),
         gm_s=dma((chans,)), gm_r=dma((chans,)),
         p_s=dma((chans, chans)), p_r=dma((chans, chans)), m_s=dma((chans,)), m_r=dma((chans,)),
     )

time: 61 us -> 56.3 us (0.923)
  Pallas kernels: 60.2 us -> 55.5 us
    pallas_call x1, Pallas kernels: 59.2 us -> 54.5 us  [body(): pl.pallas_call(functools.partial(layer_kernel, names, sizes, heads), out_...]
where the time goes in v5:
time: 56.3 us; the launch traced here: 56.1 us
  Pallas kernels  55.5 us (99%)
  between operations  0.64 us (1%)
    pallas_call x1, Pallas kernels, body(): pl.pallas_call(functools.partial(layer_kernel, names, sizes, heads), out_...  54.5 us

profile of v5, /device:TPU:0, one launch (start us, length us, event | category | flops | bytes accessed | tf_op | source)
XLA Modules:
  0.0 56.1 jit_solution(14531674247521499865)
XLA Ops:
  0.6 54.5 %layer.1 = (bf16[4,32,2560]{2,1,0:T(8,128)(2,1)S(1)}, f32[320,640]{1,0:T(8,128)S(1)}, bf16[4,80,256]{2,1,0:T(8,128)(2,1)S(1)}, f32[10,320]{1,0:T(8,128)S(1)}) custom-call(bf16[32,2560]{1,0:T(8,128)(2,1)} %bitcast.8, bf16[2560,640]{1,0:T(8,128)(2,1)} %refs_1_.1, bf16[2560,256]{1,0:T(8,128)(2,1)} %refs_2_.1, bf16[10,2560]{1,0:T(8,128)(2,1)} %bitcast.10, ...), custom_call_target="tpu_custom_call" | custom-call | tf_op jit(solution)/shard_map/layer/pallas_call | solution.py:813
  55.1 1.0 %finish.1 = (bf16[32,2560]{1,0:T(8,128)(2,1)}, f32[320,640]{1,0:T(8,128)}, f32[80,256]{1,0:T(8,128)}, f32[10,320]{1,0:T(8,128)}) custom-call(bf16[4,32,2560]{2,1,0:T(8,128)(2,1)S(1)} %get-tuple-element.12.parts, f32[320,640]{1,0:T(8,128)S(1)} %get-tuple-element.13.dw, bf16[4,80,256]{2,1,0:T(8,128)(2,1)S(1)} %get-tuple-element.14.mixes, ...), custom_call_target="tpu_custom_call" | custom-call | tf_op jit(solution)/shard_map/finish/pallas_call | solution.py:824

commit v6 on v5

--- a/solution.py
+++ b/solution.py
@@ -95,11 +95,11 @@
     return total
 
 
-def spread_back(pad, kernel, first, count):
+def spread_back(pad, kernel, first, count, cols=slice(None)):
     taps = kernel.shape[0]
     total = None
     for k in range(taps):
-        term = kernel[k : k + 1, :] * pad[pl.ds(first + taps - 1 - k, count), :]
+        term = kernel[k : k + 1, cols] * pad[pl.ds(first + taps - 1 - k, count), cols]
         total = term if total is None else total + term
     return total.astype(BF)
 
@@ -117,16 +117,18 @@
         for c in range(C):
             signal_to(barrier, {"seq": after, "chan": jnp.int32(c)})
 
-    total += 1
+    total += 1 + (D - 1) * (S - 1)
+    for e in range(1, D):
+        far = lax.rem(place[0] + e, D)
+        each(S, lambda d, far=far: signal_to(barrier, {"dp": far, "seq": lax.rem(place[1] + d, S)}))
     loads = {
         key: pltpu.make_async_copy(getattr(r, key + "_h"), getattr(r, key), r.load_sem.at[i])
         for i, key in enumerate(LOADED)
     }
     for copy in loads.values():
         copy.start()
-    front(r, sizes, place, heads, loads, barrier, total)
-    scan_back(r, sizes, place, heads)
-    back(r, sizes, place, heads)
+    crossed = front(r, sizes, place, heads, loads, barrier, total)
+    rear(r, sizes, place, heads, crossed)
 
 
 def front(r, sizes, place, heads, loads, barrier, total):
@@ -217,7 +219,7 @@
         if p + 1 < pieces:
             pass_on(p + 1)
         project(p)
-        if p == pieces // 2:
+        if p == 0:
             each(D, lambda d: swap(lax.rem(mine + d, D), mine, lax.rem(mine + d, D)).wait_recv())
             each(S, lambda d: cross(lax.rem(me + d, S), me, me).start())
             r.xs[me] = r.mid[:, me]
@@ -287,27 +289,35 @@
         q = lax.rem(me + d, S)
         cross(q, me, q).wait()
 
-    each(S, settle)
-
-
-def scan_back(r, sizes, place, heads):
-    S, C = sizes["seq"], sizes["chan"]
+    return lambda: each(S, settle)
+
+
+def rear(r, sizes, place, heads, crossed):
+    D, S, C = sizes["dp"], sizes["seq"], sizes["chan"]
     mine, me, ch = place
     length, width = r.sum_in.shape
-    half = r.sum_mix.shape[1] // 2
+    mixed = r.sum_mix.shape[1]
+    half = mixed // 2
+    model = r.w_in.shape[0]
+    rows = length // C
     pieces, lag = PIECES, PIECES // 2
     size = width // pieces
+    strips = width // LANES
+    per = pieces // strips
+    parts = C
+    cut = model // parts
     terms, outs, scratch = (r.state_term, r.back_term), (r.start, r.end), (r.scr0, r.scr1)
     spots = (me, S - 1 - me)
+    above, below = lax.rem(me + 1, S), lax.rem(me + S - 1, S)
+    others = [lax.rem(mine + e, D) for e in range(1, D)]
 
     def carry(way, piece, first=False):
         part = pl.ds(pl.multiple_of(piece * size, size), size)
-        to = lax.rem(me + 1, S) if way == 0 else lax.rem(me + S - 1, S)
         source = terms[way] if first else scratch[way]
         sems = r.chain_s.at[way, piece], r.chain_r.at[way, piece]
-        return rcopy(source.at[part], outs[way].at[part], *sems, seq=to)
-
-    for way in (0, 1):
+        return rcopy(source.at[part], outs[way].at[part], *sems, seq=above if way == 0 else below)
+
+    for way in (1, 0):
 
         @pl.when(spots[way] == 0)
         def _(way=way):
@@ -316,7 +326,7 @@
             outs[way][...] = jnp.zeros(outs[way].shape, BF)
 
     def beat(t):
-        for way in (0, 1):
+        for way in (1, 0):
             spot = spots[way]
             piece = t - lag * (spot - 1)
 
@@ -331,9 +341,6 @@
 
     def gather(q, landing, slot):
         return rcopy(r.xs, r.xc.at[:, :, landing], r.gat_s.at[q], r.gat_r.at[slot], chan=q)
-
-    each(C, lambda d: gather(lax.rem(ch + d, C), ch, ch).start())
-    r.xc[:, :, ch] = r.xs[...]
 
     spread = head_mask(width, True)
     cumulative = r.cum[...]
@@ -344,9 +351,14 @@
     lower = causal.astype(F32)
     into, out_of = r.mix[:, :half], r.mix[:, half:]
     scores = mm(out_of, into, 1, 1)
-    act = r.act[...]
-    stepped_low = (act * r.step_wide[...]).astype(BF)
-    r.stepped[...] = stepped_low
+    r.stepped[...] = (r.act[...] * r.step_wide[...]).astype(BF)
+    inner = r.sum_in[...]
+    gate = jax.nn.sigmoid(inner)
+    r.slope_in[...] = gate * (1.0 + inner * (1.0 - gate))
+    skip_wide = exact(jnp.broadcast_to(r.vec[2:3, :], (8, LANES)), spread)
+    r.skips[...] = skip_wide
+    r.pad_in[length:, :] = jnp.zeros((8, width), F32)
+    r.pad_mix[length:, :] = jnp.zeros((8, mixed), F32)
 
     def head(h):
         cols = slice(h * HDIM, (h + 1) * HDIM)
@@ -359,56 +371,148 @@
         r.z[:, cols] = mm(weights, grad_h, 0, 0)
         r.y[:, cols] = mm(weights, step_h, 1, 0)
 
+    def strip(j):
+        return slice(j * LANES, (j + 1) * LANES)
+
+    def halo(j):
+        return rcopy(r.hal_o.at[j], r.hal_i.at[j], r.hal_s.at[j], r.hal_r.at[j], seq=below)
+
+    def strip_sum(j):
+        cols = strip(j)
+
+        @pl.when(spots[1] == S - 1)
+        def _():
+            for piece in range(j * per, (j + 1) * per):
+                carry(1, piece).wait_recv()
+
+        ending = r.fading[:, cols] * mm(into, r.end[cols, :], 1, 1)
+        r.ending[:, cols] = ending
+        direct = r.skips[0:1, cols] * r.grad[:, cols].astype(F32)
+        total = (r.step_wide[:, cols] * (r.z[:, cols] + ending) + direct) * r.slope_in[:, cols]
+        r.pad_in[0:length, cols] = total
+        r.hal_o[j] = total[0:8, :]
+
+        @pl.when(me > 0)
+        def _():
+            halo(j).start()
+
+    def part(p, e, k):
+        return r.gin.at[k, e, :, pl.ds(p * LANES, LANES)]
+
+    def zcopy(p, way, k):
+        send = (r.u_s if way == "up" else r.d_s).at[p, k]
+        here = part(p, mine, k)
+        return rcopy(here, here, send, r.z_r.at[p, k], seq=above if way == "up" else below)
+
+    def ccopy(p, k, e, to):
+        return rcopy(part(p, e, k), part(p, e, k), r.x_s.at[p, to, k], r.c_r.at[p, e, k], dp=to)
+
+    def strip_out(j):
+        cols = strip(j)
+
+        @pl.when(me < S - 1)
+        def _():
+            halo(j).wait_recv()
+            r.pad_in[length:, cols] = r.hal_i[j]
+
+        r.gin[me, mine, :, cols] = spread_back(r.pad_in, r.conv_in, 0, length, cols)
+        for e in others:
+            ccopy(j, me, mine, e).start()
+
+    def strip_along(j):
+        @pl.when(me < S - 1)
+        def _():
+            zcopy(j, "up", me).start()
+
+        @pl.when(me > 0)
+        def _():
+            zcopy(j, "down", me).start()
+
     beats = pieces + lag * max(S - 3, 0)
     early = heads // 2
     for h in range(early):
         head(h)
+    near = spots[1] <= 1
+    crossed()
+    each(C, lambda d: gather(lax.rem(ch + d, C), ch, ch).start())
+    r.xc[:, :, ch] = r.xs[...]
     if beats <= 24:
-        for t in range(beats):
+        sums = {per * j + per - 1: j for j in range(strips)}
+        late = {lag + t: j for t, j in sums.items()}
+        for t in range(max(beats, heads - early)):
             beat(t)
             if early + t < heads:
                 head(early + t)
+            if t in sums:
+                pl.when(near)(functools.partial(strip_sum, sums[t]))
+            if t in late:
+                pl.when(near)(functools.partial(strip_out, late[t]))
+                pl.when(spots[1] == 2)(functools.partial(strip_sum, late[t]))
+        for j in range(strips):
+            pl.when(spots[1] > 2)(functools.partial(strip_sum, j))
+            pl.when(spots[1] > 1)(functools.partial(strip_out, j))
+            strip_along(j)
     else:
         for h in range(early, heads):
             head(h)
         lax.fori_loop(0, beats, lambda t, c: (beat(t), c)[1], 0)
+        for j in range(strips):
+            strip_sum(j)
+        for j in range(strips):
+            strip_out(j)
+            strip_along(j)
+
+    @pl.when(spots[0] == S - 1)
+    def _():
+        for piece in range(pieces):
+            carry(0, piece).wait_recv()
+
+    start, end = r.start[...], r.end[...]
+    score_grad = r.score_grad[...]
+    mixer = r.sum_mix[...]
+    gate = jax.nn.sigmoid(mixer)
+    mixer_slope = gate * (1.0 + mixer * (1.0 - gate))
+    faded = (r.fading[...] * r.stepped[...].astype(F32)).astype(BF)
+    into_grad = mm(score_grad, out_of, 0, 0) + mm(faded, end, 1, 0)
+    out_grad = mm(score_grad, into, 1, 0) + mm(r.pulled[...], start, 1, 0)
+    r.pad_mix[0:length, :half] = into_grad * mixer_slope[:, :half]
+    r.pad_mix[0:length, half:] = out_grad * mixer_slope[:, half:]
+    r.am[0:length, :] = r.pad_mix[0:length, :].astype(BF)
+    r.am[length:, :] = jnp.zeros((PAD, mixed), BF)
+    r.halm_o[...] = r.pad_mix[0:8, :]
+
+    def share_mix(q, landing, slot):
+        some = r.am.at[pl.ds(pl.multiple_of(q * rows, rows), rows + PAD)]
+        return rcopy(some, r.gm_in.at[landing], r.gm_s.at[q], r.gm_r.at[slot], chan=q)
+
+    def mix_tail(slot):
+        return rcopy(
+            r.am.at[pl.ds(0, PAD)], r.mt_in.at[slot], r.mt_s.at[0], r.mt_r.at[slot],
+            seq=below, chan=jnp.int32(C - 1),
+        )
+
+    def mix_halo():
+        return rcopy(r.halm_o, r.halm_i, r.halm_s.at[0], r.halm_s.at[1], seq=below)
+
+    each(C, lambda d: share_mix(lax.rem(ch + d, C), ch, ch).start())
+
+    @pl.when(me > 0)
+    def _():
+        mix_tail(ch).start()
+        mix_halo().start()
+
+    r.gm_in[ch] = r.am[pl.ds(pl.multiple_of(ch * rows, rows), rows + PAD), :]
+    r.gmp[...] = spread_back(r.pad_mix, r.conv_mix, 0, length)
 
     upstream = r.grad[...].astype(F32)
     stepped = r.stepped[...].astype(F32)
-    step_wide = r.step_wide[...]
-    skip_wide = exact(jnp.broadcast_to(r.vec[2:3, :], (8, LANES)), spread)[0:1, :]
-    inner, mixer = r.sum_in[...], r.sum_mix[...]
-    inner_gate, mixer_gate = jax.nn.sigmoid(inner), jax.nn.sigmoid(mixer)
-    inner_slope = inner_gate * (1.0 + inner * (1.0 - inner_gate))
-    mixer_slope = mixer_gate * (1.0 + mixer * (1.0 - mixer_gate))
+    ending = r.ending[...]
+    carried = r.grown[...] * mm(out_of, start, 1, 1)
     to_heads = functools.partial(exact, b=spread, da=1, db=1)
     z = r.z[...]
-    r.slope_in[...] = inner_slope
-    r.slope_mix[...] = mixer_slope
-    r.local[...] = (step_wide * z + skip_wide * upstream) * inner_slope
-    local_step = to_heads(r.act[...] * z)
-    local_sum = to_heads(upstream * r.y[...] - stepped * z)
-    score_grad = r.score_grad[...]
-    out_local = mm(score_grad, into, 1, 0)
-    into_local = mm(score_grad, out_of, 0, 0)
-    faded = (r.fading[...] * stepped).astype(BF)
-
-    for way in (0, 1):
-
-        @pl.when(spots[way] == S - 1)
-        def _(way=way):
-            for piece in range(pieces):
-                carry(way, piece).wait_recv()
-
-    start, end = r.start[...], r.end[...]
-    carried = r.grown[...] * mm(out_of, start, 1, 1)
-    ending = r.fading[...] * mm(into, end, 1, 1)
-    r.pad_in[0:length, :] = r.local[...] + (r.step_wide[...] * ending) * r.slope_in[...]
-    r.pad_mix[0:length, :half] = (into_local + mm(faded, end, 1, 0)) * r.slope_mix[:, :half]
-    r.pad_mix[0:length, half:] = (out_local + mm(r.pulled[...], start, 1, 0)) * r.slope_mix[:, half:]
-    step_grad = local_step + to_heads(r.act[...] * ending)
+    step_grad = to_heads(r.act[...] * (z + ending))
     tail_term = to_heads(stepped * ending)
-    sum_grad = local_sum + to_heads(upstream * carried) - tail_term
+    sum_grad = to_heads(upstream * (r.y[...] + carried) - stepped * z) - tail_term
     held = jnp.sum(start.astype(F32) * end.astype(F32), axis=1, keepdims=True)
     last = cumulative[length - 1 : length, :]
     overall = jnp.sum(tail_term, axis=0, keepdims=True) + jnp.exp(last) * jnp.sum(
@@ -417,164 +521,10 @@
     decay_grad = exact(lower, sum_grad, 0, 0) + overall
     rate = jnp.exp(r.vec[1:2, :])
     step_grad = (step_grad - rate * decay_grad) * jax.nn.sigmoid(r.raw[...] + r.vec[0:1, :])
-    r.steps[...] = step_grad.astype(BF)
-
-    for way in (0, 1):
-
-        @pl.when(spots[way] < S - 1)
-        def _(way=way):
-            for piece in range(pieces):
-                carry(way, piece).wait_send()
-
-    def settle_gather(d):
-        q = lax.rem(ch + d, C)
-        gather(q, q, q).wait()
-
-    each(C, settle_gather)
-
-
-def back(r, sizes, place, heads):
-    D, S, C = sizes["dp"], sizes["seq"], sizes["chan"]
-    mine, me, ch = place
-    length, width = r.sum_in.shape
-    mixed = r.sum_mix.shape[1]
-    model = r.w_in.shape[0]
-    rows = length // C
-    parts = C
-    mixes_low = r.pad_mix[0:length, :].astype(BF)
-    r.am[0:length, :] = mixes_low
-    r.am[length:, :] = jnp.zeros((PAD, mixed), BF)
-
-    def share_mix(q, landing, slot):
-        some = r.am.at[pl.ds(pl.multiple_of(q * rows, rows), rows + PAD)]
-        return rcopy(some, r.gm_in.at[landing], r.gm_s.at[q], r.gm_r.at[slot], chan=q)
-
-    def mix_tail(slot):
-        return rcopy(
-            r.am.at[pl.ds(0, PAD)], r.mt_in.at[slot], r.mt_s.at[0], r.mt_r.at[slot],
-            seq=lax.rem(me + S - 1, S), chan=jnp.int32(C - 1),
-        )
-
-    each(C, lambda d: share_mix(lax.rem(ch + d, C), ch, ch).start())
-
-    @pl.when(me > 0)
-    def _():
-        mix_tail(ch).start()
-
-    r.hal_o[:, :width] = r.pad_in[0:8, :]
-    r.hal_o[:, width:] = r.pad_mix[0:8, :]
-
-    def halo():
-        return rcopy(r.hal_o, r.hal_i, r.hal_sem.at[0], r.hal_sem.at[1], seq=lax.rem(me + S - 1, S))
-
-    @pl.when(me > 0)
-    def _():
-        halo().start()
-
-    r.pad_in[length:, :] = jnp.zeros((8, width), F32)
-    r.pad_mix[length:, :] = jnp.zeros((8, mixed), F32)
-    last = length - rows
-
-    def others():
-        return [lax.rem(mine + e, D) for e in range(1, D)]
-
-    def part(p, e, k):
-        return r.gin.at[k, e, pl.ds(p * rows, rows)]
-
-    def zcopy(p, way, k):
-        to = lax.rem(me + (1 if way == "up" else S - 1), S)
-        send = (r.u_s if way == "up" else r.d_s).at[p, k]
-        return rcopy(part(p, mine, k), part(p, mine, k), send, r.z_r.at[p, k], seq=to)
-
-    def ccopy(p, k, e, to):
-        return rcopy(part(p, e, k), part(p, e, k), r.x_s.at[p, to, k], r.c_r.at[p, e, k], dp=to)
-
-    def small_to(e, k, q):
-        return rcopy(r.gsm.at[k, e], r.gsm.at[k, e], r.z2_s.at[e, q], r.z2_r.at[e, k], seq=q)
-
-    def csmall(e, to):
-        return rcopy(r.gsm.at[me, e], r.gsm.at[me, e], r.x2_s.at[to], r.c2_r.at[e], dp=to)
-
-    def onward(make, k):
-        @pl.when(me < S - 1)
-        def _():
-            make("up", k).start()
-
-        @pl.when(me > 0)
-        def _():
-            make("down", k).start()
-
-    def own_part(p):
-        onward(functools.partial(zcopy, p), me)
-        for e in others():
-            ccopy(p, me, mine, e).start()
-
-    def forward(d, p):
-        for way, k, there, more in (
-            ("up", me - d, me >= d, me < S - 1),
-            ("down", me + d, me + d < S, me > 0),
-        ):
-
-            @pl.when(there)
-            def _(way=way, k=k):
-                zcopy(p, way, k).wait_recv()
-
-            @pl.when(there & more)
-            def _(way=way, k=k):
-                zcopy(p, way, k).start()
-
-            @pl.when(there)
-            def _(k=k):
-                for e in others():
-                    ccopy(p, k, mine, e).start()
-
-    def send_small(e):
-        each(S, lambda d: small_to(e, me, lax.rem(me + d, S)).start())
-
-    def cross_small():
-        for e in others():
-            csmall(e, e).wait_recv()
-            send_small(e)
-
-    norm = 1.0 / math.sqrt(D * S * length)
-
-    def columns_of(k):
-        block = r.xc[k]
-        return block.reshape(D * length, block.shape[-1])
-
-    def weight_term(k, first=False):
-        for e in others():
-            for p in range(parts):
-                ccopy(p, k, e, e).wait_recv()
-        x = columns_of(k)
-        term = norm * mm(x, r.gin[k].reshape(D * length, width), 0, 0)
-        r.o_dw[...] = term if first else r.o_dw[...] + term
-
-    def weight_terms(d):
-        for k, there in ((me - d, me >= d), (me + d, me + d < S)):
-
-            @pl.when(there)
-            def _(k=k):
-                weight_term(k)
-
-    for p in range(parts - 1):
-        piece = slice(p * rows, (p + 1) * rows)
-        r.gin[me, mine, piece, :] = spread_back(r.pad_in, r.conv_in, p * rows, rows)
-        own_part(p)
-    r.gmp[0:last, :] = spread_back(r.pad_mix, r.conv_mix, 0, last)
-    r.gsm[me, mine, rows:, 0:LANES] = r.steps[...].astype(F32).T[0:PAD, :].astype(BF)
-    own_rows = pl.ds(pl.multiple_of(ch * rows, rows), rows + PAD)
-    r.gm_in[ch] = r.am[own_rows, :]
-
-    @pl.when(me < S - 1)
-    def _():
-        halo().wait_recv()
-        r.pad_in[length:, :] = r.hal_i[:, :width]
-        r.pad_mix[length:, :] = r.hal_i[:, width:]
-
-    r.gin[me, mine, last:, :] = spread_back(r.pad_in, r.conv_in, last, rows)
-    own_part(parts - 1)
-    r.gmp[last:, :] = spread_back(r.pad_mix, r.conv_mix, last, rows)
+    steps = step_grad.astype(BF)
+    r.gsm[me, mine, rows:, 0:LANES] = step_grad.T[0:PAD, :].astype(BF)
+    steps = steps[:, 0:PAD]
+
     each(C, lambda d: share_mix(lax.rem(ch + d, C), ch, lax.rem(ch + d, C)).wait_recv())
     mix = r.gm_in[0].astype(F32)
     for q in range(1, C):
@@ -591,10 +541,40 @@
         r.gmt[rows:, :] = tail
 
     r.gsm[me, mine, 0:rows, :] = spread_back(r.gmt, r.conv_mix, 0, rows)
-    for e in others():
-        csmall(mine, e).start()
-    send_small(mine)
-    cut = model // parts
+
+    def small_to(e, k, to, q):
+        here = r.gsm.at[k, e]
+        return rcopy(here, here, r.z2_s.at[to, q], r.z2_r.at[e, k], dp=to, seq=q)
+
+    def small_all(do):
+        each(S, lambda d: do(mine, lax.rem(me + d, S)))
+        for e in others:
+            do(e, me)
+            each(S, lambda d, e=e: do(e, lax.rem(me + d, S)))
+
+    small_all(lambda e, q: small_to(mine, me, e, q).start())
+
+    def forward(p, way, d):
+        k = me - d if way == "up" else me + d
+        there = (k >= 0) if way == "up" else (k < S)
+        more = (me < S - 1) if way == "up" else (me > 0)
+
+        @pl.when(there)
+        def _():
+            zcopy(p, way, k).wait_recv()
+
+        @pl.when(there & more)
+        def _():
+            zcopy(p, way, k).start()
+
+        @pl.when(there)
+        def _():
+            for e in others:
+                ccopy(p, k, mine, e).start()
+
+    def hop(way, d):
+        for p in range(strips):
+            forward(p, way, d)
 
     def share_p(j, q, landing, slot):
         piece = pl.ds(j * cut, cut)
@@ -604,34 +584,56 @@
 
     grads = r.gin[me, mine]
     mixes = r.gmp[...]
-    steps = r.steps[:, 0:PAD]
-
-    def back_project(j):
+
+    def send_p(j, final):
+        def one(d):
+            q = lax.rem(ch + d, C)
+
+            @pl.when((q == C - 1) if final else (q < C - 1))
+            def _():
+                share_p(j, q, ch, ch).start()
+
+        each(C, one)
+
+    for j in range(parts):
         piece = slice(j * cut, (j + 1) * cut)
         out = mm(grads, r.w_in[piece, :], 1, 1) + mm(mixes, r.w_mix[piece, :], 1, 1)
         out = out + mm(steps, r.wst[0:PAD, piece], 1, 0)
         r.p_o[:, :, piece] = out.astype(BF).reshape(C, rows, cut)
-        each(C, lambda d: share_p(j, lax.rem(ch + d, C), ch, ch).start())
+        r.p_last[:, piece] = out[length - PAD :, :]
+        send_p(j, False)
+        forward(j, "down", 1)
+    for p in range(parts, strips):
+        forward(p, "down", 1)
+
+    @pl.when(me < S - 1)
+    def _():
+        mix_halo().wait_recv()
+        r.pad_mix[length:, :] = r.halm_i[...]
+        final = spread_back(r.pad_mix, r.conv_mix, length - PAD, PAD)
+        change = final.astype(F32) - r.gmp[length - PAD :, :].astype(F32)
+        fixed = r.p_last[...] + mm(change, r.w_mix[...], 1, 1)
+        r.p_o[C - 1, rows - PAD :, :] = fixed.astype(BF)
 
     for j in range(parts):
-        if j == parts - 1:
-            cross_small()
-        back_project(j)
-        forward(1, j)
-    weight_term(me, True)
-
-    def hop(d):
-        for p in range(parts):
-            forward(d, p)
-
-    hop(2)
-    for e in [mine] + others():
-        each(S, lambda d, e=e: small_to(e, lax.rem(me + d, S), lax.rem(me + d, S)).wait_recv())
-
-    mixer_columns = r.xc[:, :, ch].reshape(S * D * rows, r.xc.shape[-1])
+        send_p(j, True)
+    hop("up", 1)
+    hop("down", 2)
+    hop("up", 2)
+    small_all(lambda e, q: small_to(e, q, e, q).wait_recv())
+
+    norm = 1.0 / math.sqrt(D * S * length)
+    columns = r.xc.shape[-1]
+
+    def settle_gather(d):
+        q = lax.rem(ch + d, C)
+        gather(q, q, q).wait()
+
+    each(C, settle_gather)
+    mixer_columns = r.xc[:, :, ch].reshape(S * D * rows, columns)
     mixer_grads = r.gsm[:, :, 0:rows, :].reshape(S * D * rows, mixed)
     mixer_term = norm * mm(mixer_columns, mixer_grads, 0, 0)
-    band = mixer_term.shape[0] // C
+    band = columns // C
     for q in range(C):
         r.m_o[q] = mixer_term[q * band : (q + 1) * band, :].astype(BF)
 
@@ -639,38 +641,59 @@
         return rcopy(r.m_o.at[q], r.m_i.at[landing], r.m_s.at[q], r.m_r.at[slot], chan=q)
 
     each(C, lambda d: share_m(lax.rem(ch + d, C), ch, ch).start())
-    step_total = None
-    for k in range(S) if S <= 12 else ():
-        for e in range(D):
-            x = r.xc[k, e].reshape(length, r.xc.shape[-1])
-            term = mm(r.gsm[k, e, rows:, 0:LANES], x, 1, 0)
-            step_total = term if step_total is None else step_total + term
-    if step_total is None:
-
-        def one(k, carry):
-            for e in range(D):
-                x = r.xc[k, e].reshape(length, r.xc.shape[-1])
-                carry = carry + mm(r.gsm[k, e, rows:, 0:LANES], x, 1, 0)
-            return carry
-
-        step_total = lax.fori_loop(0, S, one, jnp.zeros((PAD, r.xc.shape[-1]), F32))
-    r.o_dws[...] = (norm * step_total)[:heads, :]
-
     if S <= 12:
         for d in range(3, S):
-            hop(d)
+            hop("down", d)
+            hop("up", d)
     else:
-        lax.fori_loop(3, S, lambda d, c: (hop(d), c)[1], 0)
+        lax.fori_loop(3, S, lambda d, c: (hop("down", d), hop("up", d), c)[2], 0)
+
+    def step_term(k, total):
+        for e in range(D):
+            x = r.xc[k, e].reshape(length, columns)
+            total = total + mm(r.gsm[k, e, rows:, 0:LANES], x, 1, 0)
+        return total
+
+    step_total = jnp.zeros((PAD, columns), F32)
+    if S <= 12:
+        for k in range(S):
+            step_total = step_term(k, step_total)
+    else:
+        step_total = lax.fori_loop(0, S, step_term, step_total)
+    r.o_dws[...] = (norm * step_total)[:heads, :]
+
+    def weight_term(k, first=False):
+        for e in others:
+            for p in range(strips):
+                ccopy(p, k, e, e).wait_recv()
+        x = r.xc[k].reshape(D * length, columns)
+        term = norm * mm(x, r.gin[k].reshape(D * length, width), 0, 0)
+        r.o_dw[...] = term if first else r.o_dw[...] + term
+
+    def weight_terms(d):
+        for k, there in ((me + d, me + d < S), (me - d, me >= d)):
+            pl.when(there)(functools.partial(weight_term, k))
+
+    weight_term(me, True)
+    each(S, weight_terms)
     r.p_i[ch] = r.p_o[ch]
     r.m_i[ch] = r.m_o[ch]
     for j in range(parts):
         each(C, lambda d, j=j: share_p(j, lax.rem(ch + d, C), ch, lax.rem(ch + d, C)).wait_recv())
-    each(S, weight_terms)
     each(C, lambda d: share_m(lax.rem(ch + d, C), ch, lax.rem(ch + d, C)).wait_recv())
+
+    for way in (0, 1):
+
+        @pl.when(spots[way] < S - 1)
+        def _(way=way):
+            for piece in range(pieces):
+                carry(way, piece).wait_send()
 
     @pl.when(me > 0)
     def _():
-        halo().wait_send()
+        for j in range(strips):
+            halo(j).wait_send()
+        mix_halo().wait_send()
         mix_tail(ch).wait_send()
 
     def settle_chan(d):
@@ -683,22 +706,19 @@
     each(C, settle_chan)
 
     def settle_line(k):
-        for e in others():
-            for p in range(parts):
+        for e in others:
+            for p in range(strips):
                 ccopy(p, k, mine, e).wait_send()
         for way, sent in (("up", (k <= me) & (me < S - 1)), ("down", (k >= me) & (me > 0))):
 
             @pl.when(sent)
             def _(way=way):
-                for p in range(parts):
+                for p in range(strips):
                     zcopy(p, way, k).wait_send()
 
     settle_line(0)
     each(S, settle_line)
-    for e in others():
-        csmall(mine, e).wait_send()
-    for e in [mine] + others():
-        each(S, lambda d, e=e: small_to(e, me, lax.rem(me + d, S)).wait_send())
+    small_all(lambda e, q: small_to(mine, me, e, q).wait_send())
 
 
 def finish_kernel(parts, dw, mixes, dws, o_ig, o_dw, o_dwm, o_dws, ig, dwm, sems):
@@ -746,6 +766,7 @@
     cols = model // groups
     state_size = mixed // 2
     assert width % PIECES == 0 and chans % 2 == 0 and seqs > 2
+    assert width % LANES == 0 and PIECES % (width // LANES) == 0
     assert length == LANES and heads + conv_inner.shape[0] - 1 <= PAD
     upstream = output_grad[0]
     step_rows = step_weight.T
@@ -754,6 +775,7 @@
     vmem = pl.BlockSpec(memory_space=pltpu.VMEM)
     hbm = pl.BlockSpec(memory_space=pltpu.HBM)
     small = rows + PAD
+    strips = width // LANES
     band = cols // chans
 
     def low(*shape):
@@ -787,24 +809,26 @@
         start=low(width, state_size), end=low(width, state_size),
         scr0=low(width, state_size), scr1=low(width, state_size),
         z=full(length, width), y=full(length, width), score_grad=full(length, length),
-        local=full(length, width), slope_in=full(length, width), slope_mix=full(length, mixed),
-        steps=low(length, LANES),
+        slope_in=full(length, width),
         pad_in=full(length + 8, width), pad_mix=full(length + 8, mixed),
         gin=low(seqs, dps, length, width), gsm=low(seqs, dps, small, mixed),
-        hal_o=full(8, width + mixed), hal_i=full(8, width + mixed),
+        hal_o=full(strips, 8, LANES), hal_i=full(strips, 8, LANES),
+        halm_o=full(8, mixed), halm_i=full(8, mixed), p_last=full(PAD, model),
+        skips=full(8, width), ending=full(length, width),
         gmp=low(length, mixed), gm_in=low(chans, small, mixed), gmt=full(small, mixed),
         am=low(length + PAD, mixed), mt_in=low(chans, PAD, mixed),
         p_o=low(chans, rows, model), m_o=low(chans, band, mixed),
-        load_sem=dma((len(LOADED),)), fh_sem=dma((2,)), hal_sem=dma((2,)),
+        load_sem=dma((len(LOADED),)), fh_sem=dma((2,)), halm_s=dma((2,)),
+        hal_s=dma((strips,)), hal_r=dma((strips,)),
         near_s=dma((chans,)), near_r=dma((chans,)),
         far_s=dma((chans // 2, chans)), far_r=dma((chans // 2, chans)),
         relay_s=dma((chans // 2, chans)), relay_r=dma((chans // 2, chans)),
         swap_s=dma((dps,)), swap_r=dma((dps,)), cross_s=dma((seqs,)), cross_r=dma((seqs,)),
         gat_s=dma((chans,)), gat_r=dma((chans,)),
         chain_s=dma((2, PIECES)), chain_r=dma((2, PIECES)),
-        z_r=dma((chans, seqs)), c_r=dma((chans, dps, seqs)),
-        u_s=dma((chans, seqs)), d_s=dma((chans, seqs)), x_s=dma((chans, dps, seqs)),
-        c2_r=dma((dps,)), z2_r=dma((dps, seqs)), x2_s=dma((dps,)),
+        z_r=dma((strips, seqs)), c_r=dma((strips, dps, seqs)),
+        u_s=dma((strips, seqs)), d_s=dma((strips, seqs)), x_s=dma((strips, dps, seqs)),
+        z2_r=dma((dps, seqs)),
         z2_s=dma((dps, seqs)), mt_s=dma((1,)), mt_r=dma((chans,)),
         gm_s=dma((chans,)), gm_r=dma((chans,)),
         p_s=dma((chans, chans)), p_r=dma((chans, chans)), m_s=dma((chans,)), m_r=dma((chans,)),

time: 56.3 us -> 51.2 us (0.909)
  Pallas kernels: 55.5 us -> 50.4 us
    pallas_call x1, Pallas kernels: 54.5 us -> 49.4 us  [body(): pl.pallas_call(functools.partial(layer_kernel, names, sizes, heads), out_...]
where the time goes in v6:
time: 51.2 us; the launch traced here: 51 us
  Pallas kernels  50.4 us (98%)
  between operations  0.64 us (1%)
    pallas_call x1, Pallas kernels, body(): pl.pallas_call(functools.partial(layer_kernel, names, sizes, heads), out_...  49.4 us

profile of v6, /device:TPU:0, one launch (start us, length us, event | category | flops | bytes accessed | tf_op | source)
XLA Modules:
  0.0 51.0 jit_solution(18073648727874462536)
XLA Ops:
  0.6 49.4 %layer.1 = (bf16[4,32,2560]{2,1,0:T(8,128)(2,1)S(1)}, f32[320,640]{1,0:T(8,128)S(1)}, bf16[4,80,256]{2,1,0:T(8,128)(2,1)S(1)}, f32[10,320]{1,0:T(8,128)S(1)}) custom-call(bf16[32,2560]{1,0:T(8,128)(2,1)} %bitcast.8, bf16[2560,640]{1,0:T(8,128)(2,1)} %refs_1_.1, bf16[2560,256]{1,0:T(8,128)(2,1)} %refs_2_.1, bf16[10,2560]{1,0:T(8,128)(2,1)} %bitcast.10, ...), custom_call_target="tpu_custom_call" | custom-call | tf_op jit(solution)/shard_map/layer/pallas_call | solution.py:837
  50.0 1.0 %finish.1 = (bf16[32,2560]{1,0:T(8,128)(2,1)}, f32[320,640]{1,0:T(8,128)}, f32[80,256]{1,0:T(8,128)}, f32[10,320]{1,0:T(8,128)}) custom-call(bf16[4,32,2560]{2,1,0:T(8,128)(2,1)S(1)} %get-tuple-element.12.parts, f32[320,640]{1,0:T(8,128)S(1)} %get-tuple-element.13.dw, bf16[4,80,256]{2,1,0:T(8,128)(2,1)S(1)} %get-tuple-element.14.mixes, ...), custom_call_target="tpu_custom_call" | custom-call | tf_op jit(solution)/shard_map/finish/pallas_call | solution.py:848

commit v7 on v6

--- a/solution.py
+++ b/solution.py
@@ -399,10 +399,10 @@
     def part(p, e, k):
         return r.gin.at[k, e, :, pl.ds(p * LANES, LANES)]
 
-    def zcopy(p, way, k):
-        send = (r.u_s if way == "up" else r.d_s).at[p, k]
-        here = part(p, mine, k)
-        return rcopy(here, here, send, r.z_r.at[p, k], seq=above if way == "up" else below)
+    def zcopy(p, way, k, e=mine):
+        send = (r.u_s if way == "up" else r.d_s).at[p, e, k]
+        here = part(p, e, k)
+        return rcopy(here, here, send, r.z_r.at[p, e, k], seq=above if way == "up" else below)
 
     def ccopy(p, k, e, to):
         return rcopy(part(p, e, k), part(p, e, k), r.x_s.at[p, to, k], r.c_r.at[p, e, k], dp=to)
@@ -448,9 +448,13 @@
             if t in late:
                 pl.when(near)(functools.partial(strip_out, late[t]))
                 pl.when(spots[1] == 2)(functools.partial(strip_sum, late[t]))
+            if t - 2 in late:
+                pl.when(spots[1] == 2)(functools.partial(strip_out, late[t - 2]))
+        done = max(beats, heads - early) - 2
         for j in range(strips):
             pl.when(spots[1] > 2)(functools.partial(strip_sum, j))
-            pl.when(spots[1] > 1)(functools.partial(strip_out, j))
+            left = spots[1] > 2 if [t for t in late if late[t] == j][0] < done else spots[1] > 1
+            pl.when(left)(functools.partial(strip_out, j))
             strip_along(j)
     else:
         for h in range(early, heads):
@@ -461,6 +465,13 @@
         for j in range(strips):
             strip_out(j)
             strip_along(j)
+
+    @pl.when(me == S - 1)
+    def _():
+        for p in range(strips):
+            for e in others:
+                ccopy(p, me, e, e).wait_recv()
+                zcopy(p, "down", me, e).start()
 
     @pl.when(spots[0] == S - 1)
     def _():
@@ -559,22 +570,26 @@
         there = (k >= 0) if way == "up" else (k < S)
         more = (me < S - 1) if way == "up" else (me > 0)
 
-        @pl.when(there)
-        def _():
-            zcopy(p, way, k).wait_recv()
-
-        @pl.when(there & more)
-        def _():
-            zcopy(p, way, k).start()
-
-        @pl.when(there)
+        for e in [mine] + (others if way == "down" else []):
+            here = there if e is mine else k == S - 1
+
+            @pl.when(here)
+            def _(e=e):
+                zcopy(p, way, k, e).wait_recv()
+
+            @pl.when(here & more)
+            def _(e=e):
+                zcopy(p, way, k, e).start()
+
+        @pl.when(there & (k < S - 1))
         def _():
             for e in others:
                 ccopy(p, k, mine, e).start()
 
-    def hop(way, d):
+    def hop(d):
         for p in range(strips):
-            forward(p, way, d)
+            forward(p, "up", d)
+            forward(p, "down", d)
 
     def share_p(j, q, landing, slot):
         piece = pl.ds(j * cut, cut)
@@ -602,8 +617,10 @@
         r.p_o[:, :, piece] = out.astype(BF).reshape(C, rows, cut)
         r.p_last[:, piece] = out[length - PAD :, :]
         send_p(j, False)
+        forward(j, "up", 1)
         forward(j, "down", 1)
     for p in range(parts, strips):
+        forward(p, "up", 1)
         forward(p, "down", 1)
 
     @pl.when(me < S - 1)
@@ -617,9 +634,7 @@
 
     for j in range(parts):
         send_p(j, True)
-    hop("up", 1)
-    hop("down", 2)
-    hop("up", 2)
+    hop(2)
     small_all(lambda e, q: small_to(e, q, e, q).wait_recv())
 
     norm = 1.0 / math.sqrt(D * S * length)
@@ -643,10 +658,9 @@
     each(C, lambda d: share_m(lax.rem(ch + d, C), ch, ch).start())
     if S <= 12:
         for d in range(3, S):
-            hop("down", d)
-            hop("up", d)
+            hop(d)
     else:
-        lax.fori_loop(3, S, lambda d, c: (hop("down", d), hop("up", d), c)[2], 0)
+        lax.fori_loop(3, S, lambda d, c: (hop(d), c)[1], 0)
 
     def step_term(k, total):
         for e in range(D):
@@ -663,9 +677,12 @@
     r.o_dws[...] = (norm * step_total)[:heads, :]
 
     def weight_term(k, first=False):
-        for e in others:
-            for p in range(strips):
-                ccopy(p, k, e, e).wait_recv()
+        @pl.when(k < S - 1)
+        def _():
+            for e in others:
+                for p in range(strips):
+                    ccopy(p, k, e, e).wait_recv()
+
         x = r.xc[k].reshape(D * length, columns)
         term = norm * mm(x, r.gin[k].reshape(D * length, width), 0, 0)
         r.o_dw[...] = term if first else r.o_dw[...] + term
@@ -706,15 +723,20 @@
     each(C, settle_chan)
 
     def settle_line(k):
-        for e in others:
-            for p in range(strips):
-                ccopy(p, k, mine, e).wait_send()
-        for way, sent in (("up", (k <= me) & (me < S - 1)), ("down", (k >= me) & (me > 0))):
+        @pl.when((k < S - 1) | (me == S - 1))
+        def _():
+            for e in others:
+                for p in range(strips):
+                    ccopy(p, k, mine, e).wait_send()
+
+        for way, e, sent in [
+            ("up", mine, (k <= me) & (me < S - 1)), ("down", mine, (k >= me) & (me > 0))
+        ] + [("down", e, (k == S - 1) & (me > 0)) for e in others]:
 
             @pl.when(sent)
-            def _(way=way):
+            def _(way=way, e=e):
                 for p in range(strips):
-                    zcopy(p, way, k).wait_send()
+                    zcopy(p, way, k, e).wait_send()
 
     settle_line(0)
     each(S, settle_line)
@@ -826,8 +848,9 @@
         swap_s=dma((dps,)), swap_r=dma((dps,)), cross_s=dma((seqs,)), cross_r=dma((seqs,)),
         gat_s=dma((chans,)), gat_r=dma((chans,)),
         chain_s=dma((2, PIECES)), chain_r=dma((2, PIECES)),
-        z_r=dma((strips, seqs)), c_r=dma((strips, dps, seqs)),
-        u_s=dma((strips, seqs)), d_s=dma((strips, seqs)), x_s=dma((strips, dps, seqs)),
+        z_r=dma((strips, dps, seqs)), c_r=dma((strips, dps, seqs)),
+        u_s=dma((strips, dps, seqs)), d_s=dma((strips, dps, seqs)),
+        x_s=dma((strips, dps, seqs)),
         z2_r=dma((dps, seqs)),
         z2_s=dma((dps, seqs)), mt_s=dma((1,)), mt_r=dma((chans,)),
         gm_s=dma((chans,)), gm_r=dma((chans,)),

time: 51.2 us -> 53.3 us (1.041)
  Pallas kernels: 50.4 us -> 52.5 us
    pallas_call x1, Pallas kernels: 49.4 us -> 51.5 us  [body(): pl.pallas_call(functools.partial(layer_kernel, names, sizes, heads), out_...]
where the time goes in v7:
time: 53.3 us; the launch traced here: 53.2 us
  Pallas kernels  52.5 us (98%)
  between operations  0.64 us (1%)
    pallas_call x1, Pallas kernels, body(): pl.pallas_call(functools.partial(layer_kernel, names, sizes, heads), out_...  51.5 us

profile of v7, /device:TPU:0, one launch (start us, length us, event | category | flops | bytes accessed | tf_op | source)
XLA Modules:
  0.0 53.2 jit_solution(14663932083362534702)
XLA Ops:
  0.6 51.5 %layer.1 = (bf16[4,32,2560]{2,1,0:T(8,128)(2,1)S(1)}, f32[320,640]{1,0:T(8,128)S(1)}, bf16[4,80,256]{2,1,0:T(8,128)(2,1)S(1)}, f32[10,320]{1,0:T(8,128)S(1)}) custom-call(bf16[32,2560]{1,0:T(8,128)(2,1)} %bitcast.8, bf16[2560,640]{1,0:T(8,128)(2,1)} %refs_1_.1, bf16[2560,256]{1,0:T(8,128)(2,1)} %refs_2_.1, bf16[10,2560]{1,0:T(8,128)(2,1)} %bitcast.10, ...), custom_call_target="tpu_custom_call" | custom-call | tf_op jit(solution)/shard_map/layer/pallas_call | solution.py:860
  52.2 1.0 %finish.1 = (bf16[32,2560]{1,0:T(8,128)(2,1)}, f32[320,640]{1,0:T(8,128)}, f32[80,256]{1,0:T(8,128)}, f32[10,320]{1,0:T(8,128)}) custom-call(bf16[4,32,2560]{2,1,0:T(8,128)(2,1)S(1)} %get-tuple-element.12.parts, f32[320,640]{1,0:T(8,128)S(1)} %get-tuple-element.13.dw, bf16[4,80,256]{2,1,0:T(8,128)(2,1)S(1)} %get-tuple-element.14.mixes, ...), custom_call_target="tpu_custom_call" | custom-call | tf_op jit(solution)/shard_map/finish/pallas_call | solution.py:871

commit v8 on v6

--- a/solution.py
+++ b/solution.py
@@ -16,7 +16,6 @@
 LIMIT = 48 * 2**20
 BF = jnp.bfloat16
 F32 = jnp.float32
-HIGH = lax.Precision.HIGHEST
 PIECES = 10
 LOADED = (
     "own", "w_in", "w_mix", "w_step", "conv_in", "conv_mix", "bias", "log", "skip", "grad",
@@ -46,10 +45,21 @@
     )
 
 
+def thirds(v):
+    high = v.astype(BF)
+    rest = v - high.astype(F32)
+    middle = rest.astype(BF)
+    return high, middle, (rest - middle.astype(F32)).astype(BF)
+
+
 def exact(a, b, da=1, db=0):
-    return lax.dot_general(
-        a, b, (((da,), (db,)), ((), ())), precision=HIGH, preferred_element_type=F32
-    )
+    high, middle, low = thirds(a)
+    return mm(high, b, da, db) + (mm(middle, b, da, db) + mm(low, b, da, db))
+
+
+def exact_left(a, b, da=1, db=0):
+    high, middle, low = thirds(b)
+    return mm(a, high, da, db) + (mm(a, middle, da, db) + mm(a, low, da, db))
 
 
 def softplus(v):
@@ -70,7 +80,7 @@
     row = lax.broadcasted_iota(jnp.int32, (length, length), 0)
     col = lax.broadcasted_iota(jnp.int32, (length, length), 1)
     lower = (row >= col).astype(F32)
-    cumulative = exact(lower, -step * rate)
+    cumulative = exact_left(lower, -step * rate)
     return step, rate, cumulative, row, col, lower
 
 
@@ -152,23 +162,30 @@
         return r.own.at[:, pl.ds(p * cut, cut)]
 
     def near(c, p):
-        return rcopy(mine_at(p), block(c, p), r.near_s.at[p], r.near_r.at[p], chan=partner)
+        return rcopy(mine_at(p), block(c, p), r.near_s.at[0], r.near_r.at[p], chan=partner)
 
     def far(to, c, slot, p):
         return rcopy(
-            mine_at(p), block(c, p), r.far_s.at[to, p], r.far_r.at[slot, p], chan=2 * to + low
+            mine_at(p), block(c, p), r.far_s.at[to], r.far_r.at[slot, p], chan=2 * to + low
         )
 
     def relay(source, lane, p):
         c = 2 * source + lane
         here = block(c, p)
-        return rcopy(here, here, r.relay_s.at[source, p], r.relay_r.at[source, p], chan=partner)
-
-    def swap(q, landing, slot):
-        return rcopy(r.blocks.at[q], r.mid.at[landing], r.swap_s.at[q], r.swap_r.at[slot], dp=q)
-
-    def cross(q, landing, slot):
-        return rcopy(r.mid.at[:, q], r.xs.at[landing], r.cross_s.at[q], r.cross_r.at[slot], seq=q)
+        return rcopy(here, here, r.relay_s.at[source], r.relay_r.at[source, p], chan=partner)
+
+    def column(e, q, landing_e, landing_q):
+        return rcopy(
+            r.blocks.at[e, q], r.xs.at[landing_q, landing_e],
+            r.cross_s.at[e, q], r.cross_r.at[landing_e, landing_q], dp=e, seq=q,
+        )
+
+    def columns_all(do):
+        each(S, lambda d: do(mine, lax.rem(me + d, S)))
+        for d in range(1, D):
+            e = lax.rem(mine + d, D)
+            do(e, me)
+            each(S, lambda d, e=e: do(e, lax.rem(me + d, S)))
 
     loads["own"].wait()
     pl.semaphore_wait(barrier, total)
@@ -180,8 +197,8 @@
         for k in range(S):
             at = (d * S + k) * cols
             r.blocks[d, k] = r.own[:, at : at + cols]
-    each(D, lambda d: swap(lax.rem(mine + d, D), mine, mine).start())
-    r.mid[mine] = r.blocks[mine]
+    columns_all(lambda e, q: column(e, q, mine, me).start())
+    r.xs[me, mine] = r.blocks[mine, me]
     r.xg[pl.ds(pl.multiple_of(ch * rows, rows), rows), :] = r.own[...]
     r.wst[...] = jnp.zeros(r.wst.shape, BF)
     r.vec[...] = jnp.zeros(r.vec.shape, F32)
@@ -219,10 +236,6 @@
         if p + 1 < pieces:
             pass_on(p + 1)
         project(p)
-        if p == 0:
-            each(D, lambda d: swap(lax.rem(mine + d, D), mine, lax.rem(mine + d, D)).wait_recv())
-            each(S, lambda d: cross(lax.rem(me + d, S), me, me).start())
-            r.xs[me] = r.mid[:, me]
     inner_low = r.wide_in[PAD:, :].astype(BF)
     mixer_low = r.wide_mix[PAD:, :].astype(BF)
     r.fh_o[:, :width] = inner_low[length - PAD :, :]
@@ -277,19 +290,15 @@
     def _():
         halo().wait_send()
 
-    for p in range(pieces):
-        near(ch, p).wait_send()
-        for d in range(1, sides):
-            source = lax.rem(side + d, sides)
-            far(source, ch, source, p).wait_send()
-            relay(source, low, p).wait_send()
-    each(D, lambda d: swap(lax.rem(mine + d, D), mine, mine).wait_send())
-
-    def settle(d):
-        q = lax.rem(me + d, S)
-        cross(q, me, q).wait()
-
-    return lambda: each(S, settle)
+    def sent(sem):
+        rcopy(r.own, r.own, sem, r.near_r.at[0], chan=partner).wait_send()
+
+    sent(r.near_s.at[0])
+    for d in range(1, sides):
+        source = lax.rem(side + d, sides)
+        sent(r.far_s.at[source])
+        sent(r.relay_s.at[source])
+    return lambda: columns_all(lambda e, q: column(e, q, e, q).wait())
 
 
 def rear(r, sizes, place, heads, crossed):
@@ -314,7 +323,7 @@
     def carry(way, piece, first=False):
         part = pl.ds(pl.multiple_of(piece * size, size), size)
         source = terms[way] if first else scratch[way]
-        sems = r.chain_s.at[way, piece], r.chain_r.at[way, piece]
+        sems = r.chain_s.at[way], r.chain_r.at[way, piece]
         return rcopy(source.at[part], outs[way].at[part], *sems, seq=above if way == 0 else below)
 
     for way in (1, 0):
@@ -375,7 +384,7 @@
         return slice(j * LANES, (j + 1) * LANES)
 
     def halo(j):
-        return rcopy(r.hal_o.at[j], r.hal_i.at[j], r.hal_s.at[j], r.hal_r.at[j], seq=below)
+        return rcopy(r.hal_o.at[j], r.hal_i.at[j], r.hal_s.at[0], r.hal_r.at[j], seq=below)
 
     def strip_sum(j):
         cols = strip(j)
@@ -400,12 +409,12 @@
         return r.gin.at[k, e, :, pl.ds(p * LANES, LANES)]
 
     def zcopy(p, way, k):
-        send = (r.u_s if way == "up" else r.d_s).at[p, k]
+        send = (r.u_s if way == "up" else r.d_s).at[k]
         here = part(p, mine, k)
         return rcopy(here, here, send, r.z_r.at[p, k], seq=above if way == "up" else below)
 
     def ccopy(p, k, e, to):
-        return rcopy(part(p, e, k), part(p, e, k), r.x_s.at[p, to, k], r.c_r.at[p, e, k], dp=to)
+        return rcopy(part(p, e, k), part(p, e, k), r.x_s.at[to, k], r.c_r.at[e, k], dp=to)
 
     def strip_out(j):
         cols = strip(j)
@@ -504,6 +513,32 @@
     r.gm_in[ch] = r.am[pl.ds(pl.multiple_of(ch * rows, rows), rows + PAD), :]
     r.gmp[...] = spread_back(r.pad_mix, r.conv_mix, 0, length)
 
+    def forward(p, way, d):
+        k = me - d if way == "up" else me + d
+        there = (k >= 0) if way == "up" else (k < S)
+        more = (me < S - 1) if way == "up" else (me > 0)
+
+        @pl.when(there)
+        def _():
+            zcopy(p, way, k).wait_recv()
+
+        @pl.when(there & more)
+        def _():
+            zcopy(p, way, k).start()
+
+        @pl.when(there)
+        def _():
+            for e in others:
+                ccopy(p, k, mine, e).start()
+
+    def both(p, d):
+        forward(p, "up", d)
+        forward(p, "down", d)
+
+    def hop(d):
+        for p in range(strips):
+            both(p, d)
+
     upstream = r.grad[...].astype(F32)
     stepped = r.stepped[...].astype(F32)
     ending = r.ending[...]
@@ -518,12 +553,14 @@
     overall = jnp.sum(tail_term, axis=0, keepdims=True) + jnp.exp(last) * jnp.sum(
         head_mask(width, False) * held, axis=0, keepdims=True
     )
-    decay_grad = exact(lower, sum_grad, 0, 0) + overall
+    decay_grad = exact_left(lower, sum_grad, 0, 0) + overall
     rate = jnp.exp(r.vec[1:2, :])
     step_grad = (step_grad - rate * decay_grad) * jax.nn.sigmoid(r.raw[...] + r.vec[0:1, :])
     steps = step_grad.astype(BF)
     r.gsm[me, mine, rows:, 0:LANES] = step_grad.T[0:PAD, :].astype(BF)
     steps = steps[:, 0:PAD]
+
+    both(0, 1)
 
     each(C, lambda d: share_mix(lax.rem(ch + d, C), ch, lax.rem(ch + d, C)).wait_recv())
     mix = r.gm_in[0].astype(F32)
@@ -554,33 +591,16 @@
 
     small_all(lambda e, q: small_to(mine, me, e, q).start())
 
-    def forward(p, way, d):
-        k = me - d if way == "up" else me + d
-        there = (k >= 0) if way == "up" else (k < S)
-        more = (me < S - 1) if way == "up" else (me > 0)
-
-        @pl.when(there)
-        def _():
-            zcopy(p, way, k).wait_recv()
-
-        @pl.when(there & more)
-        def _():
-            zcopy(p, way, k).start()
-
-        @pl.when(there)
-        def _():
-            for e in others:
-                ccopy(p, k, mine, e).start()
-
-    def hop(way, d):
-        for p in range(strips):
-            forward(p, way, d)
+    both(1, 1)
 
     def share_p(j, q, landing, slot):
         piece = pl.ds(j * cut, cut)
         return rcopy(
-            r.p_o.at[q, :, piece], r.p_i.at[landing, :, piece], r.p_s.at[j, q], r.p_r.at[j, slot], chan=q
+            r.p_o.at[q, :, piece], r.p_i.at[landing, :, piece], r.p_s.at[q], r.p_r.at[slot], chan=q
         )
+
+    def whole_p(q):
+        return rcopy(r.p_o.at[q], r.p_i.at[q], r.p_s.at[q], r.p_r.at[q], chan=q)
 
     grads = r.gin[me, mine]
     mixes = r.gmp[...]
@@ -602,9 +622,10 @@
         r.p_o[:, :, piece] = out.astype(BF).reshape(C, rows, cut)
         r.p_last[:, piece] = out[length - PAD :, :]
         send_p(j, False)
-        forward(j, "down", 1)
-    for p in range(parts, strips):
-        forward(p, "down", 1)
+        if j + 2 < strips:
+            both(j + 2, 1)
+    for p in range(parts + 2, strips):
+        both(p, 1)
 
     @pl.when(me < S - 1)
     def _():
@@ -617,9 +638,7 @@
 
     for j in range(parts):
         send_p(j, True)
-    hop("up", 1)
-    hop("down", 2)
-    hop("up", 2)
+    hop(2)
     small_all(lambda e, q: small_to(e, q, e, q).wait_recv())
 
     norm = 1.0 / math.sqrt(D * S * length)
@@ -643,10 +662,9 @@
     each(C, lambda d: share_m(lax.rem(ch + d, C), ch, ch).start())
     if S <= 12:
         for d in range(3, S):
-            hop("down", d)
-            hop("up", d)
+            hop(d)
     else:
-        lax.fori_loop(3, S, lambda d, c: (hop("down", d), hop("up", d), c)[2], 0)
+        lax.fori_loop(3, S, lambda d, c: (hop(d), c)[1], 0)
 
     def step_term(k, total):
         for e in range(D):
@@ -662,10 +680,12 @@
         step_total = lax.fori_loop(0, S, step_term, step_total)
     r.o_dws[...] = (norm * step_total)[:heads, :]
 
+    def whole(k, e, send, recv):
+        return rcopy(r.gin.at[k, e], r.gin.at[k, e], send, recv, seq=above)
+
     def weight_term(k, first=False):
         for e in others:
-            for p in range(strips):
-                ccopy(p, k, e, e).wait_recv()
+            whole(k, e, r.x_s.at[e, k], r.c_r.at[e, k]).wait_recv()
         x = r.xc[k].reshape(D * length, columns)
         term = norm * mm(x, r.gin[k].reshape(D * length, width), 0, 0)
         r.o_dw[...] = term if first else r.o_dw[...] + term
@@ -678,21 +698,18 @@
     each(S, weight_terms)
     r.p_i[ch] = r.p_o[ch]
     r.m_i[ch] = r.m_o[ch]
-    for j in range(parts):
-        each(C, lambda d, j=j: share_p(j, lax.rem(ch + d, C), ch, lax.rem(ch + d, C)).wait_recv())
+    each(C, lambda d: whole_p(lax.rem(ch + d, C)).wait_recv())
     each(C, lambda d: share_m(lax.rem(ch + d, C), ch, lax.rem(ch + d, C)).wait_recv())
 
     for way in (0, 1):
 
         @pl.when(spots[way] < S - 1)
         def _(way=way):
-            for piece in range(pieces):
-                carry(way, piece).wait_send()
+            rcopy(terms[way], outs[way], r.chain_s.at[way], r.chain_r.at[way, 0], seq=above).wait_send()
 
     @pl.when(me > 0)
     def _():
-        for j in range(strips):
-            halo(j).wait_send()
+        rcopy(r.hal_o, r.hal_i, r.hal_s.at[0], r.hal_r.at[0], seq=below).wait_send()
         mix_halo().wait_send()
         mix_tail(ch).wait_send()
 
@@ -700,21 +717,18 @@
         q = lax.rem(ch + d, C)
         share_mix(q, ch, ch).wait_send()
         share_m(q, ch, ch).wait_send()
-        for j in range(parts):
-            share_p(j, q, ch, ch).wait_send()
+        whole_p(q).wait_send()
 
     each(C, settle_chan)
 
     def settle_line(k):
         for e in others:
-            for p in range(strips):
-                ccopy(p, k, mine, e).wait_send()
+            whole(k, mine, r.x_s.at[e, k], r.c_r.at[mine, k]).wait_send()
         for way, sent in (("up", (k <= me) & (me < S - 1)), ("down", (k >= me) & (me > 0))):
 
             @pl.when(sent)
             def _(way=way):
-                for p in range(strips):
-                    zcopy(p, way, k).wait_send()
+                whole(k, mine, (r.u_s if way == "up" else r.d_s).at[k], r.z_r.at[0, k]).wait_send()
 
     settle_line(0)
     each(S, settle_line)
@@ -797,7 +811,7 @@
     scratch = {key: pltpu.VMEM(v.shape, v.dtype) for key, v in inputs.items()}
     scratch |= dict(
         wst=low(LANES, model), xg=low(length, model),
-        blocks=low(dps, seqs, rows, cols), mid=low(dps, seqs, rows, cols),
+        blocks=low(dps, seqs, rows, cols),
         xs=low(seqs, dps, rows, cols), xc=low(seqs, dps, chans, rows, cols),
         wide_in=full(PAD + length, width), wide_mix=full(PAD + length, mixed),
         fh_o=low(PAD, width + mixed), fh_i=low(PAD, width + mixed), vec=full(8, LANES),
@@ -819,19 +833,19 @@
         am=low(length + PAD, mixed), mt_in=low(chans, PAD, mixed),
         p_o=low(chans, rows, model), m_o=low(chans, band, mixed),
         load_sem=dma((len(LOADED),)), fh_sem=dma((2,)), halm_s=dma((2,)),
-        hal_s=dma((strips,)), hal_r=dma((strips,)),
-        near_s=dma((chans,)), near_r=dma((chans,)),
-        far_s=dma((chans // 2, chans)), far_r=dma((chans // 2, chans)),
-        relay_s=dma((chans // 2, chans)), relay_r=dma((chans // 2, chans)),
-        swap_s=dma((dps,)), swap_r=dma((dps,)), cross_s=dma((seqs,)), cross_r=dma((seqs,)),
+        hal_s=dma((1,)), hal_r=dma((strips,)),
+        near_s=dma((1,)), near_r=dma((chans,)),
+        far_s=dma((chans // 2,)), far_r=dma((chans // 2, chans)),
+        relay_s=dma((chans // 2,)), relay_r=dma((chans // 2, chans)),
+        cross_s=dma((dps, seqs)), cross_r=dma((dps, seqs)),
         gat_s=dma((chans,)), gat_r=dma((chans,)),
-        chain_s=dma((2, PIECES)), chain_r=dma((2, PIECES)),
-        z_r=dma((strips, seqs)), c_r=dma((strips, dps, seqs)),
-        u_s=dma((strips, seqs)), d_s=dma((strips, seqs)), x_s=dma((strips, dps, seqs)),
+        chain_s=dma((2,)), chain_r=dma((2, PIECES)),
+        z_r=dma((strips, seqs)), c_r=dma((dps, seqs)),
+        u_s=dma((seqs,)), d_s=dma((seqs,)), x_s=dma((dps, seqs)),
         z2_r=dma((dps, seqs)),
         z2_s=dma((dps, seqs)), mt_s=dma((1,)), mt_r=dma((chans,)),
         gm_s=dma((chans,)), gm_r=dma((chans,)),
-        p_s=dma((chans, chans)), p_r=dma((chans, chans)), m_s=dma((chans,)), m_r=dma((chans,)),
+        p_s=dma((chans,)), p_r=dma((chans,)), m_s=dma((chans,)), m_r=dma((chans,)),
     )
     names = [key + "_h" for key in inputs] + list(outputs) + list(scratch)
     parts, inner_grad, mix_parts, step_grad = pl.pallas_call(

time: 51.2 us -> 48.3 us (0.943)
  Pallas kernels: 50.4 us -> 47.5 us
    pallas_call x1, Pallas kernels: 49.4 us -> 46.5 us  [body(): pl.pallas_call(functools.partial(layer_kernel, names, sizes, heads), out_...]
where the time goes in v8:
time: 48.3 us; the launch traced here: 48.1 us
  Pallas kernels  47.5 us (98%)
  between operations  0.64 us (1%)
    pallas_call x1, Pallas kernels, body(): pl.pallas_call(functools.partial(layer_kernel, names, sizes, heads), out_...  46.5 us
    pallas_call x1, Pallas kernels, body(): pl.pallas_call(finish_kernel, out_shape=(jax.ShapeDtypeStruct((rows, mode...  1.01 us

profile of v8, /device:TPU:0, one launch (start us, length us, event | category | flops | bytes accessed | tf_op | source)
XLA Modules:
  0.0 48.1 jit_solution(5978580558086511728)
XLA Ops:
  0.6 46.5 %layer.1 = (bf16[4,32,2560]{2,1,0:T(8,128)(2,1)S(1)}, f32[320,640]{1,0:T(8,128)S(1)}, bf16[4,80,256]{2,1,0:T(8,128)(2,1)S(1)}, f32[10,320]{1,0:T(8,128)S(1)}) custom-call(bf16[32,2560]{1,0:T(8,128)(2,1)} %bitcast.8, bf16[2560,640]{1,0:T(8,128)(2,1)} %refs_1_.1, bf16[2560,256]{1,0:T(8,128)(2,1)} %refs_2_.1, bf16[10,2560]{1,0:T(8,128)(2,1)} %bitcast.10, ...), custom_call_target="tpu_custom_call" | custom-call | tf_op jit(solution)/shard_map/layer/pallas_call | solution.py:851
  47.1 1.0 %finish.1 = (bf16[32,2560]{1,0:T(8,128)(2,1)}, f32[320,640]{1,0:T(8,128)}, f32[80,256]{1,0:T(8,128)}, f32[10,320]{1,0:T(8,128)}) custom-call(bf16[4,32,2560]{2,1,0:T(8,128)(2,1)S(1)} %get-tuple-element.12.parts, f32[320,640]{1,0:T(8,128)S(1)} %get-tuple-element.13.dw, bf16[4,80,256]{2,1,0:T(8,128)(2,1)S(1)} %get-tuple-element.14.mixes, ...), custom_call_target="tpu_custom_call" | custom-call | tf_op jit(solution)/shard_map/finish/pallas_call | solution.py:862

commit v9 on v8

--- a/solution.py
+++ b/solution.py
@@ -149,17 +149,22 @@
     mixed = r.sum_mix.shape[1]
     cols = model // (D * S)
     half = mixed // 2
-    pieces = C
-    cut = model // pieces
+    splits = 2
+    high = rows // 2
+    cut = model // splits
+    pieces = [(1, k) for k in range(splits)] + [(0, k) for k in range(splits)]
     sides = C // 2
     side, low = lax.div(ch, 2), lax.rem(ch, 2)
     partner = ch + 1 - 2 * low
 
     def block(c, p):
-        return r.xg.at[pl.ds(pl.multiple_of(c * rows, rows), rows), pl.ds(p * cut, cut)]
+        part, k = pieces[p]
+        first = pl.multiple_of(c * rows + part * high, high)
+        return r.xg.at[pl.ds(first, high), pl.ds(k * cut, cut)]
 
     def mine_at(p):
-        return r.own.at[:, pl.ds(p * cut, cut)]
+        part, k = pieces[p]
+        return r.own.at[pl.ds(part * high, high), pl.ds(k * cut, cut)]
 
     def near(c, p):
         return rcopy(mine_at(p), block(c, p), r.near_s.at[0], r.near_r.at[p], chan=partner)
@@ -189,7 +194,7 @@
 
     loads["own"].wait()
     pl.semaphore_wait(barrier, total)
-    for p in range(pieces):
+    for p in range(len(pieces)):
         for d in range(1, sides):
             far(lax.rem(side + d, sides), ch, side, p).start()
         near(ch, p).start()
@@ -219,35 +224,33 @@
         for d in range(1, sides):
             source = lax.rem(side + d, sides)
             relay(source, 1 - low, p).wait_recv()
-        piece = slice(p * cut, (p + 1) * cut)
-        x = r.xg[:, piece]
+        part, k = pieces[p]
+        piece = slice(k * cut, (k + 1) * cut)
+        x = jnp.concatenate([r.xg[c * rows + part * high : c * rows + (part + 1) * high, piece] for c in range(C)])
         inner = mm(x, r.w_in[piece, :], 1, 0)
         mixer = mm(x, r.w_mix[piece, :], 1, 0)
         raw = mm(x, r.wst[:, piece], 1, 1)
-        if p == 0:
-            r.wide_in[PAD:, :], r.wide_mix[PAD:, :], r.raw[...] = inner, mixer, raw
-        else:
-            r.wide_in[PAD:, :] = r.wide_in[PAD:, :] + inner
-            r.wide_mix[PAD:, :] = r.wide_mix[PAD:, :] + mixer
-            r.raw[...] = r.raw[...] + raw
+        for c in range(C):
+            at = c * rows + part * high
+            here = slice(c * high, (c + 1) * high)
+            for ref, pad, term in ((r.wide_in, PAD, inner), (r.wide_mix, PAD, mixer), (r.raw, 0, raw)):
+                old = ref[pad + at : pad + at + high, :] if k else 0.0
+                ref[pad + at : pad + at + high, :] = old + term[here, :]
+
+    def halo():
+        return rcopy(r.fh_o, r.fh_i, r.fh_sem.at[0], r.fh_sem.at[1], seq=lax.rem(me + 1, S))
 
     pass_on(0)
-    for p in range(pieces):
-        if p + 1 < pieces:
+    for p in range(len(pieces)):
+        if p + 1 < len(pieces):
             pass_on(p + 1)
         project(p)
+        if p == splits - 1:
+            r.fh_o[:, :width] = r.wide_in[length:, :].astype(BF)
+            r.fh_o[:, width:] = r.wide_mix[length:, :].astype(BF)
+            pl.when(me < S - 1)(lambda: halo().start())
     inner_low = r.wide_in[PAD:, :].astype(BF)
     mixer_low = r.wide_mix[PAD:, :].astype(BF)
-    r.fh_o[:, :width] = inner_low[length - PAD :, :]
-    r.fh_o[:, width:] = mixer_low[length - PAD :, :]
-
-    def halo():
-        return rcopy(r.fh_o, r.fh_i, r.fh_sem.at[0], r.fh_sem.at[1], seq=lax.rem(me + 1, S))
-
-    @pl.when(me < S - 1)
-    def _():
-        halo().start()
-
     r.wide_in[PAD:, :] = inner_low.astype(F32)
     r.wide_mix[PAD:, :] = mixer_low.astype(F32)
     r.wide_in[0:PAD, :] = jnp.zeros((PAD, width), F32)
@@ -428,10 +431,17 @@
         for e in others:
             ccopy(j, me, mine, e).start()
 
-    def strip_along(j):
-        @pl.when(me < S - 1)
+    def strip_up(j):
+        zcopy(j, "up", me).start()
+
+    def strip_early(j):
+        strip_out(j)
+        strip_up(j)
+
+    def strip_along(j, sent):
+        @pl.when((me < S - 1) & (spots[1] != 2) if sent else me < S - 1)
         def _():
-            zcopy(j, "up", me).start()
+            strip_up(j)
 
         @pl.when(me > 0)
         def _():
@@ -457,10 +467,13 @@
             if t in late:
                 pl.when(near)(functools.partial(strip_out, late[t]))
                 pl.when(spots[1] == 2)(functools.partial(strip_sum, late[t]))
+            if t - 2 in late:
+                pl.when(spots[1] == 2)(functools.partial(strip_early, late[t - 2]))
+        done = {j: t + 2 < max(beats, heads - early) for t, j in late.items()}
         for j in range(strips):
             pl.when(spots[1] > 2)(functools.partial(strip_sum, j))
-            pl.when(spots[1] > 1)(functools.partial(strip_out, j))
-            strip_along(j)
+            pl.when(spots[1] > (2 if done[j] else 1))(functools.partial(strip_out, j))
+            strip_along(j, done[j])
     else:
         for h in range(early, heads):
             head(h)
@@ -469,7 +482,7 @@
             strip_sum(j)
         for j in range(strips):
             strip_out(j)
-            strip_along(j)
+            strip_along(j, False)
 
     @pl.when(spots[0] == S - 1)
     def _():
@@ -560,8 +573,6 @@
     r.gsm[me, mine, rows:, 0:LANES] = step_grad.T[0:PAD, :].astype(BF)
     steps = steps[:, 0:PAD]
 
-    both(0, 1)
-
     each(C, lambda d: share_mix(lax.rem(ch + d, C), ch, lax.rem(ch + d, C)).wait_recv())
     mix = r.gm_in[0].astype(F32)
     for q in range(1, C):
@@ -589,9 +600,8 @@
             do(e, me)
             each(S, lambda d, e=e: do(e, lax.rem(me + d, S)))
 
-    small_all(lambda e, q: small_to(mine, me, e, q).start())
-
-    both(1, 1)
+
+    both(0, 1)
 
     def share_p(j, q, landing, slot):
         piece = pl.ds(j * cut, cut)
@@ -622,9 +632,11 @@
         r.p_o[:, :, piece] = out.astype(BF).reshape(C, rows, cut)
         r.p_last[:, piece] = out[length - PAD :, :]
         send_p(j, False)
-        if j + 2 < strips:
-            both(j + 2, 1)
-    for p in range(parts + 2, strips):
+        if j + 1 < strips:
+            both(j + 1, 1)
+        if j == 1:
+            small_all(lambda e, q: small_to(mine, me, e, q).start())
+    for p in range(parts + 1, strips):
         both(p, 1)
 
     @pl.when(me < S - 1)
@@ -780,7 +792,7 @@
     cols = model // groups
     state_size = mixed // 2
     assert width % PIECES == 0 and chans % 2 == 0 and seqs > 2
-    assert width % LANES == 0 and PIECES % (width // LANES) == 0
+    assert rows == 2 * PAD and width % LANES == 0 and PIECES % (width // LANES) == 0
     assert length == LANES and heads + conv_inner.shape[0] - 1 <= PAD
     upstream = output_grad[0]
     step_rows = step_weight.T

time: 48.3 us -> 49.2 us (1.019)
  Pallas kernels: 47.5 us -> 48.5 us
    pallas_call x1, Pallas kernels: 46.5 us -> 47.4 us  [body(): pl.pallas_call(functools.partial(layer_kernel, names, sizes, heads), out_...]
where the time goes in v9:
time: 49.2 us; the launch traced here: 49.1 us
  Pallas kernels  48.5 us (99%)
  between operations  0.64 us (1%)
    pallas_call x1, Pallas kernels, body(): pl.pallas_call(functools.partial(layer_kernel, names, sizes, heads), out_...  47.4 us
    pallas_call x1, Pallas kernels, body(): pl.pallas_call(finish_kernel, out_shape=(jax.ShapeDtypeStruct((rows, mode...  1.01 us

profile of v9, /device:TPU:0, one launch (start us, length us, event | category | flops | bytes accessed | tf_op | source)
XLA Modules:
  0.0 49.1 jit_solution(3223669097619479557)
XLA Ops:
  0.6 47.4 %layer.1 = (bf16[4,32,2560]{2,1,0:T(8,128)(2,1)S(1)}, f32[320,640]{1,0:T(8,128)S(1)}, bf16[4,80,256]{2,1,0:T(8,128)(2,1)S(1)}, f32[10,320]{1,0:T(8,128)S(1)}) custom-call(bf16[32,2560]{1,0:T(8,128)(2,1)} %bitcast.8, bf16[2560,640]{1,0:T(8,128)(2,1)} %refs_1_.1, bf16[2560,256]{1,0:T(8,128)(2,1)} %refs_2_.1, bf16[10,2560]{1,0:T(8,128)(2,1)} %bitcast.10, ...), custom_call_target="tpu_custom_call" | custom-call | tf_op jit(solution)/shard_map/layer/pallas_call | solution.py:863
  48.1 1.0 %finish.1 = (bf16[32,2560]{1,0:T(8,128)(2,1)}, f32[320,640]{1,0:T(8,128)}, f32[80,256]{1,0:T(8,128)}, f32[10,320]{1,0:T(8,128)}) custom-call(bf16[4,32,2560]{2,1,0:T(8,128)(2,1)S(1)} %get-tuple-element.12.parts, f32[320,640]{1,0:T(8,128)S(1)} %get-tuple-element.13.dw, bf16[4,80,256]{2,1,0:T(8,128)(2,1)S(1)} %get-tuple-element.14.mixes, ...), custom_call_target="tpu_custom_call" | custom-call | tf_op jit(solution)/shard_map/finish/pallas_call | solution.py:874

commit v10 on v9

--- a/solution.py
+++ b/solution.py
@@ -313,6 +313,7 @@
     model = r.w_in.shape[0]
     rows = length // C
     pieces, lag = PIECES, PIECES // 2
+    lags = (lag + 3, lag)
     size = width // pieces
     strips = width // LANES
     per = pieces // strips
@@ -340,7 +341,7 @@
     def beat(t):
         for way in (1, 0):
             spot = spots[way]
-            piece = t - lag * (spot - 1)
+            piece = t - lags[way] * (spot - 1)
 
             @pl.when((piece >= 0) & (piece < pieces) & (spot > 0) & (spot < S - 1))
             def _(way=way, piece=piece):
@@ -447,7 +448,7 @@
         def _():
             zcopy(j, "down", me).start()
 
-    beats = pieces + lag * max(S - 3, 0)
+    beats = pieces + lags[0] * max(S - 3, 0)
     early = heads // 2
     for h in range(early):
         head(h)
@@ -573,6 +574,8 @@
     r.gsm[me, mine, rows:, 0:LANES] = step_grad.T[0:PAD, :].astype(BF)
     steps = steps[:, 0:PAD]
 
+    both(0, 1)
+
     each(C, lambda d: share_mix(lax.rem(ch + d, C), ch, lax.rem(ch + d, C)).wait_recv())
     mix = r.gm_in[0].astype(F32)
     for q in range(1, C):
@@ -590,18 +593,27 @@
 
     r.gsm[me, mine, 0:rows, :] = spread_back(r.gmt, r.conv_mix, 0, rows)
 
-    def small_to(e, k, to, q):
+    def small_along(e, k, q):
         here = r.gsm.at[k, e]
-        return rcopy(here, here, r.z2_s.at[to, q], r.z2_r.at[e, k], dp=to, seq=q)
+        return rcopy(here, here, r.z2_s.at[e, q], r.z2_r.at[e, k], seq=q)
+
+    def cross_small(to):
+        here = r.gsm.at[me, mine]
+        return rcopy(here, here, r.z2_s.at[to, me], r.z2_r.at[mine, me], dp=to)
+
+    def crossed_small(e):
+        here = r.gsm.at[me, e]
+        return rcopy(here, here, r.z2_s.at[e, me], r.z2_r.at[e, me], dp=e)
+
+    def send_small(e):
+        each(S, lambda d: small_along(e, me, lax.rem(me + d, S)).start())
 
     def small_all(do):
-        each(S, lambda d: do(mine, lax.rem(me + d, S)))
-        for e in others:
-            do(e, me)
+        for e in [mine] + others:
             each(S, lambda d, e=e: do(e, lax.rem(me + d, S)))
 
-
-    both(0, 1)
+    both(1, 1)
+    both(2, 1)
 
     def share_p(j, q, landing, slot):
         piece = pl.ds(j * cut, cut)
@@ -632,11 +644,13 @@
         r.p_o[:, :, piece] = out.astype(BF).reshape(C, rows, cut)
         r.p_last[:, piece] = out[length - PAD :, :]
         send_p(j, False)
-        if j + 1 < strips:
-            both(j + 1, 1)
-        if j == 1:
-            small_all(lambda e, q: small_to(mine, me, e, q).start())
-    for p in range(parts + 1, strips):
+        if j + 3 < strips:
+            both(j + 3, 1)
+        if j == 0:
+            send_small(mine)
+            for e in others:
+                cross_small(e).start()
+    for p in range(parts + 3, strips):
         both(p, 1)
 
     @pl.when(me < S - 1)
@@ -650,9 +664,18 @@
 
     for j in range(parts):
         send_p(j, True)
-    hop(2)
-    small_all(lambda e, q: small_to(e, q, e, q).wait_recv())
-
+    for p in range(strips):
+        both(p, 2)
+        if p == strips // 2:
+            for e in others:
+                crossed_small(e).wait_recv()
+                send_small(e)
+    if S <= 12:
+        for d in range(3, S):
+            hop(d)
+    else:
+        lax.fori_loop(3, S, lambda d, c: (hop(d), c)[1], 0)
+    small_all(lambda e, q: small_along(e, q, q).wait_recv())
     norm = 1.0 / math.sqrt(D * S * length)
     columns = r.xc.shape[-1]
 
@@ -672,12 +695,6 @@
         return rcopy(r.m_o.at[q], r.m_i.at[landing], r.m_s.at[q], r.m_r.at[slot], chan=q)
 
     each(C, lambda d: share_m(lax.rem(ch + d, C), ch, ch).start())
-    if S <= 12:
-        for d in range(3, S):
-            hop(d)
-    else:
-        lax.fori_loop(3, S, lambda d, c: (hop(d), c)[1], 0)
-
     def step_term(k, total):
         for e in range(D):
             x = r.xc[k, e].reshape(length, columns)
@@ -744,7 +761,9 @@
 
     settle_line(0)
     each(S, settle_line)
-    small_all(lambda e, q: small_to(mine, me, e, q).wait_send())
+    small_all(lambda e, q: small_along(e, me, q).wait_send())
+    for e in others:
+        cross_small(e).wait_send()
 
 
 def finish_kernel(parts, dw, mixes, dws, o_ig, o_dw, o_dwm, o_dws, ig, dwm, sems):

time: 49.2 us -> 46.8 us (0.951)
  Pallas kernels: 48.5 us -> 45.9 us
    pallas_call x1, Pallas kernels: 47.4 us -> 44.9 us  [body(): pl.pallas_call(functools.partial(layer_kernel, names, sizes, heads), out_...]
where the time goes in v10:
time: 46.8 us; the launch traced here: 46.5 us
  Pallas kernels  45.9 us (98%)
  between operations  0.64 us (1%)
    pallas_call x1, Pallas kernels, body(): pl.pallas_call(functools.partial(layer_kernel, names, sizes, heads), out_...  44.9 us
    pallas_call x1, Pallas kernels, body(): pl.pallas_call(finish_kernel, out_shape=(jax.ShapeDtypeStruct((rows, mode...  1.01 us

profile of v10, /device:TPU:0, one launch (start us, length us, event | category | flops | bytes accessed | tf_op | source)
XLA Modules:
  0.0 46.5 jit_solution(9699714148538566509)
XLA Ops:
  0.6 44.9 %layer.1 = (bf16[4,32,2560]{2,1,0:T(8,128)(2,1)S(1)}, f32[320,640]{1,0:T(8,128)S(1)}, bf16[4,80,256]{2,1,0:T(8,128)(2,1)S(1)}, f32[10,320]{1,0:T(8,128)S(1)}) custom-call(bf16[32,2560]{1,0:T(8,128)(2,1)} %bitcast.8, bf16[2560,640]{1,0:T(8,128)(2,1)} %refs_1_.1, bf16[2560,256]{1,0:T(8,128)(2,1)} %refs_2_.1, bf16[10,2560]{1,0:T(8,128)(2,1)} %bitcast.10, ...), custom_call_target="tpu_custom_call" | custom-call | tf_op jit(solution)/shard_map/layer/pallas_call | solution.py:882
  45.5 1.0 %finish.1 = (bf16[32,2560]{1,0:T(8,128)(2,1)}, f32[320,640]{1,0:T(8,128)}, f32[80,256]{1,0:T(8,128)}, f32[10,320]{1,0:T(8,128)}) custom-call(bf16[4,32,2560]{2,1,0:T(8,128)(2,1)S(1)} %get-tuple-element.12.parts, f32[320,640]{1,0:T(8,128)S(1)} %get-tuple-element.13.dw, bf16[4,80,256]{2,1,0:T(8,128)(2,1)S(1)} %get-tuple-element.14.mixes, ...), custom_call_target="tpu_custom_call" | custom-call | tf_op jit(solution)/shard_map/finish/pallas_call | solution.py:893

commit v11 on v10

--- a/solution.py
+++ b/solution.py
@@ -313,7 +313,9 @@
     model = r.w_in.shape[0]
     rows = length // C
     pieces, lag = PIECES, PIECES // 2
-    lags = (lag + 3, lag)
+    wait = lag + 3
+    catch_up = {wait + i: [i] for i in range(2)}
+    catch_up |= {wait + 2 + i: [2 * i + 2, 2 * i + 3] for i in range((pieces - 2) // 2)}
     size = width // pieces
     strips = width // LANES
     per = pieces // strips
@@ -338,19 +340,33 @@
                 carry(way, piece, True).start()
             outs[way][...] = jnp.zeros(outs[way].shape, BF)
 
+    def pass_state(way, piece):
+        carry(way, piece).wait_recv()
+        part = pl.ds(pl.multiple_of(piece * size, size), size)
+        before = outs[way][part, :].astype(F32)
+        term = terms[way][part, :].astype(F32)
+        scratch[way][part, :] = (r.decay[part, :] * before + term).astype(BF)
+        carry(way, piece).start()
+
     def beat(t):
         for way in (1, 0):
             spot = spots[way]
-            piece = t - lags[way] * (spot - 1)
+            piece = t - lag * (spot - 1)
 
             @pl.when((piece >= 0) & (piece < pieces) & (spot > 0) & (spot < S - 1))
             def _(way=way, piece=piece):
-                carry(way, piece).wait_recv()
-                part = pl.ds(pl.multiple_of(piece * size, size), size)
-                before = outs[way][part, :].astype(F32)
-                term = terms[way][part, :].astype(F32)
-                scratch[way][part, :] = (r.decay[part, :] * before + term).astype(BF)
-                carry(way, piece).start()
+                pass_state(way, piece)
+
+    def short_beat(t):
+        beat_of = ((1, 1, [t]), (1, 2, [t - lag]), (0, 1, [t]), (0, 2, catch_up.get(t, [])))
+        for way, spot, some in beat_of:
+            some = [p for p in some if 0 <= p < pieces]
+            if some:
+
+                @pl.when(spots[way] == spot)
+                def _(way=way, some=some):
+                    for piece in some:
+                        pass_state(way, piece)
 
     def gather(q, landing, slot):
         return rcopy(r.xs, r.xc.at[:, :, landing], r.gat_s.at[q], r.gat_r.at[slot], chan=q)
@@ -448,7 +464,7 @@
         def _():
             zcopy(j, "down", me).start()
 
-    beats = pieces + lags[0] * max(S - 3, 0)
+    beats = pieces + lag * max(S - 3, 0)
     early = heads // 2
     for h in range(early):
         head(h)
@@ -456,11 +472,11 @@
     crossed()
     each(C, lambda d: gather(lax.rem(ch + d, C), ch, ch).start())
     r.xc[:, :, ch] = r.xs[...]
-    if beats <= 24:
+    if S == 4:
         sums = {per * j + per - 1: j for j in range(strips)}
         late = {lag + t: j for t, j in sums.items()}
         for t in range(max(beats, heads - early)):
-            beat(t)
+            short_beat(t)
             if early + t < heads:
                 head(early + t)
             if t in sums:
@@ -485,11 +501,44 @@
             strip_out(j)
             strip_along(j, False)
 
+    def forward(p, way, d):
+        k = me - d if way == "up" else me + d
+        there = (k >= 0) if way == "up" else (k < S)
+        more = (me < S - 1) if way == "up" else (me > 0)
+
+        @pl.when(there)
+        def _():
+            zcopy(p, way, k).wait_recv()
+
+        @pl.when(there & more)
+        def _():
+            zcopy(p, way, k).start()
+
+        @pl.when(there)
+        def _():
+            for e in others:
+                ccopy(p, k, mine, e).start()
+
+    def both(p, d):
+        forward(p, "up", d)
+        forward(p, "down", d)
+
+    def hop(d):
+        for p in range(strips):
+            both(p, d)
+
+    def soon(p):
+        pl.when(spots[1] != 2)(lambda: both(p, 1))
+
+    def later(p):
+        pl.when(spots[1] == 2)(lambda: both(p, 1))
+
     @pl.when(spots[0] == S - 1)
     def _():
         for piece in range(pieces):
             carry(0, piece).wait_recv()
 
+    soon(0)
     start, end = r.start[...], r.end[...]
     score_grad = r.score_grad[...]
     mixer = r.sum_mix[...]
@@ -527,31 +576,7 @@
     r.gm_in[ch] = r.am[pl.ds(pl.multiple_of(ch * rows, rows), rows + PAD), :]
     r.gmp[...] = spread_back(r.pad_mix, r.conv_mix, 0, length)
 
-    def forward(p, way, d):
-        k = me - d if way == "up" else me + d
-        there = (k >= 0) if way == "up" else (k < S)
-        more = (me < S - 1) if way == "up" else (me > 0)
-
-        @pl.when(there)
-        def _():
-            zcopy(p, way, k).wait_recv()
-
-        @pl.when(there & more)
-        def _():
-            zcopy(p, way, k).start()
-
-        @pl.when(there)
-        def _():
-            for e in others:
-                ccopy(p, k, mine, e).start()
-
-    def both(p, d):
-        forward(p, "up", d)
-        forward(p, "down", d)
-
-    def hop(d):
-        for p in range(strips):
-            both(p, d)
+    soon(1)
 
     upstream = r.grad[...].astype(F32)
     stepped = r.stepped[...].astype(F32)
@@ -574,7 +599,7 @@
     r.gsm[me, mine, rows:, 0:LANES] = step_grad.T[0:PAD, :].astype(BF)
     steps = steps[:, 0:PAD]
 
-    both(0, 1)
+    soon(2)
 
     each(C, lambda d: share_mix(lax.rem(ch + d, C), ch, lax.rem(ch + d, C)).wait_recv())
     mix = r.gm_in[0].astype(F32)
@@ -612,8 +637,9 @@
         for e in [mine] + others:
             each(S, lambda d, e=e: do(e, lax.rem(me + d, S)))
 
-    both(1, 1)
-    both(2, 1)
+    for p in range(3, strips):
+        soon(p)
+    later(0)
 
     def share_p(j, q, landing, slot):
         piece = pl.ds(j * cut, cut)
@@ -644,14 +670,12 @@
         r.p_o[:, :, piece] = out.astype(BF).reshape(C, rows, cut)
         r.p_last[:, piece] = out[length - PAD :, :]
         send_p(j, False)
-        if j + 3 < strips:
-            both(j + 3, 1)
+        if j != 1:
+            later(max(j, 1))
         if j == 0:
             send_small(mine)
             for e in others:
                 cross_small(e).start()
-    for p in range(parts + 3, strips):
-        both(p, 1)
 
     @pl.when(me < S - 1)
     def _():
@@ -664,6 +688,8 @@
 
     for j in range(parts):
         send_p(j, True)
+    for p in range(parts, strips):
+        later(p)
     for p in range(strips):
         both(p, 2)
         if p == strips // 2:
@@ -811,7 +837,7 @@
     cols = model // groups
     state_size = mixed // 2
     assert width % PIECES == 0 and chans % 2 == 0 and seqs > 2
-    assert rows == 2 * PAD and width % LANES == 0 and PIECES % (width // LANES) == 0
+    assert width > 3 * LANES and chans == 4 and rows == 2 * PAD and width % LANES == 0 and PIECES % (width // LANES) == 0
     assert length == LANES and heads + conv_inner.shape[0] - 1 <= PAD
     upstream = output_grad[0]
     step_rows = step_weight.T

time: 46.8 us -> 47.4 us (1.013)
  Pallas kernels: 45.9 us -> 46.6 us
    pallas_call x1, Pallas kernels: 44.9 us -> 45.6 us  [body(): pl.pallas_call(functools.partial(layer_kernel, names, sizes, heads), out_...]
where the time goes in v11:
time: 47.4 us; the launch traced here: 47.3 us
  Pallas kernels  46.6 us (98%)
  between operations  0.64 us (1%)
    pallas_call x1, Pallas kernels, body(): pl.pallas_call(functools.partial(layer_kernel, names, sizes, heads), out_...  45.6 us
    pallas_call x1, Pallas kernels, body(): pl.pallas_call(finish_kernel, out_shape=(jax.ShapeDtypeStruct((rows, mode...  1.01 us

profile of v11, /device:TPU:0, one launch (start us, length us, event | category | flops | bytes accessed | tf_op | source)
XLA Modules:
  0.0 47.3 jit_solution(16007800473011866816)
XLA Ops:
  0.6 45.6 %layer.1 = (bf16[4,32,2560]{2,1,0:T(8,128)(2,1)S(1)}, f32[320,640]{1,0:T(8,128)S(1)}, bf16[4,80,256]{2,1,0:T(8,128)(2,1)S(1)}, f32[10,320]{1,0:T(8,128)S(1)}) custom-call(bf16[32,2560]{1,0:T(8,128)(2,1)} %bitcast.8, bf16[2560,640]{1,0:T(8,128)(2,1)} %refs_1_.1, bf16[2560,256]{1,0:T(8,128)(2,1)} %refs_2_.1, bf16[10,2560]{1,0:T(8,128)(2,1)} %bitcast.10, ...), custom_call_target="tpu_custom_call" | custom-call | tf_op jit(solution)/shard_map/layer/pallas_call | solution.py:908
  46.3 1.0 %finish.1 = (bf16[32,2560]{1,0:T(8,128)(2,1)}, f32[320,640]{1,0:T(8,128)}, f32[80,256]{1,0:T(8,128)}, f32[10,320]{1,0:T(8,128)}) custom-call(bf16[4,32,2560]{2,1,0:T(8,128)(2,1)S(1)} %get-tuple-element.12.parts, f32[320,640]{1,0:T(8,128)S(1)} %get-tuple-element.13.dw, bf16[4,80,256]{2,1,0:T(8,128)(2,1)S(1)} %get-tuple-element.14.mixes, ...), custom_call_target="tpu_custom_call" | custom-call | tf_op jit(solution)/shard_map/finish/pallas_call | solution.py:919

commit v12 on v10

--- a/solution.py
+++ b/solution.py
@@ -313,7 +313,7 @@
     model = r.w_in.shape[0]
     rows = length // C
     pieces, lag = PIECES, PIECES // 2
-    lags = (lag + 3, lag)
+    lags = (lag + 1, lag)
     size = width // pieces
     strips = width // LANES
     per = pieces // strips

time: 46.8 us -> 47.1 us (level)
  no operation moved by 1% of the time
where the time goes in v12:
time: 47.1 us; the launch traced here: 46.9 us
  Pallas kernels  46.3 us (98%)
  between operations  0.64 us (1%)
    pallas_call x1, Pallas kernels, body(): pl.pallas_call(functools.partial(layer_kernel, names, sizes, heads), out_...  45.3 us
    pallas_call x1, Pallas kernels, body(): pl.pallas_call(finish_kernel, out_shape=(jax.ShapeDtypeStruct((rows, mode...  1.01 us

profile of v12, /device:TPU:0, one launch (start us, length us, event | category | flops | bytes accessed | tf_op | source)
XLA Modules:
  0.0 46.9 jit_solution(9097050396819155565)
XLA Ops:
  0.6 45.3 %layer.1 = (bf16[4,32,2560]{2,1,0:T(8,128)(2,1)S(1)}, f32[320,640]{1,0:T(8,128)S(1)}, bf16[4,80,256]{2,1,0:T(8,128)(2,1)S(1)}, f32[10,320]{1,0:T(8,128)S(1)}) custom-call(bf16[32,2560]{1,0:T(8,128)(2,1)} %bitcast.8, bf16[2560,640]{1,0:T(8,128)(2,1)} %refs_1_.1, bf16[2560,256]{1,0:T(8,128)(2,1)} %refs_2_.1, bf16[10,2560]{1,0:T(8,128)(2,1)} %bitcast.10, ...), custom_call_target="tpu_custom_call" | custom-call | tf_op jit(solution)/shard_map/layer/pallas_call | solution.py:882
  45.9 1.0 %finish.1 = (bf16[32,2560]{1,0:T(8,128)(2,1)}, f32[320,640]{1,0:T(8,128)}, f32[80,256]{1,0:T(8,128)}, f32[10,320]{1,0:T(8,128)}) custom-call(bf16[4,32,2560]{2,1,0:T(8,128)(2,1)S(1)} %get-tuple-element.12.parts, f32[320,640]{1,0:T(8,128)S(1)} %get-tuple-element.13.dw, bf16[4,80,256]{2,1,0:T(8,128)(2,1)S(1)} %get-tuple-element.14.mixes, ...), custom_call_target="tpu_custom_call" | custom-call | tf_op jit(solution)/shard_map/finish/pallas_call | solution.py:893
